TPU v7x, 256 devices: a whole 4x4x8 slice. The times are simulated.
256 devices in a mesh: rows: 32 (over x_lo, z, core), cols: 8 (over x_hi, y).
Axes of the slice: x: 4 (x_hi: 2, x_lo: 2; x = x_hi * 2 + x_lo), y: 4, z: 8, core: 2. Of those that a mesh axis runs over, the one named last changes fastest.
Arguments:
- rhs: float32 [65536, 16], P(('rows', 'cols')), may hold values from -6 to 6
- diagonal: float32 [65536], P(('rows', 'cols')), may hold values from 1 to 16
- blocks: float32 [512, 16, 128, 128], P('rows', 'cols'), may hold values from -0.078125 to 0.078125
- block_cols: int32 [512, 16], P('rows', 'cols'), may hold values from 0 to 63
- counts: int32 [512, 8], P('rows', 'cols'), may hold values from 1 to 2
Outputs:
- solution: float32 [65536, 16], P(('rows', 'cols'))
Inputs may be any that keep to these rules, and one draw needn't show every extreme that they name: Every entry of block_cols names a block column within its slot's group, from 0 to 63; entries may repeat within a row. `counts`: every count lies between 1 and 2; the slots past the count in a group hold blocks that are not used.
All inputs are finite; a program needn't handle non-finite values.
Results may differ from a plain program's by a relative error of at most 0.0001.
Values sent between devices are 32-bit elements; how exact they have to be, the bound alone decides.
No kernel may reach another device: no remote copies, remote signals or barrier semaphores. Data moves between devices by JAX's collectives and lax.ppermute only.
A program may use at most 64 MiB of HBM per device.

v0:
```python
import math

import jax
import jax.numpy as jnp
from jax import lax
from jax.sharding import PartitionSpec as P

ITERS = 4


def copy_for_each(shard, axis):
    length = lax.axis_size(axis)
    return lax.all_to_all(
        jnp.broadcast_to(shard[None], (length, *shard.shape)), axis, 0, 0, tiled=True
    )


def in_order(pieces, dim):
    pieces = jnp.moveaxis(pieces, 0, dim)
    lengths = pieces.shape
    return pieces.reshape(*lengths[:dim], lengths[dim] * lengths[dim + 1], *lengths[dim + 2 :])


def gathered_copies(shard, axis, dim):
    pieces = copy_for_each(shard, axis)
    return in_order(pieces, dim)


def of_everyone(shard, axis):
    return copy_for_each(shard, axis).sum(axis=0)


def in_one_piece(arrays, axis, dim, along):
    widths = [math.prod(a.shape[along:]) for a in arrays]
    both = jnp.concatenate(
        [a.reshape(*a.shape[:along], w) for a, w in zip(arrays, widths)], axis=along
    )
    whole = lax.all_gather(both, axis, axis=dim, tiled=True)
    pieces = jnp.split(whole, [sum(widths[:k]) for k in range(1, len(widths))], axis=along)
    return tuple(
        (b.reshape(*whole.shape[:along], *a.shape[along:]) for a, b in zip(arrays, pieces))
    )


def together(arrays, axis):
    vector, at, finished = (jnp.concatenate([a.reshape(-1) for a in arrays]), 0, [])
    subtotal = of_everyone(vector, axis)
    for a in arrays:
        finished.append(subtotal[at : at + a.size].reshape(a.shape))
        at += a.size
    return tuple(finished)


def solve_block(matrix, right):
    size = matrix.shape[0]
    joined = jnp.concatenate([matrix, right], axis=1)
    for index in range(size):
        pivot_row = joined[index] / joined[index, index]
        joined = joined - joined[:, index : index + 1] * pivot_row[None, :]
        joined = joined.at[index].set(pivot_row)
    return joined[:, size:]


def gram(left, right):
    return jnp.dot(left.T, right, precision=lax.Precision.HIGHEST)


def times_block(vectors, small):
    return jnp.dot(vectors, small, precision=lax.Precision.HIGHEST)


def per_device(rhs, diagonal, blocks, block_cols, counts):
    width = blocks.shape[2]
    piece_rows = rhs.shape[0]
    used = (lax.broadcasted_iota(jnp.int32, block_cols.shape, 1) < counts).astype(jnp.float32)

    def block_rows(gathered, count):
        number = count // width
        segment = gathered.reshape(-1, width, gathered.shape[1])
        picked = segment[block_cols] * used[:, :, None, None]
        product = jnp.einsum("rkij,rkjs->ris", blocks, picked, precision=lax.Precision.HIGHEST)
        return product.reshape(number * width, gathered.shape[1])

    def product_of(piece):
        gathered = gathered_copies(piece, "rows", 0)
        total = block_rows(gathered, blocks.shape[0] * width)
        return of_everyone(total, "cols")

    start_rows, diag_rows = in_one_piece((rhs, diagonal), "cols", 0, 1)
    offset = lax.axis_index("cols") * piece_rows

    def apply(vectors):
        piece = lax.dynamic_slice_in_dim(vectors, offset, piece_rows, 0)
        return diag_rows[:, None] * vectors + product_of(piece)

    solution = jnp.zeros_like(start_rows)
    residual = start_rows
    direction = start_rows
    for iteration in range(ITERS):
        image = apply(direction)
        matrix, right = together((gram(start_rows, image), gram(start_rows, residual)), "rows")
        alpha = solve_block(matrix, right)
        middle = residual - times_block(image, alpha)
        second = apply(middle)
        along, square, cross = together(
            (jnp.sum(second * middle), jnp.sum(second * second), gram(start_rows, second)), "rows"
        )
        omega = along / square
        solution = solution + times_block(direction, alpha) + omega * middle
        residual = middle - omega * second
        beta = -solve_block(matrix, cross)
        direction = residual + times_block(direction - omega * image, beta)
    return lax.dynamic_slice_in_dim(solution, offset, piece_rows, 0)


def solution(mesh):
    in_specs = (
        P(("rows", "cols"), None),
        P(("rows", "cols")),
        P("rows", "cols", None, None),
        P("rows", "cols"),
        P("rows", "cols"),
    )
    out_specs = P(("rows", "cols"), None)
    return jax.shard_map(
        per_device, mesh=mesh, in_specs=in_specs, out_specs=out_specs, check_vma=False
    )
```

profile of v0, /device:TPU:1, one launch (start us, length us, event | category | flops | bytes accessed | tf_op | source)
XLA Modules:
  0.0 813.1 jit_solution(13670134889492838594)
XLA Ops:
  0.9 29.4 %all_gather.3 = f32[2048,17]{0,1:T(8,128)S(1)} all-gather(f32[256,17]{0,1:T(8,128)S(1)} %pad_maximum_fusion), channel_id=1, replica_groups=mesh['rows'=32,'cols'=8] {'cols'}, dimensions={0}, use_global_device_ids=true | all-gather | bytes 156672 | tf_op jit(solution)/shard_map/all_gather | solution.py:38
  31.2 15.9 %all-to-all-start = ((f32[32,256,16]{1,2,0:T(8,128)}), f32[32,256,16]{1,2,0:T(8,128)S(1)}, u32[]{:S(2)}, u32[]{:S(2)}) async-start(f32[32,256,16]{1,2,0:T(8,128)} %broadcast_in_dim.66), calls=%async_computation | async-start | bytes 1048576 | tf_op jit(solution)/shard_map/all_to_all | solution.py:13
  47.4 16.3 %all-to-all-done = f32[32,256,16]{1,2,0:T(8,128)S(1)} async-done(((f32[32,256,16]{1,2,0:T(8,128)}), f32[32,256,16]{1,2,0:T(8,128)S(1)}, u32[]{:S(2)}, u32[]{:S(2)}) %all-to-all-start) | async-done | bytes 524320 | tf_op jit(solution)/shard_map/all_to_all | solution.py:13
  69.8 6.2 all-to-all-start.1
  76.4 12.5 %all-to-all-done.1 = f32[8,2048,16]{1,2,0:T(8,128)S(1)} async-done(((f32[8,2048,16]{1,2,0:T(8,128)}), f32[8,2048,16]{1,2,0:T(8,128)S(1)}, u32[]{:S(2)}, u32[]{:S(2)}) %all-to-all-start.1) | async-done | bytes 1048608 | tf_op jit(solution)/shard_map/all_to_all | solution.py:13
  89.3 15.1 %all_to_all.128 = f32[32,1,512]{2,1,0:T(1,128)S(1)} all-to-all(f32[32,1,512]{2,1,0:T(1,128)S(1)} %broadcast_in_dim.70), channel_id=1, replica_groups=mesh['rows'=32,'cols'=8] {'rows'}, dimensions={0} | all-to-all | bytes 131072 | tf_op jit(solution)/shard_map/all_to_all | solution.py:13
  142.9 20.6 %all_to_all.129 = f32[32,256,16]{1,2,0:T(8,128)S(1)} all-to-all(f32[32,256,16]{1,2,0:T(8,128)S(1)} %broadcast_in_dim.71), channel_id=1, replica_groups=mesh['rows'=32,'cols'=8] {'rows'}, dimensions={0} | all-to-all | bytes 1048576 | tf_op jit(solution)/shard_map/all_to_all | solution.py:13
  168.5 18.7 %all_to_all.130 = f32[8,2048,16]{1,2,0:T(8,128)S(1)} all-to-all(f32[8,2048,16]{1,2,0:T(8,128)S(1)} %broadcast_in_dim.73), channel_id=1, replica_groups=mesh['rows'=32,'cols'=8] {'cols'}, dimensions={0} | all-to-all | bytes 2097152 | tf_op jit(solution)/shard_map/all_to_all | solution.py:13
  192.3 15.1 %all_to_all.131 = f32[32,1,258]{2,1,0:T(1,128)S(1)} all-to-all(f32[32,1,258]{2,1,0:T(1,128)S(1)} %broadcast_in_dim.74), channel_id=1, replica_groups=mesh['rows'=32,'cols'=8] {'rows'}, dimensions={0} | all-to-all | bytes 66048 | tf_op jit(solution)/shard_map/all_to_all | solution.py:13
  246.3 20.4 %all_to_all.132 = f32[32,256,16]{1,2,0:T(8,128)S(1)} all-to-all(f32[32,256,16]{1,2,0:T(8,128)S(1)} %broadcast_in_dim.75), channel_id=1, replica_groups=mesh['rows'=32,'cols'=8] {'rows'}, dimensions={0} | all-to-all | bytes 1048576 | tf_op jit(solution)/shard_map/all_to_all | solution.py:13
  272.8 3.6 all-to-all-start.7
  277.7 11.8 %all-to-all-done.7 = f32[8,2048,16]{1,2,0:T(8,128)S(1)} async-done(((f32[8,2048,16]{1,2,0:T(8,128)}), f32[8,2048,16]{1,2,0:T(8,128)S(1)}, u32[]{:S(2)}, u32[]{:S(2)}) %all-to-all-start.7) | async-done | bytes 1048608 | tf_op jit(solution)/shard_map/all_to_all | solution.py:13
  291.6 15.5 %all_to_all.133 = f32[32,1,512]{2,1,0:T(1,128)S(1)} all-to-all(f32[32,1,512]{2,1,0:T(1,128)S(1)} %broadcast_in_dim.78), channel_id=1, replica_groups=mesh['rows'=32,'cols'=8] {'rows'}, dimensions={0} | all-to-all | bytes 131072 | tf_op jit(solution)/shard_map/all_to_all | solution.py:13
  343.8 20.6 %all_to_all.134 = f32[32,256,16]{1,2,0:T(8,128)S(1)} all-to-all(f32[32,256,16]{1,2,0:T(8,128)S(1)} %broadcast_in_dim.79), channel_id=1, replica_groups=mesh['rows'=32,'cols'=8] {'rows'}, dimensions={0} | all-to-all | bytes 1048576 | tf_op jit(solution)/shard_map/all_to_all | solution.py:13
  369.5 18.6 %all_to_all.135 = f32[8,2048,16]{1,2,0:T(8,128)S(1)} all-to-all(f32[8,2048,16]{1,2,0:T(8,128)S(1)} %broadcast_in_dim.81), channel_id=1, replica_groups=mesh['rows'=32,'cols'=8] {'cols'}, dimensions={0} | all-to-all | bytes 2097152 | tf_op jit(solution)/shard_map/all_to_all | solution.py:13
  393.2 15.1 %all_to_all.136 = f32[32,1,258]{2,1,0:T(1,128)S(1)} all-to-all(f32[32,1,258]{2,1,0:T(1,128)S(1)} %broadcast_in_dim.82), channel_id=1, replica_groups=mesh['rows'=32,'cols'=8] {'rows'}, dimensions={0} | all-to-all | bytes 66048 | tf_op jit(solution)/shard_map/all_to_all | solution.py:13
  447.5 20.4 %all_to_all.137 = f32[32,256,16]{1,2,0:T(8,128)S(1)} all-to-all(f32[32,256,16]{1,2,0:T(8,128)S(1)} %broadcast_in_dim.83), channel_id=1, replica_groups=mesh['rows'=32,'cols'=8] {'rows'}, dimensions={0} | all-to-all | bytes 1048576 | tf_op jit(solution)/shard_map/all_to_all | solution.py:13
  474.0 3.6 all-to-all-start.13
  478.8 11.8 %all-to-all-done.13 = f32[8,2048,16]{1,2,0:T(8,128)S(1)} async-done(((f32[8,2048,16]{1,2,0:T(8,128)}), f32[8,2048,16]{1,2,0:T(8,128)S(1)}, u32[]{:S(2)}, u32[]{:S(2)}) %all-to-all-start.13) | async-done | bytes 1048608 | tf_op jit(solution)/shard_map/all_to_all | solution.py:13
  492.7 15.5 %all_to_all.138 = f32[32,1,512]{2,1,0:T(1,128)S(1)} all-to-all(f32[32,1,512]{2,1,0:T(1,128)S(1)} %broadcast_in_dim.86), channel_id=1, replica_groups=mesh['rows'=32,'cols'=8] {'rows'}, dimensions={0} | all-to-all | bytes 131072 | tf_op jit(solution)/shard_map/all_to_all | solution.py:13
  545.6 20.6 %all_to_all.139 = f32[32,256,16]{1,2,0:T(8,128)S(1)} all-to-all(f32[32,256,16]{1,2,0:T(8,128)S(1)} %broadcast_in_dim.87), channel_id=1, replica_groups=mesh['rows'=32,'cols'=8] {'rows'}, dimensions={0} | all-to-all | bytes 1048576 | tf_op jit(solution)/shard_map/all_to_all | solution.py:13
  571.2 18.6 %all_to_all.140 = f32[8,2048,16]{1,2,0:T(8,128)S(1)} all-to-all(f32[8,2048,16]{1,2,0:T(8,128)S(1)} %broadcast_in_dim.89), channel_id=1, replica_groups=mesh['rows'=32,'cols'=8] {'cols'}, dimensions={0} | all-to-all | bytes 2097152 | tf_op jit(solution)/shard_map/all_to_all | solution.py:13
  594.9 15.1 %all_to_all.141 = f32[32,1,258]{2,1,0:T(1,128)S(1)} all-to-all(f32[32,1,258]{2,1,0:T(1,128)S(1)} %broadcast_in_dim.90), channel_id=1, replica_groups=mesh['rows'=32,'cols'=8] {'rows'}, dimensions={0} | all-to-all | bytes 66048 | tf_op jit(solution)/shard_map/all_to_all | solution.py:13
  648.3 20.4 %all_to_all.142 = f32[32,256,16]{1,2,0:T(8,128)S(1)} all-to-all(f32[32,256,16]{1,2,0:T(8,128)S(1)} %broadcast_in_dim.91), channel_id=1, replica_groups=mesh['rows'=32,'cols'=8] {'rows'}, dimensions={0} | all-to-all | bytes 1048576 | tf_op jit(solution)/shard_map/all_to_all | solution.py:13
  674.8 3.6 all-to-all-start.19
  679.7 11.8 %all-to-all-done.19 = f32[8,2048,16]{1,2,0:T(8,128)S(1)} async-done(((f32[8,2048,16]{1,2,0:T(8,128)}), f32[8,2048,16]{1,2,0:T(8,128)S(1)}, u32[]{:S(2)}, u32[]{:S(2)}) %all-to-all-start.19) | async-done | bytes 1048608 | tf_op jit(solution)/shard_map/all_to_all | solution.py:13
  693.6 15.5 %all_to_all.143 = f32[32,1,512]{2,1,0:T(1,128)S(1)} all-to-all(f32[32,1,512]{2,1,0:T(1,128)S(1)} %broadcast_in_dim.94), channel_id=1, replica_groups=mesh['rows'=32,'cols'=8] {'rows'}, dimensions={0} | all-to-all | bytes 131072 | tf_op jit(solution)/shard_map/all_to_all | solution.py:13
  745.2 20.6 %all_to_all.144 = f32[32,256,16]{1,2,0:T(8,128)S(1)} all-to-all(f32[32,256,16]{1,2,0:T(8,128)S(1)} %broadcast_in_dim.95), channel_id=1, replica_groups=mesh['rows'=32,'cols'=8] {'rows'}, dimensions={0} | all-to-all | bytes 1048576 | tf_op jit(solution)/shard_map/all_to_all | solution.py:13
  771.9 4.7 all-to-all-start.22
  777.7 11.8 %all-to-all-done.22 = f32[8,2048,16]{1,2,0:T(8,128)} async-done(((f32[8,2048,16]{1,2,0:T(8,128)}), f32[8,2048,16]{1,2,0:T(8,128)}, u32[]{:S(2)}, u32[]{:S(2)}) %all-to-all-start.22) | async-done | bytes 1048608 | tf_op jit(solution)/shard_map/all_to_all | solution.py:13
  793.8 7.5 all-to-all-start.23
  801.7 7.7 all-to-all-done.23
  (866 shorter events, 340.6 us)
Async XLA Ops:
  0.0 66.8 %copy-start = (f32[16,2,128,128]{3,2,1,0:T(8,128)S(1)}, f32[16,2,128,128]{3,2,1,0:T(8,128)}, u32[]{:S(2)}) copy-start(f32[16,2,128,128]{3,2,1,0:T(8,128)} %param.231) | copy-start | bytes 6291460
  0.0 47.1 %copy-start.13 = (s32[16,2]{0,1:T(2,128)S(1)}, s32[16,2]{0,1:T(2,128)}, u32[]{:S(2)}) copy-start(s32[16,2]{0,1:T(2,128)} %param.232) | copy-start | bytes 388
  0.0 47.3 %copy-start.14 = (s32[16,1]{0,1:T(1,128)S(1)}, s32[16,1]{0,1:T(1,128)}, u32[]{:S(2)}) copy-start(s32[16,1]{0,1:T(1,128)} %param.233) | copy-start | bytes 196
  31.2 32.5 %all-to-all-start = ((f32[32,256,16]{1,2,0:T(8,128)}), f32[32,256,16]{1,2,0:T(8,128)S(1)}, u32[]{:S(2)}, u32[]{:S(2)}) async-start(f32[32,256,16]{1,2,0:T(8,128)} %broadcast_in_dim.66), calls=%async_computation | async-start | bytes 1048576 | tf_op jit(solution)/shard_map/all_to_all | solution.py:13
  69.8 19.0 %all-to-all-start.1 = ((f32[8,2048,16]{1,2,0:T(8,128)}), f32[8,2048,16]{1,2,0:T(8,128)S(1)}, u32[]{:S(2)}, u32[]{:S(2)}) async-start(f32[8,2048,16]{1,2,0:T(8,128)} %broadcast_in_dim.69), calls=%async_computation.1 | async-start | bytes 2097152 | tf_op jit(solution)/shard_map/all_to_all | solution.py:13
  88.9 52.6 %copy-start.9 = (f32[2048,16]{0,1:T(8,128)}, f32[2048,16]{0,1:T(8,128)S(1)}, u32[]{:S(2)}) copy-start(f32[2048,16]{0,1:T(8,128)S(1)} %reduce_sum.216) | copy-start | bytes 393220
  244.2 2.1 copy-start.11
  245.6 0.7 copy-start.1
  272.8 16.6 %all-to-all-start.7 = ((f32[8,2048,16]{1,2,0:T(8,128)}), f32[8,2048,16]{1,2,0:T(8,128)S(1)}, u32[]{:S(2)}, u32[]{:S(2)}) async-start(f32[8,2048,16]{1,2,0:T(8,128)} %broadcast_in_dim.77), calls=%async_computation.7 | async-start | bytes 2097152 | tf_op jit(solution)/shard_map/all_to_all | solution.py:13
  343.1 0.6 copy-start.5
  445.3 2.2 copy-start.12
  446.8 0.6 copy-start.3
  474.0 16.6 %all-to-all-start.13 = ((f32[8,2048,16]{1,2,0:T(8,128)}), f32[8,2048,16]{1,2,0:T(8,128)S(1)}, u32[]{:S(2)}, u32[]{:S(2)}) async-start(f32[8,2048,16]{1,2,0:T(8,128)} %broadcast_in_dim.85), calls=%async_computation.13 | async-start | bytes 2097152 | tf_op jit(solution)/shard_map/all_to_all | solution.py:13
  544.8 0.7 copy-start.6
  645.9 2.4 copy-start.10
  647.6 0.6 copy-start.7
  674.8 16.6 %all-to-all-start.19 = ((f32[8,2048,16]{1,2,0:T(8,128)}), f32[8,2048,16]{1,2,0:T(8,128)S(1)}, u32[]{:S(2)}, u32[]{:S(2)}) async-start(f32[8,2048,16]{1,2,0:T(8,128)} %broadcast_in_dim.93), calls=%async_computation.19 | async-start | bytes 2097152 | tf_op jit(solution)/shard_map/all_to_all | solution.py:13
  770.7 6.3 copy-start.2
  770.7 6.7 copy-start.4
  771.9 29.4 %copy-start.8 = (f32[2048,16]{0,1:T(8,128)S(1)}, f32[2048,16]{0,1:T(8,128)}, u32[]{:S(2)}) copy-start(f32[2048,16]{0,1:T(8,128)} %copy-done.7) | copy-start | bytes 393220
  771.9 17.7 %all-to-all-start.22 = ((f32[8,2048,16]{1,2,0:T(8,128)}), f32[8,2048,16]{1,2,0:T(8,128)}, u32[]{:S(2)}, u32[]{:S(2)}) async-start(f32[8,2048,16]{1,2,0:T(8,128)} %broadcast_in_dim.97), calls=%async_computation.22 | async-start | bytes 2097152 | tf_op jit(solution)/shard_map/all_to_all | solution.py:13
  793.8 15.6 %all-to-all-start.23 = ((f32[32,1,258]{2,1,0:T(1,128)}), f32[32,1,258]{2,1,0:T(1,128)S(1)}, u32[]{:S(2)}, u32[]{:S(2)}) async-start(f32[32,1,258]{2,1,0:T(1,128)} %broadcast_in_dim.98), calls=%async_computation.23 | async-start | bytes 98304 | tf_op jit(solution)/shard_map/all_to_all | solution.py:13
where the time goes:
time: 826 us; the launch traced here: 813 us
  blocking collectives  336 us (41%)
  other arithmetic  170 us (21%)
  local copies, waits for them, and re-layouts  133 us (16%)
  waiting for transfers between devices  83.5 us (10%)
  starting transfers between devices  45 us (5%)
  matrix products  37.5 us (5%)
    all_to_all x17, blocking collectives, copy_for_each(): lax.all_to_all(jnp.broadcast_to(shard[None], (length, *shard.shape)), axi...  307 us
    all_to_all x7, waiting for transfers between devices, copy_for_each(): lax.all_to_all(jnp.broadcast_to(shard[None], (length, *shard.shape)), axi...  83.5 us
    div x112, other arithmetic, solve_block(): pivot_row = joined[index] / joined[index, index]  72.2 us
    slice x109, local copies, waits for them, and re-layouts, solve_block(): pivot_row = joined[index] / joined[index, index]  68.3 us
    mul x105, other arithmetic, solve_block(): joined = joined - joined[:, index:index + 1] * pivot_row[None, :]  67.2 us
    all_to_all x7, starting transfers between devices, copy_for_each(): lax.all_to_all(jnp.broadcast_to(shard[None], (length, *shard.shape)), axi...  45 us
    all_gather x1, blocking collectives, in_one_piece(): whole = lax.all_gather(both, axis, axis=dim, tiled=True)  29.4 us
    slice x109, local copies, waits for them, and re-layouts, solve_block(): joined = joined - joined[:, index:index + 1] * pivot_row[None, :]  19.5 us
  transfers between devices with their start and end apart: 7, of which 7 were waited for; matrix products, arithmetic and copies ran while one was open for 1% of the time, Pallas kernels for 0%

commit v1 on v0

v1 whole, which is shorter than its diff:
```python
import jax
import jax.numpy as jnp
from jax import lax
from jax.experimental import pallas as pl
from jax.experimental.pallas import tpu as pltpu
from jax.sharding import PartitionSpec as P

ITERS = 4
S = 16
BS = 128
F32 = jnp.float32
HI = lax.Precision.HIGHEST
VMEM = pl.BlockSpec(memory_space=pltpu.VMEM)
SMEM = pl.BlockSpec(memory_space=pltpu.SMEM)
TILE = 8


def sds(*shape, dtype=F32):
    return jax.ShapeDtypeStruct(shape, dtype)


def call(body, outs, specs, *args, name, scratch=()):
    return pl.pallas_call(
        body,
        out_shape=outs,
        in_specs=specs,
        out_specs=jax.tree.map(lambda _: VMEM, outs),
        scratch_shapes=scratch,
        name=name,
    )(*args)


def dot(a, b, contract=((1,), (0,))):
    return lax.dot_general(a, b, (contract, ((), ())), precision=HI, preferred_element_type=F32)


def bdot(a, b):
    return lax.dot_general(a, b, (((1,), (0,)), ((), ())), preferred_element_type=F32)


def halves(x):
    high = x.astype(jnp.bfloat16)
    return high, (x - high.astype(F32)).astype(jnp.bfloat16)


def wide(ref, at=()):
    return jnp.concatenate([ref[(*at, slice(0, S))], ref[(*at, slice(S, 2 * S))]], axis=1)


def spread(ref, value, tile):
    for k in range(ref.shape[0]):
        ref[k, 0:S] = value[:, :BS]
        ref[k, S : 2 * S] = value[:, BS:]
        ref[k, 2 * S : 2 * S + TILE] = tile


def solve(matrix, right):
    joined = jnp.concatenate([matrix, right], axis=1)
    row = lax.broadcasted_iota(jnp.int32, joined.shape, 0)
    for i in range(S):
        pivot = joined[i : i + 1, :] / joined[i : i + 1, i : i + 1]
        joined = jnp.where(row == i, pivot, joined - joined[:, i : i + 1] * pivot)
    return joined[:, S:]


def mix(vectors, small):
    return dot(small.T, vectors)


def grams(left, right):
    return dot(left, right, ((1,), (1,)))


def pack(products, extra=None):
    if extra is not None:
        row = lax.broadcasted_iota(jnp.int32, products.shape, 0)
        col = lax.broadcasted_iota(jnp.int32, products.shape, 1)
        for k, value in enumerate(extra):
            products = jnp.where((row == 0) & (col == S + k), value, products)
    return jnp.concatenate([products[8 * g : 8 * g + 8] for g in range(4)], axis=1)


def unpack(tile):
    whole = jnp.concatenate([tile[:, 32 * g : 32 * g + 32] for g in range(4)], axis=0)
    return whole[:S, :S], whole[:S, S:], whole[S:, :S], whole[S:, S:]


def total(ref):
    value = ref[0]
    for k in range(1, ref.shape[0]):
        value = value + ref[k]
    image = jnp.concatenate([value[0:S], value[S : 2 * S]], axis=1)
    return image, value[2 * S :]


def entire(x):
    return jnp.sum(jnp.sum(x, axis=1, keepdims=True), axis=0, keepdims=True)


def prepare_body(blocks, shadow_rows, cols, counts, core, packed, mine, other, acc):
    acc[...] = jnp.zeros_like(acc)

    def step(i, _):
        piece = shadow_rows[i // 2, pl.ds(pl.multiple_of((i % 2) * S, S), S), :]
        for k in range(2):
            keep = (k < counts[i, 0]).astype(F32)
            block = blocks[i, k] * keep
            target = cols[i, k]
            acc[target] += dot(piece, block)
            high, low = halves(block.T)
            packed[i, k * BS : (k + 1) * BS, 0:BS] = high
            packed[i, k * BS : (k + 1) * BS, BS : 2 * BS] = low
        return 0

    lax.fori_loop(0, 16, step, 0)
    me = core[0]
    for m in range(16):
        for b in range(2):
            mine[m, b * S : (b + 1) * S] = acc[m * 4 + me * 2 + b]
            other[m, b * S : (b + 1) * S] = acc[m * 4 + (1 - me) * 2 + b]


def product_body(own, peer, packed, cols, core, out):
    me = core[0]
    rows = own.shape[1]
    if rows > 2 * S:
        tile = own[0, 2 * S :]
        tile2 = peer[0, 2 * S :]
        for m in range(1, 16):
            tile = tile + own[m, 2 * S :]
            tile2 = tile2 + peer[m, 2 * S :]
        tile = tile + tile2
    for i in range(16):
        picked = []
        for k in range(2):
            col = cols[i, k]
            m = col // 4
            b = pl.multiple_of((col % 2) * S, S)
            here = own[m, pl.ds(b, S), :]
            there = peer[m, pl.ds(b, S), :]
            picked.append(jnp.where((col // 2) % 2 == me, here, there))
        high, low = halves(jnp.concatenate(picked, axis=1))
        result = bdot(jnp.concatenate([high, low], axis=0), packed[i])
        result = (result[:S, :BS] + result[:S, BS:]) + (result[S:, :BS] + result[S:, BS:])
        out[i // 2, (i % 2) * S : (i % 2 + 1) * S] = result
    if rows > 2 * S:
        for c in range(8):
            out[c, 2 * S :] = tile


def first_body(parts, arrived, shadow, diag, image, weights, message):
    value, _ = total(parts)
    rhs = shadow[...]
    v = value + diag[...] * rhs
    w = arrived[0, 0 : 2 * S]
    for m in range(1, 16):
        w = w + arrived[m, 0 : 2 * S]
    w = jnp.concatenate([w[0:S], w[S:]], axis=1) + diag[...] * rhs
    image[...] = v
    weights[...] = w
    products = grams(jnp.concatenate([w, rhs], axis=0), jnp.concatenate([v, rhs], axis=0))
    spread(message, v, pack(products))


def second_half(t, q, v, p, x, matrix, cross, w, s, u_out, base_out, t_out, cross_out, message):
    beta = -solve(matrix, cross)
    u = t + mix(v, beta)
    u_out[...] = u
    base_out[...] = q + mix(p, beta)
    t_out[...] = t
    cross_out[...] = cross
    products = grams(jnp.concatenate([w, s], axis=0), jnp.concatenate([u, q], axis=0))
    spread(message, u, pack(products, (entire(t * t), entire(t * q))))


def lead_body(parts, shadow, diag, image, weights, q_out, x_out, u_out, base_out, t_out, cross_out, message):
    value, tile = total(parts)
    s = shadow[...]
    v = image[...]
    z = value + diag[...] * v
    w_v, _, matrix, right = unpack(tile)
    alpha = solve(matrix, right)
    t = v - mix(z, alpha)
    q = s - mix(v, alpha)
    cross = matrix - dot(w_v, alpha)
    q_out[...] = q
    x_out[...] = mix(s, alpha)
    second_half(
        t, q, v, s, None, matrix, cross, weights[...], s, u_out, base_out, t_out, cross_out, message
    )


def even_body(
    parts, shadow, diag, weights, q, x, u, base, t, cross, q_out, x_out, v_out, p_out, matrix_out, message
):
    value, tile = total(parts)
    y = value + diag[...] * u[...]
    w_u, sums, s_u, s_q = unpack(tile)
    omega = sums[0:1, 1:2] / sums[0:1, 0:1]
    matrix = s_u - omega * w_u
    right = s_q - omega * cross[...]
    alpha = solve(matrix, right)
    v = u[...] - omega * y
    p = base[...] - omega * u[...]
    middle = (q[...] - omega * t[...]) - mix(v, alpha)
    x_out[...] = x[...] + omega * q[...] + mix(p, alpha)
    q_out[...] = middle
    v_out[...] = v
    p_out[...] = p
    matrix_out[...] = matrix
    products = grams(
        jnp.concatenate([weights[...], shadow[...]], axis=0),
        jnp.concatenate([middle, middle], axis=0),
    )
    spread(message, middle, pack(products))


def odd_body(
    parts, shadow, diag, weights, q, v, p, matrix, u_out, base_out, t_out, cross_out, message
):
    value, tile = total(parts)
    t = value + diag[...] * q[...]
    cross = unpack(tile)[0]
    second_half(
        t, q[...], v[...], p[...], None, matrix[...], cross, weights[...], shadow[...],
        u_out, base_out, t_out, cross_out, message,
    )


def last_body(parts, diag, q, sums):
    value, _ = total(parts)
    t = value + diag[...] * q[...]
    lane = lax.broadcasted_iota(jnp.int32, (1, BS), 1)
    sums[...] = jnp.where(lane == 0, entire(t * t), jnp.where(lane == 1, entire(t * q[...]), 0.0))


def end_body(sums, x, q, out):
    value = jnp.sum(sums[...], axis=0, keepdims=True)
    omega = value[0:1, 1:2] / value[0:1, 0:1]
    out[...] = x[...] + omega * q[...]


def per_device(rhs, diagonal, blocks, block_cols, counts):
    rows = lax.axis_size("rows")
    core_groups = [list(range(c, rows, 2)) for c in range(2)]
    partner = [(r, r ^ 1) for r in range(rows)]
    core = (lax.axis_index("rows") % 2).astype(jnp.int32).reshape(1)
    shadow = rhs.T
    diag = diagonal.reshape(1, 2 * BS)
    vec = sds(S, 2 * BS)
    small = sds(S, S)
    message = sds(16, 2 * S + TILE, BS)

    def among(x):
        return lax.all_to_all(x, "rows", 0, 0, tiled=True, axis_index_groups=core_groups)

    def across(x):
        return lax.all_to_all(x, "cols", 0, 0, tiled=True)

    def product(own):
        peer = lax.ppermute(own, "rows", partner)
        out = call(
            product_body, sds(8, own.shape[1], BS), [VMEM, VMEM, VMEM, SMEM, SMEM],
            own, peer, packed, block_cols, core, name="product",
        )
        return across(out)

    piece = jnp.concatenate([shadow[:, :BS], shadow[:, BS:]], axis=0)
    shadow_rows = across(jnp.broadcast_to(piece[None], (8, 2 * S, BS)))
    packed, mine, other = call(
        prepare_body,
        (sds(16, 2 * BS, 2 * BS, dtype=jnp.bfloat16), sds(16, 2 * S, BS), sds(16, 2 * S, BS)),
        [VMEM, VMEM, SMEM, SMEM, SMEM],
        blocks, shadow_rows, block_cols, counts, core,
        name="prepare", scratch=[pltpu.VMEM((64, S, BS), F32)],
    )
    mine = mine + lax.ppermute(other, "rows", partner)
    both = jnp.concatenate([mine, jnp.broadcast_to(piece[None], (16, 2 * S, BS))], axis=1)
    arrived = among(both)
    parts = product(arrived[:, 2 * S :])
    v, w, msg = call(
        first_body, (vec, vec, message), [VMEM] * 4, parts, arrived, shadow, diag, name="first"
    )
    parts = product(among(msg))
    q, x, u, base, t, cross, msg = call(
        lead_body, (vec, vec, vec, vec, vec, small, message), [VMEM] * 5,
        parts, shadow, diag, v, w, name="lead",
    )
    for iteration in range(1, ITERS):
        parts = product(among(msg))
        q, x, v, p, matrix, msg = call(
            even_body, (vec, vec, vec, vec, small, message), [VMEM] * 10,
            parts, shadow, diag, w, q, x, u, base, t, cross, name="even",
        )
        parts = product(among(msg))
        if iteration < ITERS - 1:
            u, base, t, cross, msg = call(
                odd_body, (vec, vec, vec, small, message), [VMEM] * 8,
                parts, shadow, diag, w, q, v, p, matrix, name="odd",
            )
    sums = call(last_body, sds(1, BS), [VMEM] * 3, parts, diag, q, name="last")
    everyone = rows * lax.axis_size("cols")
    sums = jnp.broadcast_to(sums[None], (everyone, 1, BS))
    sums = lax.all_to_all(sums, ("rows", "cols"), 0, 0, tiled=True)
    out = call(end_body, vec, [VMEM] * 3, sums.reshape(everyone, BS), x, q, name="end")
    return out.T


def solution(mesh):
    in_specs = (
        P(("rows", "cols"), None),
        P(("rows", "cols")),
        P("rows", "cols", None, None),
        P("rows", "cols"),
        P("rows", "cols"),
    )
    out_specs = P(("rows", "cols"), None)
    return jax.shard_map(
        per_device, mesh=mesh, in_specs=in_specs, out_specs=out_specs, check_vma=False
    )
```

time: 826 us -> 350 us (0.42); the launches traced: 813 us -> 348 us
  other arithmetic: 170 us -> 1.03 us
  local copies, waits for them, and re-layouts: 133 us -> 11.4 us
  blocking collectives: 336 us -> 224 us
  waiting for transfers between devices: 83.5 us -> 15.6 us
  Pallas kernels: 0 us -> 59.9 us
  matrix products: 37.5 us -> 0 us
  starting transfers between devices: 45 us -> 35.6 us
    slice x229 -> x2, local copies, waits for them, and re-layouts: 90.4 us -> 0.73 us  [the longest x1 0.72 us: per_device(): piece = jnp.concatenate([shadow[:, :BS], shadow[:, BS:]], axis=0)]
    all_to_all x17, blocking collectives: 307 us -> 224 us  [the longest x8 115 us: among(): lax.all_to_all(x, 'rows', 0, 0, tiled=True, axis_index_groups=core_groups)]
    all_to_all x7 -> x1, waiting for transfers between devices: 83.5 us -> 4.26 us  [across(): return lax.all_to_all(x, 'cols', 0, 0, tiled=True)]
    div x112 -> x0, other arithmetic: 72.2 us -> none  [solve_block(): pivot_row = joined[index] / joined[index, index]]
    mul x105 -> x0, other arithmetic: 67.2 us -> none  [solve_block(): joined = joined - joined[:, index:index + 1] * pivot_row[None, :]]
    pallas_call x0 -> x18, Pallas kernels: none -> 59.9 us  [call(): pl.pallas_call(body, out_shape=outs, in_specs=specs, out_specs=jax.tree.m...]
    dot_general x31 -> x0, matrix products: 37.5 us -> none  [the longest x8 15.1 us: block_rows(): jnp.einsum('rkij,rkjs->ris', blocks, picked, precision=lax.Precision.HIGH...]
    all_to_all x7 -> x1, starting transfers between devices: 45 us -> 7.47 us  [across(): return lax.all_to_all(x, 'cols', 0, 0, tiled=True)]
  transfers between devices with their start and end apart: 7 -> 10, of which waited for: 7 -> 10; matrix products, arithmetic and copies ran while one was open for 1% -> 1% of each run, Pallas kernels for 0% -> 0%
where the time goes in v1:
time: 350 us; the launch traced here: 348 us
  blocking collectives  224 us (64%)
  Pallas kernels  59.9 us (17%)
  starting transfers between devices  35.6 us (10%)
  waiting for transfers between devices  15.6 us (4%)
  local copies, waits for them, and re-layouts  11.4 us (3%)
    all_to_all x8, blocking collectives, among(): lax.all_to_all(x, 'rows', 0, 0, tiled=True, axis_index_groups=core_groups)  115 us
    all_to_all x8, blocking collectives, across(): return lax.all_to_all(x, 'cols', 0, 0, tiled=True)  89.3 us
    pallas_call x18, Pallas kernels, call(): pl.pallas_call(body, out_shape=outs, in_specs=specs, out_specs=jax.tree.m...  59.9 us
    ppermute x8, starting transfers between devices, product(): peer = lax.ppermute(own, 'rows', partner)  26 us
    all_to_all x1, blocking collectives, per_device(): sums = lax.all_to_all(sums, ('rows', 'cols'), 0, 0, tiled=True)  20.2 us
    ppermute x8, waiting for transfers between devices, product(): peer = lax.ppermute(own, 'rows', partner)  9.95 us
    unnamed x38, local copies, waits for them, and re-layouts  9.28 us
    all_to_all x1, starting transfers between devices, across(): return lax.all_to_all(x, 'cols', 0, 0, tiled=True)  7.47 us
  transfers between devices with their start and end apart: 10, of which 10 were waited for; matrix products, arithmetic and copies ran while one was open for 1% of the time, Pallas kernels for 0%

profile of v1, /device:TPU:1, one launch (start us, length us, event | category | flops | bytes accessed | tf_op | source)
XLA Modules:
  0.0 348.0 jit_solution(3033791016174689975)
XLA Ops:
  1.4 7.5 %all-to-all-start = ((f32[8,32,128]{2,1,0:T(8,128)}), f32[8,32,128]{2,1,0:T(8,128)S(1)}, u32[]{:S(2)}, u32[]{:S(2)}) async-start(f32[8,32,128]{2,1,0:T(8,128)} %broadcast_in_dim.8), calls=%async_computation | async-start | bytes 262144 | tf_op jit(solution)/shard_map/all_to_all | solution.py:258
  11.5 4.3 %all-to-all-done.shadow_rows = f32[8,32,128]{2,1,0:T(8,128)S(1)} async-done(((f32[8,32,128]{2,1,0:T(8,128)}), f32[8,32,128]{2,1,0:T(8,128)S(1)}, u32[]{:S(2)}, u32[]{:S(2)}) %all-to-all-start) | async-done | bytes 131104 | tf_op jit(solution)/shard_map/all_to_all | solution.py:258
  16.4 6.7 %prepare.1 = (bf16[16,256,256]{2,1,0:T(8,128)(2,1)}, f32[16,32,128]{2,1,0:T(8,128)}, f32[16,32,128]{2,1,0:T(8,128)}) custom-call(f32[16,2,128,128]{3,2,1,0:T(8,128)} %blocks.1, f32[8,32,128]{2,1,0:T(8,128)} %copy-done.9, s32[16,2]{1,0:T(8,128)} %copy.16.cols, s32[16,1]{1,0:T(8,128)} %copy.17.counts, s32[1]{0:T(128)} %bitcast.1.core), custom_call_target="tpu_custom_call" | custom-call | tf_op jit(solution)/shard_map/prepare/pallas_call | solution.py:23
  27.7 21.8 %all_to_all.90.arrived = f32[16,64,128]{2,1,0:T(8,128)S(1)} all-to-all(f32[16,64,128]{2,1,0:T(8,128)S(1)} %pad_maximum_fusion), channel_id=1, replica_groups={{0,16,32,48,64,80,96,112,128,144,160,176,192,208,224,240},{8,24,40,56,7..., dimensions={0} | all-to-all | bytes 1048576 | tf_op jit(solution)/shard_map/all_to_all | solution.py:255
  57.1 10.9 %all_to_all.91.parts = f32[8,32,128]{2,1,0:T(8,128)} all-to-all(f32[8,32,128]{2,1,0:T(8,128)} %product.8), channel_id=1, replica_groups=mesh['rows'=32,'cols'=8] {'cols'}, dimensions={0} | all-to-all | bytes 262144 | tf_op jit(solution)/shard_map/all_to_all | solution.py:258
  70.1 13.4 %all_to_all.92.own = f32[16,40,128]{2,1,0:T(8,128)S(1)} all-to-all(f32[16,40,128]{2,1,0:T(8,128)} %get-tuple-element.46), channel_id=1, replica_groups={{0,16,32,48,64,80,96,112,128,144,160,176,192,208,224,240},{8,24,40,56,7..., dimensions={0} | all-to-all | bytes 655360 | tf_op jit(solution)/shard_map/all_to_all | solution.py:255
  91.8 11.1 %all_to_all.93.parts = f32[8,40,128]{2,1,0:T(8,128)} all-to-all(f32[8,40,128]{2,1,0:T(8,128)} %product.9), channel_id=1, replica_groups=mesh['rows'=32,'cols'=8] {'cols'}, dimensions={0} | all-to-all | bytes 327680 | tf_op jit(solution)/shard_map/all_to_all | solution.py:258
  102.9 5.2 %lead.1 = (f32[16,256]{1,0:T(8,128)}, f32[16,256]{1,0:T(8,128)}, f32[16,256]{1,0:T(8,128)}, f32[16,256]{1,0:T(8,128)}, f32[16,256]{1,0:T(8,128)}, /*index=5*/f32[16,16]{1,0:T(8,128)}, f32[16,40,128]{2,1,0:T(8,128)}) custom-call(f32[8,40,128]{2,1,0:T(8,128)} %all_to_all.93.parts, f32[16,256]{1,0:T(8,128)} %bitcast.8, f32[1,256]{1,0:T(1,128)} %bitcast.16, ...), custom_call_target="tpu_custom_call" | custom-call | tf_op jit(solution)/shard_map/lead/pallas_call | solution.py:23
  108.1 13.4 %all_to_all.94.own = f32[16,40,128]{2,1,0:T(8,128)S(1)} all-to-all(f32[16,40,128]{2,1,0:T(8,128)} %get-tuple-element.49), channel_id=1, replica_groups={{0,16,32,48,64,80,96,112,128,144,160,176,192,208,224,240},{8,24,40,56,7..., dimensions={0} | all-to-all | bytes 655360 | tf_op jit(solution)/shard_map/all_to_all | solution.py:255
  121.5 3.3 collective-permute-start.3
  129.8 11.2 %all_to_all.95.parts = f32[8,40,128]{2,1,0:T(8,128)} all-to-all(f32[8,40,128]{2,1,0:T(8,128)} %product.10), channel_id=1, replica_groups=mesh['rows'=32,'cols'=8] {'cols'}, dimensions={0} | all-to-all | bytes 327680 | tf_op jit(solution)/shard_map/all_to_all | solution.py:258
  141.1 3.8 %even.3 = (f32[16,256]{1,0:T(8,128)}, f32[16,256]{1,0:T(8,128)}, f32[16,256]{1,0:T(8,128)}, f32[16,256]{1,0:T(8,128)}, f32[16,16]{1,0:T(8,128)}, /*index=5*/f32[16,40,128]{2,1,0:T(8,128)}) custom-call(f32[8,40,128]{2,1,0:T(8,128)} %all_to_all.95.parts, f32[16,256]{1,0:T(8,128)} %bitcast.9, f32[1,256]{1,0:T(1,128)} %bitcast.17, ...), custom_call_target="tpu_custom_call" | custom-call | tf_op jit(solution)/shard_map/even/pallas_call | solution.py:23
  144.9 13.3 %all_to_all.96.own = f32[16,40,128]{2,1,0:T(8,128)S(1)} all-to-all(f32[16,40,128]{2,1,0:T(8,128)} %get-tuple-element.56), channel_id=1, replica_groups={{0,16,32,48,64,80,96,112,128,144,160,176,192,208,224,240},{8,24,40,56,7..., dimensions={0} | all-to-all | bytes 655360 | tf_op jit(solution)/shard_map/all_to_all | solution.py:255
  158.1 3.3 collective-permute-start.4
  166.5 11.2 %all_to_all.97.parts = f32[8,40,128]{2,1,0:T(8,128)} all-to-all(f32[8,40,128]{2,1,0:T(8,128)} %product.11), channel_id=1, replica_groups=mesh['rows'=32,'cols'=8] {'cols'}, dimensions={0} | all-to-all | bytes 327680 | tf_op jit(solution)/shard_map/all_to_all | solution.py:258
  177.7 3.6 %odd.2 = (f32[16,256]{1,0:T(8,128)}, f32[16,256]{1,0:T(8,128)}, f32[16,256]{1,0:T(8,128)}, f32[16,16]{1,0:T(8,128)}, f32[16,40,128]{2,1,0:T(8,128)}) custom-call(f32[8,40,128]{2,1,0:T(8,128)} %all_to_all.97.parts, f32[16,256]{1,0:T(8,128)} %bitcast.10, f32[1,256]{1,0:T(1,128)} %bitcast.18, f32[16,256]{1,0:T(8,128)} %get-tuple-element.48.weights, ...), custom_call_target="tpu_custom_call" | custom-call | tf_op jit(solution)/shard_map/odd/pallas_call | solution.py:23
  181.3 13.3 %all_to_all.98.own = f32[16,40,128]{2,1,0:T(8,128)S(1)} all-to-all(f32[16,40,128]{2,1,0:T(8,128)} %get-tuple-element.61), channel_id=1, replica_groups={{0,16,32,48,64,80,96,112,128,144,160,176,192,208,224,240},{8,24,40,56,7..., dimensions={0} | all-to-all | bytes 655360 | tf_op jit(solution)/shard_map/all_to_all | solution.py:255
  194.6 3.3 collective-permute-start.5
  202.9 11.2 %all_to_all.99.parts = f32[8,40,128]{2,1,0:T(8,128)} all-to-all(f32[8,40,128]{2,1,0:T(8,128)} %product.12), channel_id=1, replica_groups=mesh['rows'=32,'cols'=8] {'cols'}, dimensions={0} | all-to-all | bytes 327680 | tf_op jit(solution)/shard_map/all_to_all | solution.py:258
  214.1 3.8 %even.4 = (f32[16,256]{1,0:T(8,128)}, f32[16,256]{1,0:T(8,128)}, f32[16,256]{1,0:T(8,128)}, f32[16,256]{1,0:T(8,128)}, f32[16,16]{1,0:T(8,128)}, /*index=5*/f32[16,40,128]{2,1,0:T(8,128)}) custom-call(f32[8,40,128]{2,1,0:T(8,128)} %all_to_all.99.parts, f32[16,256]{1,0:T(8,128)} %bitcast.11, f32[1,256]{1,0:T(1,128)} %bitcast.19, ...), custom_call_target="tpu_custom_call" | custom-call | tf_op jit(solution)/shard_map/even/pallas_call | solution.py:23
  217.9 13.3 %all_to_all.100.own = f32[16,40,128]{2,1,0:T(8,128)S(1)} all-to-all(f32[16,40,128]{2,1,0:T(8,128)} %get-tuple-element.67), channel_id=1, replica_groups={{0,16,32,48,64,80,96,112,128,144,160,176,192,208,224,240},{8,24,40,56,7..., dimensions={0} | all-to-all | bytes 655360 | tf_op jit(solution)/shard_map/all_to_all | solution.py:255
  231.2 3.3 collective-permute-start.6
  239.6 11.2 %all_to_all.101.parts = f32[8,40,128]{2,1,0:T(8,128)} all-to-all(f32[8,40,128]{2,1,0:T(8,128)} %product.13), channel_id=1, replica_groups=mesh['rows'=32,'cols'=8] {'cols'}, dimensions={0} | all-to-all | bytes 327680 | tf_op jit(solution)/shard_map/all_to_all | solution.py:258
  250.8 3.6 %odd.3 = (f32[16,256]{1,0:T(8,128)}, f32[16,256]{1,0:T(8,128)}, f32[16,256]{1,0:T(8,128)}, f32[16,16]{1,0:T(8,128)}, f32[16,40,128]{2,1,0:T(8,128)}) custom-call(f32[8,40,128]{2,1,0:T(8,128)} %all_to_all.101.parts, f32[16,256]{1,0:T(8,128)} %bitcast.12, f32[1,256]{1,0:T(1,128)} %bitcast.20, f32[16,256]{1,0:T(8,128)} %get-tuple-element.48.weights, ...), custom_call_target="tpu_custom_call" | custom-call | tf_op jit(solution)/shard_map/odd/pallas_call | solution.py:23
  254.4 13.3 %all_to_all.102.own = f32[16,40,128]{2,1,0:T(8,128)S(1)} all-to-all(f32[16,40,128]{2,1,0:T(8,128)} %get-tuple-element.72), channel_id=1, replica_groups={{0,16,32,48,64,80,96,112,128,144,160,176,192,208,224,240},{8,24,40,56,7..., dimensions={0} | all-to-all | bytes 655360 | tf_op jit(solution)/shard_map/all_to_all | solution.py:255
  267.6 3.3 collective-permute-start.7
  276.0 11.2 %all_to_all.103.parts = f32[8,40,128]{2,1,0:T(8,128)} all-to-all(f32[8,40,128]{2,1,0:T(8,128)} %product.14), channel_id=1, replica_groups=mesh['rows'=32,'cols'=8] {'cols'}, dimensions={0} | all-to-all | bytes 327680 | tf_op jit(solution)/shard_map/all_to_all | solution.py:258
  287.2 3.8 %even.5 = (f32[16,256]{1,0:T(8,128)}, f32[16,256]{1,0:T(8,128)}, f32[16,256]{1,0:T(8,128)}, f32[16,256]{1,0:T(8,128)}, f32[16,16]{1,0:T(8,128)}, /*index=5*/f32[16,40,128]{2,1,0:T(8,128)}) custom-call(f32[8,40,128]{2,1,0:T(8,128)} %all_to_all.103.parts, f32[16,256]{1,0:T(8,128)} %bitcast.13, f32[1,256]{1,0:T(1,128)} %bitcast.21, ...), custom_call_target="tpu_custom_call" | custom-call | tf_op jit(solution)/shard_map/even/pallas_call | solution.py:23
  291.0 13.3 %all_to_all.104.own = f32[16,40,128]{2,1,0:T(8,128)S(1)} all-to-all(f32[16,40,128]{2,1,0:T(8,128)} %get-tuple-element.78), channel_id=1, replica_groups={{0,16,32,48,64,80,96,112,128,144,160,176,192,208,224,240},{8,24,40,56,7..., dimensions={0} | all-to-all | bytes 655360 | tf_op jit(solution)/shard_map/all_to_all | solution.py:255
  304.3 3.3 collective-permute-start.8
  312.6 11.2 %all_to_all.105.parts = f32[8,40,128]{2,1,0:T(8,128)} all-to-all(f32[8,40,128]{2,1,0:T(8,128)} %product.15), channel_id=1, replica_groups=mesh['rows'=32,'cols'=8] {'cols'}, dimensions={0} | all-to-all | bytes 327680 | tf_op jit(solution)/shard_map/all_to_all | solution.py:258
  326.1 20.2 %all_to_all.106 = f32[256,1,128]{2,1,0:T(1,128)} all-to-all(f32[256,1,128]{2,1,0:T(1,128)S(1)} %broadcast_in_dim.11), channel_id=1, replica_groups=mesh['rows'=32,'cols'=8] {'rows','cols'}, dimensions={0} | all-to-all | bytes 262144 | tf_op jit(solution)/shard_map/all_to_all | solution.py:304
  (69 shorter events, 61.4 us)
Async XLA Ops:
  1.4 14.4 %all-to-all-start = ((f32[8,32,128]{2,1,0:T(8,128)}), f32[8,32,128]{2,1,0:T(8,128)S(1)}, u32[]{:S(2)}, u32[]{:S(2)}) async-start(f32[8,32,128]{2,1,0:T(8,128)} %broadcast_in_dim.8), calls=%async_computation | async-start | bytes 262144 | tf_op jit(solution)/shard_map/all_to_all | solution.py:258
  15.8 0.7 copy-start.9
  23.1 3.5 collective-permute-start
  49.4 18.6 %copy-start = (f32[16,64,128]{2,1,0:T(8,128)}, f32[16,64,128]{2,1,0:T(8,128)S(1)}, u32[]{:S(2)}) copy-start(f32[16,64,128]{2,1,0:T(8,128)S(1)} %all_to_all.90.arrived) | copy-start | bytes 1572868
  49.4 4.0 %copy-start.8 = (f32[16,32,128]{2,1,0:T(8,128)}, f32[16,32,128]{2,1,0:T(8,128)S(1)}, u32[]{:S(2)}) copy-start(f32[16,32,128]{2,1,0:T(8,128)S(1)} %slice.14.own) | copy-start | bytes 786436
  49.4 4.0 %collective-permute-start.1 = (f32[16,32,128]{2,1,0:T(8,128)S(1)}, f32[16,32,128]{2,1,0:T(8,128)S(1)}, u32[]{:S(2)}, u32[]{:S(2)}) collective-permute-start(f32[16,32,128]{2,1,0:T(8,128)S(1)} %slice.14.own), channel_id=1, source_target_pairs={{0,8},{8,0},{16,24},{24,16},{32,40},{40,32},{48,56},{56,48},{64,72... | collective-permute-start | bytes 786440 | tf_op jit(solution)/shard_map/ppermute | solution.py:261
  53.4 0.7 copy-start.17
  83.5 4.5 %copy-start.2 = (f32[16,40,128]{2,1,0:T(8,128)}, f32[16,40,128]{2,1,0:T(8,128)S(1)}, u32[]{:S(2)}) copy-start(f32[16,40,128]{2,1,0:T(8,128)S(1)} %all_to_all.92.own) | copy-start | bytes 983044
  83.5 4.5 %collective-permute-start.2 = (f32[16,40,128]{2,1,0:T(8,128)S(1)}, f32[16,40,128]{2,1,0:T(8,128)S(1)}, u32[]{:S(2)}, u32[]{:S(2)}) collective-permute-start(f32[16,40,128]{2,1,0:T(8,128)S(1)} %all_to_all.92.own), channel_id=1, source_target_pairs={{0,8},{8,0},{16,24},{24,16},{32,40},{40,32},{48,56},{56,48},{64,72... | collective-permute-start | bytes 983048 | tf_op jit(solution)/shard_map/ppermute | solution.py:261
  88.0 0.7 copy-start.11
  121.5 4.6 %copy-start.3 = (f32[16,40,128]{2,1,0:T(8,128)}, f32[16,40,128]{2,1,0:T(8,128)S(1)}, u32[]{:S(2)}) copy-start(f32[16,40,128]{2,1,0:T(8,128)S(1)} %all_to_all.94.own) | copy-start | bytes 983044
  121.5 4.6 %collective-permute-start.3 = (f32[16,40,128]{2,1,0:T(8,128)S(1)}, f32[16,40,128]{2,1,0:T(8,128)S(1)}, u32[]{:S(2)}, u32[]{:S(2)}) collective-permute-start(f32[16,40,128]{2,1,0:T(8,128)S(1)} %all_to_all.94.own), channel_id=1, source_target_pairs={{0,8},{8,0},{16,24},{24,16},{32,40},{40,32},{48,56},{56,48},{64,72... | collective-permute-start | bytes 983048 | tf_op jit(solution)/shard_map/ppermute | solution.py:261
  126.1 0.7 copy-start.12
  158.1 4.6 %copy-start.4 = (f32[16,40,128]{2,1,0:T(8,128)}, f32[16,40,128]{2,1,0:T(8,128)S(1)}, u32[]{:S(2)}) copy-start(f32[16,40,128]{2,1,0:T(8,128)S(1)} %all_to_all.96.own) | copy-start | bytes 983044
  158.1 4.6 %collective-permute-start.4 = (f32[16,40,128]{2,1,0:T(8,128)S(1)}, f32[16,40,128]{2,1,0:T(8,128)S(1)}, u32[]{:S(2)}, u32[]{:S(2)}) collective-permute-start(f32[16,40,128]{2,1,0:T(8,128)S(1)} %all_to_all.96.own), channel_id=1, source_target_pairs={{0,8},{8,0},{16,24},{24,16},{32,40},{40,32},{48,56},{56,48},{64,72... | collective-permute-start | bytes 983048 | tf_op jit(solution)/shard_map/ppermute | solution.py:261
  162.7 0.7 copy-start.13
  194.6 4.6 %copy-start.5 = (f32[16,40,128]{2,1,0:T(8,128)}, f32[16,40,128]{2,1,0:T(8,128)S(1)}, u32[]{:S(2)}) copy-start(f32[16,40,128]{2,1,0:T(8,128)S(1)} %all_to_all.98.own) | copy-start | bytes 983044
  194.6 4.6 %collective-permute-start.5 = (f32[16,40,128]{2,1,0:T(8,128)S(1)}, f32[16,40,128]{2,1,0:T(8,128)S(1)}, u32[]{:S(2)}, u32[]{:S(2)}) collective-permute-start(f32[16,40,128]{2,1,0:T(8,128)S(1)} %all_to_all.98.own), channel_id=1, source_target_pairs={{0,8},{8,0},{16,24},{24,16},{32,40},{40,32},{48,56},{56,48},{64,72... | collective-permute-start | bytes 983048 | tf_op jit(solution)/shard_map/ppermute | solution.py:261
  199.2 0.7 copy-start.14
  231.2 4.6 %copy-start.6 = (f32[16,40,128]{2,1,0:T(8,128)}, f32[16,40,128]{2,1,0:T(8,128)S(1)}, u32[]{:S(2)}) copy-start(f32[16,40,128]{2,1,0:T(8,128)S(1)} %all_to_all.100.own) | copy-start | bytes 983044
  231.2 4.6 %collective-permute-start.6 = (f32[16,40,128]{2,1,0:T(8,128)S(1)}, f32[16,40,128]{2,1,0:T(8,128)S(1)}, u32[]{:S(2)}, u32[]{:S(2)}) collective-permute-start(f32[16,40,128]{2,1,0:T(8,128)S(1)} %all_to_all.100.own), channel_id=1, source_target_pairs={{0,8},{8,0},{16,24},{24,16},{32,40},{40,32},{48,56},{56,48},{64,72... | collective-permute-start | bytes 983048 | tf_op jit(solution)/shard_map/ppermute | solution.py:261
  235.8 0.7 copy-start.15
  267.6 4.6 %copy-start.7 = (f32[16,40,128]{2,1,0:T(8,128)}, f32[16,40,128]{2,1,0:T(8,128)S(1)}, u32[]{:S(2)}) copy-start(f32[16,40,128]{2,1,0:T(8,128)S(1)} %all_to_all.102.own) | copy-start | bytes 983044
  267.6 4.6 %collective-permute-start.7 = (f32[16,40,128]{2,1,0:T(8,128)S(1)}, f32[16,40,128]{2,1,0:T(8,128)S(1)}, u32[]{:S(2)}, u32[]{:S(2)}) collective-permute-start(f32[16,40,128]{2,1,0:T(8,128)S(1)} %all_to_all.102.own), channel_id=1, source_target_pairs={{0,8},{8,0},{16,24},{24,16},{32,40},{40,32},{48,56},{56,48},{64,72... | collective-permute-start | bytes 983048 | tf_op jit(solution)/shard_map/ppermute | solution.py:261
  272.2 0.7 copy-start.16
  304.3 4.6 %copy-start.1 = (f32[16,40,128]{2,1,0:T(8,128)}, f32[16,40,128]{2,1,0:T(8,128)S(1)}, u32[]{:S(2)}) copy-start(f32[16,40,128]{2,1,0:T(8,128)S(1)} %all_to_all.104.own) | copy-start | bytes 983044
  304.3 4.6 %collective-permute-start.8 = (f32[16,40,128]{2,1,0:T(8,128)S(1)}, f32[16,40,128]{2,1,0:T(8,128)S(1)}, u32[]{:S(2)}, u32[]{:S(2)}) collective-permute-start(f32[16,40,128]{2,1,0:T(8,128)S(1)} %all_to_all.104.own), channel_id=1, source_target_pairs={{0,8},{8,0},{16,24},{24,16},{32,40},{40,32},{48,56},{56,48},{64,72... | collective-permute-start | bytes 983048 | tf_op jit(solution)/shard_map/ppermute | solution.py:261
  308.9 0.7 copy-start.10

commit v2 on v1

--- a/solution.py
+++ b/solution.py
@@ -16,17 +16,22 @@
 
 
 def sds(*shape, dtype=F32):
-    return jax.ShapeDtypeStruct(shape, dtype)
+    return pltpu.VMEM(shape, dtype)
 
 
 def call(body, outs, specs, *args, name, scratch=()):
+    args = [
+        pltpu.with_memory_space_constraint(a, pltpu.VMEM) if spec is VMEM else a
+        for a, spec in zip(args, specs)
+    ]
     return pl.pallas_call(
         body,
         out_shape=outs,
         in_specs=specs,
-        out_specs=jax.tree.map(lambda _: VMEM, outs),
+        out_specs=tuple(VMEM for _ in outs) if isinstance(outs, tuple) else VMEM,
         scratch_shapes=scratch,
         name=name,
+        compiler_params=pltpu.CompilerParams(vmem_limit_bytes=8 << 20),
     )(*args)
 
 
@@ -41,6 +46,14 @@
 def halves(x):
     high = x.astype(jnp.bfloat16)
     return high, (x - high.astype(F32)).astype(jnp.bfloat16)
+
+
+def chip_of(seat):
+    return (seat // 2 % 2) * 8 + (seat % 2) * 4 + seat // 4
+
+
+def seat_of(chip):
+    return (chip % 4) * 4 + (chip // 8) * 2 + chip // 4 % 2
 
 
 def wide(ref, at=()):
@@ -116,8 +129,8 @@
     me = core[0]
     for m in range(16):
         for b in range(2):
-            mine[m, b * S : (b + 1) * S] = acc[m * 4 + me * 2 + b]
-            other[m, b * S : (b + 1) * S] = acc[m * 4 + (1 - me) * 2 + b]
+            mine[m, b * S : (b + 1) * S] = acc[chip_of(m) * 4 + me * 2 + b]
+            other[m, b * S : (b + 1) * S] = acc[chip_of(m) * 4 + (1 - me) * 2 + b]
 
 
 def product_body(own, peer, packed, cols, core, out):
@@ -134,7 +147,7 @@
         picked = []
         for k in range(2):
             col = cols[i, k]
-            m = col // 4
+            m = seat_of(col // 4)
             b = pl.multiple_of((col % 2) * S, S)
             here = own[m, pl.ds(b, S), :]
             there = peer[m, pl.ds(b, S), :]
@@ -242,7 +255,7 @@
 
 def per_device(rhs, diagonal, blocks, block_cols, counts):
     rows = lax.axis_size("rows")
-    core_groups = [list(range(c, rows, 2)) for c in range(2)]
+    core_groups = [[2 * chip_of(m) + c for m in range(rows // 2)] for c in range(2)]
     partner = [(r, r ^ 1) for r in range(rows)]
     core = (lax.axis_index("rows") % 2).astype(jnp.int32).reshape(1)
     shadow = rhs.T

time: 350 us -> 304 us (0.87)
  Pallas kernels: 59.9 us -> 31.4 us
  blocking collectives: 224 us -> 213 us
  local copies, waits for them, and re-layouts: 11.4 us -> 5.18 us
    pallas_call x18, Pallas kernels: 59.9 us -> 31.4 us  [call(): pl.pallas_call(body, out_shape=outs, in_specs=specs, out_specs=tuple((VME...]
    all_to_all x8, blocking collectives: 89.3 us -> 80.6 us  [across(): return lax.all_to_all(x, 'cols', 0, 0, tiled=True)]
    unnamed x38 -> x9, local copies, waits for them, and re-layouts: 9.28 us -> 3.7 us
  transfers between devices with their start and end apart: 10 -> 10, of which waited for: 10 -> 10; matrix products, arithmetic and copies ran while one was open for 1% -> 0% of each run, Pallas kernels for 0% -> 0%
where the time goes in v2:
time: 304 us; the launch traced here: 303 us
  blocking collectives  213 us (70%)
  starting transfers between devices  36.9 us (12%)
  Pallas kernels  31.4 us (10%)
  waiting for transfers between devices  16.6 us (5%)
  local copies, waits for them, and re-layouts  5.18 us (2%)
    all_to_all x8, blocking collectives, among(): lax.all_to_all(x, 'rows', 0, 0, tiled=True, axis_index_groups=core_groups)  113 us
    all_to_all x8, blocking collectives, across(): return lax.all_to_all(x, 'cols', 0, 0, tiled=True)  80.6 us
    pallas_call x18, Pallas kernels, call(): pl.pallas_call(body, out_shape=outs, in_specs=specs, out_specs=tuple((VME...  31.4 us
    ppermute x8, starting transfers between devices, product(): peer = lax.ppermute(own, 'rows', partner)  27.3 us
    all_to_all x1, blocking collectives, per_device(): sums = lax.all_to_all(sums, ('rows', 'cols'), 0, 0, tiled=True)  19.4 us
    ppermute x8, waiting for transfers between devices, product(): peer = lax.ppermute(own, 'rows', partner)  9.95 us
    all_to_all x1, starting transfers between devices, across(): return lax.all_to_all(x, 'cols', 0, 0, tiled=True)  7.47 us
  transfers between devices with their start and end apart: 10, of which 10 were waited for; matrix products, arithmetic and copies ran while one was open for 0% of the time, Pallas kernels for 0%

profile of v2, /device:TPU:1, one launch (start us, length us, event | category | flops | bytes accessed | tf_op | source)
XLA Modules:
  0.0 303.4 jit_solution(1564066168083030520)
XLA Ops:
  1.4 7.5 %all-to-all-start = ((f32[8,32,128]{2,1,0:T(8,128)}), f32[8,32,128]{2,1,0:T(8,128)S(1)}, u32[]{:S(2)}, u32[]{:S(2)}) async-start(f32[8,32,128]{2,1,0:T(8,128)} %broadcast_in_dim.8), calls=%async_computation | async-start | bytes 262144 | tf_op jit(solution)/shard_map/all_to_all | solution.py:271
  10.3 5.4 %all-to-all-done.shadow_rows = f32[8,32,128]{2,1,0:T(8,128)S(1)} async-done(((f32[8,32,128]{2,1,0:T(8,128)}), f32[8,32,128]{2,1,0:T(8,128)S(1)}, u32[]{:S(2)}, u32[]{:S(2)}) %all-to-all-start) | async-done | bytes 131104 | tf_op jit(solution)/shard_map/all_to_all | solution.py:271
  17.4 4.5 %prepare.1 = (bf16[16,256,256]{2,1,0:T(8,128)(2,1)S(1)}, f32[16,32,128]{2,1,0:T(8,128)S(1)}, f32[16,32,128]{2,1,0:T(8,128)S(1)}) custom-call(f32[16,2,128,128]{3,2,1,0:T(8,128)S(1)} %copy-done, f32[8,32,128]{2,1,0:T(8,128)S(1)} %all-to-all-done.shadow_rows, s32[16,2]{1,0:T(8,128)S(1)} %copy.16.cols, s32[16,1]{1,0:T(8,128)S(1)} %copy.17.counts, s32[1]{0:T(128)} %bitcast.1.core), custom_call_target="tpu_custom_call" | custom-call | tf_op jit(solution)/shard_map/prepare/pallas_call | solution.py:27
  21.9 2.2 collective-permute-start
  25.4 24.3 %all_to_all.90.arrived = f32[16,64,128]{2,1,0:T(8,128)S(1)} all-to-all(f32[16,64,128]{2,1,0:T(8,128)S(1)} %pad_maximum_fusion), channel_id=1, replica_groups={{0,64,128,192,16,80,144,208,32,96,160,224,48,112,176,240},{8,72,136,200..., dimensions={0} | all-to-all | bytes 1048576 | tf_op jit(solution)/shard_map/all_to_all | solution.py:268
  54.1 9.8 %all_to_all.91.parts = f32[8,32,128]{2,1,0:T(8,128)S(1)} all-to-all(f32[8,32,128]{2,1,0:T(8,128)S(1)} %product.8), channel_id=1, replica_groups=mesh['rows'=32,'cols'=8] {'cols'}, dimensions={0} | all-to-all | bytes 262144 | tf_op jit(solution)/shard_map/all_to_all | solution.py:271
  64.1 13.0 %all_to_all.92.own = f32[16,40,128]{2,1,0:T(8,128)S(1)} all-to-all(f32[16,40,128]{2,1,0:T(8,128)S(1)} %get-tuple-element.46), channel_id=1, replica_groups={{0,64,128,192,16,80,144,208,32,96,160,224,48,112,176,240},{8,72,136,200..., dimensions={0} | all-to-all | bytes 655360 | tf_op jit(solution)/shard_map/all_to_all | solution.py:268
  77.1 3.6 %collective-permute-start.2 = (f32[16,40,128]{2,1,0:T(8,128)S(1)}, f32[16,40,128]{2,1,0:T(8,128)S(1)}, u32[]{:S(2)}, u32[]{:S(2)}) collective-permute-start(f32[16,40,128]{2,1,0:T(8,128)S(1)} %all_to_all.92.own), channel_id=1, source_target_pairs={{0,8},{8,0},{16,24},{24,16},{32,40},{40,32},{48,56},{56,48},{64,72... | collective-permute-start | bytes 983048 | tf_op jit(solution)/shard_map/ppermute | solution.py:274
  83.6 9.8 %all_to_all.93.parts = f32[8,40,128]{2,1,0:T(8,128)S(1)} all-to-all(f32[8,40,128]{2,1,0:T(8,128)S(1)} %product.9), channel_id=1, replica_groups=mesh['rows'=32,'cols'=8] {'cols'}, dimensions={0} | all-to-all | bytes 327680 | tf_op jit(solution)/shard_map/all_to_all | solution.py:271
  93.4 3.5 %lead.1 = (f32[16,256]{1,0:T(8,128)S(1)}, f32[16,256]{1,0:T(8,128)S(1)}, f32[16,256]{1,0:T(8,128)S(1)}, f32[16,256]{1,0:T(8,128)S(1)}, f32[16,256]{1,0:T(8,128)S...) custom-call(f32[8,40,128]{2,1,0:T(8,128)S(1)} %all_to_all.93.parts, f32[16,256]{1,0:T(8,128)S(1)} %bitcast.9, ...), custom_call_target="tpu_custom_call" | custom-call | tf_op jit(solution)/shard_map/lead/pallas_call | solution.py:27
  96.9 12.7 %all_to_all.94.own = f32[16,40,128]{2,1,0:T(8,128)S(1)} all-to-all(f32[16,40,128]{2,1,0:T(8,128)S(1)} %get-tuple-element.49), channel_id=1, replica_groups={{0,64,128,192,16,80,144,208,32,96,160,224,48,112,176,240},{8,72,136,200..., dimensions={0} | all-to-all | bytes 655360 | tf_op jit(solution)/shard_map/all_to_all | solution.py:268
  109.6 3.6 %collective-permute-start.3 = (f32[16,40,128]{2,1,0:T(8,128)S(1)}, f32[16,40,128]{2,1,0:T(8,128)S(1)}, u32[]{:S(2)}, u32[]{:S(2)}) collective-permute-start(f32[16,40,128]{2,1,0:T(8,128)S(1)} %all_to_all.94.own), channel_id=1, source_target_pairs={{0,8},{8,0},{16,24},{24,16},{32,40},{40,32},{48,56},{56,48},{64,72... | collective-permute-start | bytes 983048 | tf_op jit(solution)/shard_map/ppermute | solution.py:274
  116.0 10.6 %all_to_all.95.parts = f32[8,40,128]{2,1,0:T(8,128)S(1)} all-to-all(f32[8,40,128]{2,1,0:T(8,128)S(1)} %product.10), channel_id=1, replica_groups=mesh['rows'=32,'cols'=8] {'cols'}, dimensions={0} | all-to-all | bytes 327680 | tf_op jit(solution)/shard_map/all_to_all | solution.py:271
  126.6 2.1 even.3
  128.7 12.6 %all_to_all.96.own = f32[16,40,128]{2,1,0:T(8,128)S(1)} all-to-all(f32[16,40,128]{2,1,0:T(8,128)S(1)} %get-tuple-element.56), channel_id=1, replica_groups={{0,64,128,192,16,80,144,208,32,96,160,224,48,112,176,240},{8,72,136,200..., dimensions={0} | all-to-all | bytes 655360 | tf_op jit(solution)/shard_map/all_to_all | solution.py:268
  141.3 3.7 %collective-permute-start.4 = (f32[16,40,128]{2,1,0:T(8,128)S(1)}, f32[16,40,128]{2,1,0:T(8,128)S(1)}, u32[]{:S(2)}, u32[]{:S(2)}) collective-permute-start(f32[16,40,128]{2,1,0:T(8,128)S(1)} %all_to_all.96.own), channel_id=1, source_target_pairs={{0,8},{8,0},{16,24},{24,16},{32,40},{40,32},{48,56},{56,48},{64,72... | collective-permute-start | bytes 983048 | tf_op jit(solution)/shard_map/ppermute | solution.py:274
  147.8 9.9 %all_to_all.97.parts = f32[8,40,128]{2,1,0:T(8,128)S(1)} all-to-all(f32[8,40,128]{2,1,0:T(8,128)S(1)} %product.11), channel_id=1, replica_groups=mesh['rows'=32,'cols'=8] {'cols'}, dimensions={0} | all-to-all | bytes 327680 | tf_op jit(solution)/shard_map/all_to_all | solution.py:271
  159.5 12.7 %all_to_all.98.own = f32[16,40,128]{2,1,0:T(8,128)S(1)} all-to-all(f32[16,40,128]{2,1,0:T(8,128)S(1)} %get-tuple-element.61), channel_id=1, replica_groups={{0,64,128,192,16,80,144,208,32,96,160,224,48,112,176,240},{8,72,136,200..., dimensions={0} | all-to-all | bytes 655360 | tf_op jit(solution)/shard_map/all_to_all | solution.py:268
  172.2 3.6 %collective-permute-start.5 = (f32[16,40,128]{2,1,0:T(8,128)S(1)}, f32[16,40,128]{2,1,0:T(8,128)S(1)}, u32[]{:S(2)}, u32[]{:S(2)}) collective-permute-start(f32[16,40,128]{2,1,0:T(8,128)S(1)} %all_to_all.98.own), channel_id=1, source_target_pairs={{0,8},{8,0},{16,24},{24,16},{32,40},{40,32},{48,56},{56,48},{64,72... | collective-permute-start | bytes 983048 | tf_op jit(solution)/shard_map/ppermute | solution.py:274
  178.7 10.4 %all_to_all.99.parts = f32[8,40,128]{2,1,0:T(8,128)S(1)} all-to-all(f32[8,40,128]{2,1,0:T(8,128)S(1)} %product.12), channel_id=1, replica_groups=mesh['rows'=32,'cols'=8] {'cols'}, dimensions={0} | all-to-all | bytes 327680 | tf_op jit(solution)/shard_map/all_to_all | solution.py:271
  189.1 2.1 even.4
  191.1 12.7 %all_to_all.100.own = f32[16,40,128]{2,1,0:T(8,128)S(1)} all-to-all(f32[16,40,128]{2,1,0:T(8,128)S(1)} %get-tuple-element.67), channel_id=1, replica_groups={{0,64,128,192,16,80,144,208,32,96,160,224,48,112,176,240},{8,72,136,200..., dimensions={0} | all-to-all | bytes 655360 | tf_op jit(solution)/shard_map/all_to_all | solution.py:268
  203.8 3.6 %collective-permute-start.6 = (f32[16,40,128]{2,1,0:T(8,128)S(1)}, f32[16,40,128]{2,1,0:T(8,128)S(1)}, u32[]{:S(2)}, u32[]{:S(2)}) collective-permute-start(f32[16,40,128]{2,1,0:T(8,128)S(1)} %all_to_all.100.own), channel_id=1, source_target_pairs={{0,8},{8,0},{16,24},{24,16},{32,40},{40,32},{48,56},{56,48},{64,72... | collective-permute-start | bytes 983048 | tf_op jit(solution)/shard_map/ppermute | solution.py:274
  210.2 9.9 %all_to_all.101.parts = f32[8,40,128]{2,1,0:T(8,128)S(1)} all-to-all(f32[8,40,128]{2,1,0:T(8,128)S(1)} %product.13), channel_id=1, replica_groups=mesh['rows'=32,'cols'=8] {'cols'}, dimensions={0} | all-to-all | bytes 327680 | tf_op jit(solution)/shard_map/all_to_all | solution.py:271
  221.9 12.7 %all_to_all.102.own = f32[16,40,128]{2,1,0:T(8,128)S(1)} all-to-all(f32[16,40,128]{2,1,0:T(8,128)S(1)} %get-tuple-element.72), channel_id=1, replica_groups={{0,64,128,192,16,80,144,208,32,96,160,224,48,112,176,240},{8,72,136,200..., dimensions={0} | all-to-all | bytes 655360 | tf_op jit(solution)/shard_map/all_to_all | solution.py:268
  234.6 3.6 %collective-permute-start.7 = (f32[16,40,128]{2,1,0:T(8,128)S(1)}, f32[16,40,128]{2,1,0:T(8,128)S(1)}, u32[]{:S(2)}, u32[]{:S(2)}) collective-permute-start(f32[16,40,128]{2,1,0:T(8,128)S(1)} %all_to_all.102.own), channel_id=1, source_target_pairs={{0,8},{8,0},{16,24},{24,16},{32,40},{40,32},{48,56},{56,48},{64,72... | collective-permute-start | bytes 983048 | tf_op jit(solution)/shard_map/ppermute | solution.py:274
  241.1 10.4 %all_to_all.103.parts = f32[8,40,128]{2,1,0:T(8,128)S(1)} all-to-all(f32[8,40,128]{2,1,0:T(8,128)S(1)} %product.14), channel_id=1, replica_groups=mesh['rows'=32,'cols'=8] {'cols'}, dimensions={0} | all-to-all | bytes 327680 | tf_op jit(solution)/shard_map/all_to_all | solution.py:271
  251.5 2.6 even.5
  254.1 12.6 %all_to_all.104.own = f32[16,40,128]{2,1,0:T(8,128)S(1)} all-to-all(f32[16,40,128]{2,1,0:T(8,128)S(1)} %get-tuple-element.78), channel_id=1, replica_groups={{0,64,128,192,16,80,144,208,32,96,160,224,48,112,176,240},{8,72,136,200..., dimensions={0} | all-to-all | bytes 655360 | tf_op jit(solution)/shard_map/all_to_all | solution.py:268
  266.7 3.6 %collective-permute-start.8 = (f32[16,40,128]{2,1,0:T(8,128)S(1)}, f32[16,40,128]{2,1,0:T(8,128)S(1)}, u32[]{:S(2)}, u32[]{:S(2)}) collective-permute-start(f32[16,40,128]{2,1,0:T(8,128)S(1)} %all_to_all.104.own), channel_id=1, source_target_pairs={{0,8},{8,0},{16,24},{24,16},{32,40},{40,32},{48,56},{56,48},{64,72... | collective-permute-start | bytes 983048 | tf_op jit(solution)/shard_map/ppermute | solution.py:274
  273.2 9.9 %all_to_all.105.parts = f32[8,40,128]{2,1,0:T(8,128)S(1)} all-to-all(f32[8,40,128]{2,1,0:T(8,128)S(1)} %product.15), channel_id=1, replica_groups=mesh['rows'=32,'cols'=8] {'cols'}, dimensions={0} | all-to-all | bytes 327680 | tf_op jit(solution)/shard_map/all_to_all | solution.py:271
  283.2 19.4 %all_to_all.106 = f32[256,1,128]{2,1,0:T(1,128)S(1)} all-to-all(f32[256,1,128]{2,1,0:T(1,128)S(1)} %broadcast_in_dim.11), channel_id=1, replica_groups=mesh['rows'=32,'cols'=8] {'rows','cols'}, dimensions={0} | all-to-all | bytes 262144 | tf_op jit(solution)/shard_map/all_to_all | solution.py:317
  (40 shorter events, 34.7 us)
Async XLA Ops:
  1.4 14.4 %all-to-all-start = ((f32[8,32,128]{2,1,0:T(8,128)}), f32[8,32,128]{2,1,0:T(8,128)S(1)}, u32[]{:S(2)}, u32[]{:S(2)}) async-start(f32[8,32,128]{2,1,0:T(8,128)} %broadcast_in_dim.8), calls=%async_computation | async-start | bytes 262144 | tf_op jit(solution)/shard_map/all_to_all | solution.py:271
  15.8 1.6 copy-start
  21.9 3.3 %collective-permute-start = (f32[16,32,128]{2,1,0:T(8,128)S(1)}, f32[16,32,128]{2,1,0:T(8,128)S(1)}, u32[]{:S(2)}, u32[]{:S(2)}) collective-permute-start(f32[16,32,128]{2,1,0:T(8,128)S(1)} %get-tuple-element.44), channel_id=1, source_target_pairs={{0,8},{8,0},{16,24},{24,16},{32,40},{40,32},{48,56},{56,48},{64,72... | collective-permute-start | bytes 786440 | tf_op jit(solution)/shard_map/ppermute | solution.py:290
  25.4 38.5 %copy-start.1 = (f32[256,16]{0,1:T(8,128)S(1)}, f32[256,16]{0,1:T(8,128)}, u32[]{:S(2)}) copy-start(f32[256,16]{0,1:T(8,128)} %param.5) | copy-start | bytes 49156
  25.4 38.5 %copy-start.2 = (f32[256]{0:T(256)S(1)}, f32[256]{0:T(256)}, u32[]{:S(2)}) copy-start(f32[256]{0:T(256)} %param.6) | copy-start | bytes 3076
  49.7 2.9 collective-permute-start.1
  77.1 4.9 %collective-permute-start.2 = (f32[16,40,128]{2,1,0:T(8,128)S(1)}, f32[16,40,128]{2,1,0:T(8,128)S(1)}, u32[]{:S(2)}, u32[]{:S(2)}) collective-permute-start(f32[16,40,128]{2,1,0:T(8,128)S(1)} %all_to_all.92.own), channel_id=1, source_target_pairs={{0,8},{8,0},{16,24},{24,16},{32,40},{40,32},{48,56},{56,48},{64,72... | collective-permute-start | bytes 983048 | tf_op jit(solution)/shard_map/ppermute | solution.py:274
  109.6 4.9 %collective-permute-start.3 = (f32[16,40,128]{2,1,0:T(8,128)S(1)}, f32[16,40,128]{2,1,0:T(8,128)S(1)}, u32[]{:S(2)}, u32[]{:S(2)}) collective-permute-start(f32[16,40,128]{2,1,0:T(8,128)S(1)} %all_to_all.94.own), channel_id=1, source_target_pairs={{0,8},{8,0},{16,24},{24,16},{32,40},{40,32},{48,56},{56,48},{64,72... | collective-permute-start | bytes 983048 | tf_op jit(solution)/shard_map/ppermute | solution.py:274
  141.3 4.9 %collective-permute-start.4 = (f32[16,40,128]{2,1,0:T(8,128)S(1)}, f32[16,40,128]{2,1,0:T(8,128)S(1)}, u32[]{:S(2)}, u32[]{:S(2)}) collective-permute-start(f32[16,40,128]{2,1,0:T(8,128)S(1)} %all_to_all.96.own), channel_id=1, source_target_pairs={{0,8},{8,0},{16,24},{24,16},{32,40},{40,32},{48,56},{56,48},{64,72... | collective-permute-start | bytes 983048 | tf_op jit(solution)/shard_map/ppermute | solution.py:274
  172.2 4.9 %collective-permute-start.5 = (f32[16,40,128]{2,1,0:T(8,128)S(1)}, f32[16,40,128]{2,1,0:T(8,128)S(1)}, u32[]{:S(2)}, u32[]{:S(2)}) collective-permute-start(f32[16,40,128]{2,1,0:T(8,128)S(1)} %all_to_all.98.own), channel_id=1, source_target_pairs={{0,8},{8,0},{16,24},{24,16},{32,40},{40,32},{48,56},{56,48},{64,72... | collective-permute-start | bytes 983048 | tf_op jit(solution)/shard_map/ppermute | solution.py:274
  203.8 4.9 %collective-permute-start.6 = (f32[16,40,128]{2,1,0:T(8,128)S(1)}, f32[16,40,128]{2,1,0:T(8,128)S(1)}, u32[]{:S(2)}, u32[]{:S(2)}) collective-permute-start(f32[16,40,128]{2,1,0:T(8,128)S(1)} %all_to_all.100.own), channel_id=1, source_target_pairs={{0,8},{8,0},{16,24},{24,16},{32,40},{40,32},{48,56},{56,48},{64,72... | collective-permute-start | bytes 983048 | tf_op jit(solution)/shard_map/ppermute | solution.py:274
  234.6 4.9 %collective-permute-start.7 = (f32[16,40,128]{2,1,0:T(8,128)S(1)}, f32[16,40,128]{2,1,0:T(8,128)S(1)}, u32[]{:S(2)}, u32[]{:S(2)}) collective-permute-start(f32[16,40,128]{2,1,0:T(8,128)S(1)} %all_to_all.102.own), channel_id=1, source_target_pairs={{0,8},{8,0},{16,24},{24,16},{32,40},{40,32},{48,56},{56,48},{64,72... | collective-permute-start | bytes 983048 | tf_op jit(solution)/shard_map/ppermute | solution.py:274
  266.7 4.9 %collective-permute-start.8 = (f32[16,40,128]{2,1,0:T(8,128)S(1)}, f32[16,40,128]{2,1,0:T(8,128)S(1)}, u32[]{:S(2)}, u32[]{:S(2)}) collective-permute-start(f32[16,40,128]{2,1,0:T(8,128)S(1)} %all_to_all.104.own), channel_id=1, source_target_pairs={{0,8},{8,0},{16,24},{24,16},{32,40},{40,32},{48,56},{56,48},{64,72... | collective-permute-start | bytes 983048 | tf_op jit(solution)/shard_map/ppermute | solution.py:274

commit v3 on v1

v3 whole, which is shorter than its diff:
```python
import jax
import jax.numpy as jnp
from jax import lax
from jax.experimental import pallas as pl
from jax.experimental.pallas import tpu as pltpu
from jax.sharding import PartitionSpec as P

ITERS = 4
S = 16
BS = 128
F32 = jnp.float32
HI = lax.Precision.HIGHEST
VMEM = pl.BlockSpec(memory_space=pltpu.VMEM)
SMEM = pl.BlockSpec(memory_space=pltpu.SMEM)
HBM = pl.BlockSpec(memory_space=pltpu.HBM)
TILE = 8


def sds(*shape, dtype=F32):
    return pltpu.VMEM(shape, dtype)


def call(body, outs, specs, *args, name, scratch=()):
    args = [
        a if spec is SMEM else pltpu.with_memory_space_constraint(a, spec.memory_space)
        for a, spec in zip(args, specs)
    ]
    return pl.pallas_call(
        body,
        out_shape=outs,
        in_specs=specs,
        out_specs=tuple(VMEM for _ in outs) if isinstance(outs, tuple) else VMEM,
        scratch_shapes=scratch,
        name=name,
        compiler_params=pltpu.CompilerParams(vmem_limit_bytes=8 << 20),
    )(*args)


def dot(a, b, contract=((1,), (0,))):
    return lax.dot_general(a, b, (contract, ((), ())), precision=HI, preferred_element_type=F32)


def bdot(a, b):
    return lax.dot_general(a, b, (((1,), (0,)), ((), ())), preferred_element_type=F32)


def halves(x):
    high = x.astype(jnp.bfloat16)
    return high, (x - high.astype(F32)).astype(jnp.bfloat16)


def wide(ref, at=()):
    return jnp.concatenate([ref[(*at, slice(0, S))], ref[(*at, slice(S, 2 * S))]], axis=1)


def spread(ref, value, tile):
    for k in range(ref.shape[0]):
        ref[k, 0:S] = value[:, :BS]
        ref[k, S : 2 * S] = value[:, BS:]
        ref[k, 2 * S : 2 * S + TILE] = tile


def narrow(x):
    return jnp.concatenate([x[:, :BS], x[:, BS:]], axis=0)


def solve(matrix, right):
    joined = jnp.concatenate([matrix, right], axis=1)
    row = lax.broadcasted_iota(jnp.int32, joined.shape, 0)
    for i in range(S):
        column = jnp.broadcast_to(joined[:, i : i + 1], joined.shape)
        pivot = joined[i : i + 1, :] / column[i : i + 1, :]
        joined = jnp.where(row == i, pivot, joined - column * pivot)
    return joined[:, S:]


def mix(vectors, small):
    return dot(small.T, vectors)


def grams(left, right):
    return dot(left, right, ((1,), (1,)))


def pack(products, extra=None):
    if extra is not None:
        row = lax.broadcasted_iota(jnp.int32, products.shape, 0)
        col = lax.broadcasted_iota(jnp.int32, products.shape, 1)
        for k, value in enumerate(extra):
            products = jnp.where((row == 0) & (col == S + k), value, products)
    return jnp.concatenate([products[8 * g : 8 * g + 8] for g in range(4)], axis=1)


def unpack(tile):
    whole = jnp.concatenate([tile[:, 32 * g : 32 * g + 32] for g in range(4)], axis=0)
    return whole[:S, :S], whole[:S, S:], whole[S:, :S], whole[S:, S:]


def total(ref, first=0, last=None):
    value = ref[0, first:last]
    for k in range(1, ref.shape[0]):
        value = value + ref[k, first:last]
    image = jnp.concatenate([value[0:S], value[S : 2 * S]], axis=1)
    return image, value[2 * S :]


def entire(x):
    return jnp.sum(jnp.sum(x, axis=1, keepdims=True), axis=0, keepdims=True)


def fetch(blocks, held, done):
    copies = [pltpu.make_async_copy(blocks.at[i], held.at[i], done.at[i]) for i in range(16)]
    for copy in copies:
        copy.start()
    return copies


def prepare_body(source, counts, packed, blocks, done):
    copies = fetch(source, blocks, done)
    for i in range(16):
        copies[i].wait()
        for k in range(2):
            keep = (k < counts[0, i]).astype(F32)
            high, low = halves((blocks[i, k] * keep).T)
            packed[i, k * BS : (k + 1) * BS, 0:BS] = high
            packed[i, k * BS : (k + 1) * BS, BS : 2 * BS] = low


def transposed_body(source, arrived, cols, counts, core, mine, other, acc, blocks, done):
    copies = fetch(source, blocks, done)
    acc[...] = jnp.zeros_like(acc)
    for i in range(16):
        copies[i].wait()
        b = 2 * S + i % 2 * S
        piece = arrived[i // 2, b : b + S]
        for k in range(2):
            keep = (k < counts[0, i]).astype(F32)
            acc[cols[k, i]] += dot(piece * keep, blocks[i, k])
    me = core[0]
    for m in range(16):
        for b in range(2):
            mine[m, b * S : (b + 1) * S] = acc[m * 4 + me * 2 + b]
            other[m, b * S : (b + 1) * S] = acc[m * 4 + (1 - me) * 2 + b]


def product_body(own, peer, packed, cols, core, *rest):
    piece, out = rest if len(rest) == 2 else (None, *rest)
    me = core[0]
    if piece is None:
        extra = own[0, 2 * S : 2 * S + TILE]
        extra2 = peer[0, 2 * S : 2 * S + TILE]
        for m in range(1, 16):
            extra = extra + own[m, 2 * S : 2 * S + TILE]
            extra2 = extra2 + peer[m, 2 * S : 2 * S + TILE]
        extra = extra + extra2
    else:
        extra = piece[...]
    for i in range(16):
        picked = []
        for k in range(2):
            col = cols[k, i]
            m = col // 4
            b = pl.multiple_of((col % 2) * S, S)
            here = own[m, pl.ds(b, S), :]
            there = peer[m, pl.ds(b, S), :]
            picked.append(jnp.where((col // 2) % 2 == me, here, there))
        high, low = halves(jnp.concatenate(picked, axis=1))
        result = bdot(jnp.concatenate([high, low], axis=0), packed[i])
        result = (result[:S, :BS] + result[:S, BS:]) + (result[S:, :BS] + result[S:, BS:])
        out[i // 2, (i % 2) * S : (i % 2 + 1) * S] = result
    for c in range(8):
        out[c, 2 * S :] = extra


def first_body(parts, mine, theirs, shadow, diag, image, message):
    value, _ = total(parts, 0, 2 * S)
    s = shadow[...]
    v = value + diag[...] * s
    image[...] = v
    products = grams(jnp.concatenate([s, s], axis=0), jnp.concatenate([v, s], axis=0))
    spread(message, v, pack(products))
    for m in range(16):
        message[m, 2 * S + TILE :] = mine[m] + theirs[m]


def lead_body(
    parts, arrived, shadow, diag, image,
    z_out, t_out, q_out, x_out, weights, matrix_out, right_out, message,
):
    value, tile = total(parts)
    s = shadow[...]
    v = image[...]
    z = value + diag[...] * v
    _, _, matrix, right = unpack(tile)
    alpha = solve(matrix, right)
    t = v - mix(z, alpha)
    q = s - mix(v, alpha)
    w = total(arrived, 2 * S + TILE)[0] + diag[...] * s
    z_out[...] = z
    t_out[...] = t
    q_out[...] = q
    x_out[...] = mix(s, alpha)
    weights[...] = w
    matrix_out[...] = matrix
    right_out[...] = right - dot(matrix, alpha)
    products = grams(jnp.concatenate([s, w], axis=0), jnp.concatenate([t, v], axis=0))
    spread(message, t, pack(products, (entire(t * t), entire(t * q))))


def middle_step(
    y, u, base, t, q, x, w, s, w_u, s_u, s_q, cross, tt, tq, q_out, x_out, v_out, p_out, matrix_out, message
):
    omega = tq / tt
    matrix = s_u - omega * w_u
    right = s_q - omega * cross
    alpha = solve(matrix, right)
    v = u - omega * y
    p = base - omega * u
    middle = (q - omega * t) - mix(v, alpha)
    x_out[...] = x + omega * q + mix(p, alpha)
    q_out[...] = middle
    v_out[...] = v
    p_out[...] = p
    matrix_out[...] = matrix
    products = grams(jnp.concatenate([w, s], axis=0), jnp.concatenate([middle, middle], axis=0))
    spread(message, middle, pack(products))


def second_body(
    parts, shadow, diag, image, weights, z, t, q, x, matrix, right, *outs
):
    value, tile = total(parts)
    f = value + diag[...] * t[...]
    cross, sums, w_t, w_v = unpack(tile)
    beta = -solve(matrix[...], cross)
    u = t[...] + mix(image[...], beta)
    y = f + mix(z[...], beta)
    base = q[...] + mix(shadow[...], beta)
    middle_step(
        y, u, base, t[...], q[...], x[...], weights[...], shadow[...],
        w_t + dot(w_v, beta), cross + dot(matrix[...], beta), right[...], cross,
        sums[0:1, 0:1], sums[0:1, 1:2], *outs,
    )


def even_body(parts, shadow, diag, weights, q, x, u, base, t, cross, *outs):
    value, tile = total(parts)
    y = value + diag[...] * u[...]
    w_u, sums, s_u, s_q = unpack(tile)
    middle_step(
        y, u[...], base[...], t[...], q[...], x[...], weights[...], shadow[...],
        w_u, s_u, s_q, cross[...], sums[0:1, 0:1], sums[0:1, 1:2], *outs,
    )


def odd_body(
    parts, shadow, diag, weights, q, v, p, matrix, u_out, base_out, t_out, cross_out, message
):
    value, tile = total(parts)
    t = value + diag[...] * q[...]
    cross = unpack(tile)[0]
    beta = -solve(matrix[...], cross)
    u = t + mix(v[...], beta)
    u_out[...] = u
    base_out[...] = q[...] + mix(p[...], beta)
    t_out[...] = t
    cross_out[...] = cross
    products = grams(
        jnp.concatenate([weights[...], shadow[...]], axis=0), jnp.concatenate([u, q[...]], axis=0)
    )
    spread(message, u, pack(products, (entire(t * t), entire(t * q[...]))))


def last_body(parts, diag, q, sums):
    value, _ = total(parts)
    t = value + diag[...] * q[...]
    lane = lax.broadcasted_iota(jnp.int32, (1, BS), 1)
    sums[...] = jnp.where(lane == 0, entire(t * t), jnp.where(lane == 1, entire(t * q[...]), 0.0))


def end_body(sums, x, q, out):
    value = jnp.sum(sums[...], axis=0, keepdims=True)
    omega = value[0:1, 1:2] / value[0:1, 0:1]
    out[...] = x[...] + omega * q[...]


def per_device(rhs, diagonal, blocks, block_cols, counts):
    core = lax.axis_index("core").astype(jnp.int32).reshape(1)
    block_cols = block_cols.T
    counts = counts.T
    shadow = rhs.T
    diag = diagonal.reshape(1, 2 * BS)
    vec = sds(S, 2 * BS)
    small = sds(S, S)
    message = sds(16, 2 * S + TILE, BS)

    def among(x):
        return lax.all_to_all(x, ("x", "z"), 0, 0, tiled=True)

    def across(x):
        return lax.all_to_all(x, "cols", 0, 0, tiled=True)

    def product(own, *piece):
        peer = lax.ppermute(own, "core", [(0, 1), (1, 0)])
        out = call(
            product_body, sds(8, 2 * S + (2 * S if piece else TILE), BS),
            [VMEM, VMEM, VMEM, SMEM, SMEM] + [VMEM] * len(piece),
            own, peer, packed, block_cols, core, *piece, name="product",
        )
        return across(out)

    held = [pltpu.VMEM((16, 2, BS, BS), F32), pltpu.SemaphoreType.DMA((16,))]
    piece = jnp.concatenate([shadow[:, :BS], shadow[:, BS:]], axis=0)
    packed = call(
        prepare_body, sds(16, 2 * BS, 2 * BS, dtype=jnp.bfloat16), [HBM, SMEM],
        blocks, counts, name="prepare", scratch=held,
    )
    parts = product(among(jnp.broadcast_to(piece[None], (16, 2 * S, BS))), piece)
    mine, other = call(
        transposed_body, (sds(16, 2 * S, BS), sds(16, 2 * S, BS)), [HBM, VMEM, SMEM, SMEM, SMEM],
        blocks, parts, block_cols, counts, core,
        name="transposed", scratch=[pltpu.VMEM((64, S, BS), F32), *held],
    )
    theirs = lax.ppermute(other, "core", [(0, 1), (1, 0)])
    v, msg = call(
        first_body, (vec, sds(16, 4 * S + TILE, BS)), [VMEM] * 5,
        parts, mine, theirs, shadow, diag, name="first",
    )
    arrived = among(msg)
    z, t, q, x, w, matrix, right, msg = call(
        lead_body, (vec, vec, vec, vec, vec, small, small, message), [VMEM] * 5,
        product(arrived), arrived, shadow, diag, v, name="lead",
    )
    for iteration in range(1, ITERS):
        parts = product(among(msg))
        outs = (vec, vec, vec, vec, small, message)
        if iteration == 1:
            q, x, v, p, matrix, msg = call(
                second_body, outs, [VMEM] * 11,
                parts, shadow, diag, v, w, z, t, q, x, matrix, right, name="second",
            )
        else:
            q, x, v, p, matrix, msg = call(
                even_body, outs, [VMEM] * 10,
                parts, shadow, diag, w, q, x, u, base, t, cross, name="even",
            )
        parts = product(among(msg))
        if iteration < ITERS - 1:
            u, base, t, cross, msg = call(
                odd_body, (vec, vec, vec, small, message), [VMEM] * 8,
                parts, shadow, diag, w, q, v, p, matrix, name="odd",
            )
    sums = call(last_body, sds(1, BS), [VMEM] * 3, parts, diag, q, name="last")
    everyone = 2 * 16 * 8
    sums = jnp.broadcast_to(sums[None], (everyone, 1, BS))
    sums = lax.all_to_all(sums, ("x", "z", "core", "cols"), 0, 0, tiled=True)
    out = call(end_body, vec, [VMEM] * 3, sums.reshape(everyone, BS), x, q, name="end")
    return out.T


def solution(mesh):
    parts = ("x", "z", "core")
    mesh = jax.sharding.Mesh(mesh.devices.reshape(2, 8, 2, 8), (*parts, "cols"))
    in_specs = (
        P((*parts, "cols"), None),
        P((*parts, "cols")),
        P(parts, "cols", None, None),
        P(parts, "cols"),
        P(parts, "cols"),
    )
    out_specs = P((*parts, "cols"), None)
    return jax.shard_map(
        per_device, mesh=mesh, in_specs=in_specs, out_specs=out_specs, check_vma=False
    )
```

time: 350 us -> 292 us (0.83)
  Pallas kernels: 59.9 us -> 31.4 us
  local copies, waits for them, and re-layouts: 11.4 us -> 2.09 us
  blocking collectives: 224 us -> 216 us
  waiting for transfers between devices: 15.6 us -> 10.3 us
  starting transfers between devices: 35.6 us -> 31 us
    pallas_call x18 -> x19, Pallas kernels: 59.9 us -> 31.4 us  [call(): pl.pallas_call(body, out_shape=outs, in_specs=specs, out_specs=tuple((VME...]
    unnamed x38 -> x11, local copies, waits for them, and re-layouts: 9.28 us -> 1.29 us
    all_to_all x1 -> x0, starting transfers between devices: 7.47 us -> none  [across(): return lax.all_to_all(x, 'cols', 0, 0, tiled=True)]
    all_to_all x8, blocking collectives: 89.3 us -> 83.6 us  [across(): return lax.all_to_all(x, 'cols', 0, 0, tiled=True)]
    all_to_all x1 -> x0, waiting for transfers between devices: 4.26 us -> none  [across(): return lax.all_to_all(x, 'cols', 0, 0, tiled=True)]
  transfers between devices with their start and end apart: 10 -> 9, of which waited for: 10 -> 8; matrix products, arithmetic and copies ran while one was open for 1% -> 0% of each run, Pallas kernels for 0% -> 1%
where the time goes in v3:
time: 292 us; the launch traced here: 291 us
  blocking collectives  216 us (74%)
  Pallas kernels  31.4 us (11%)
  starting transfers between devices  31 us (11%)
  waiting for transfers between devices  10.3 us (4%)
    all_to_all x8, blocking collectives, among(): return lax.all_to_all(x, ('x', 'z'), 0, 0, tiled=True)  112 us
    all_to_all x8, blocking collectives, across(): return lax.all_to_all(x, 'cols', 0, 0, tiled=True)  83.6 us
    pallas_call x19, Pallas kernels, call(): pl.pallas_call(body, out_shape=outs, in_specs=specs, out_specs=tuple((VME...  31.4 us
    ppermute x8, starting transfers between devices, product(): peer = lax.ppermute(own, 'core', [(0, 1), (1, 0)])  29.2 us
    all_to_all x1, blocking collectives, per_device(): sums = lax.all_to_all(sums, ('x', 'z', 'core', 'cols'), 0, 0, tiled=True)  20.3 us
    ppermute x8, waiting for transfers between devices, product(): peer = lax.ppermute(own, 'core', [(0, 1), (1, 0)])  9.17 us
  transfers between devices with their start and end apart: 9, of which 8 were waited for; matrix products, arithmetic and copies ran while one was open for 0% of the time, Pallas kernels for 1%

profile of v3, /device:TPU:1, one launch (start us, length us, event | category | flops | bytes accessed | tf_op | source)
XLA Modules:
  0.0 290.9 jit_solution(13600687219741095574)
XLA Ops:
  0.8 18.6 %all_to_all.85.own = f32[16,32,128]{2,1,0:T(8,128)S(1)} all-to-all(f32[16,32,128]{2,1,0:T(8,128)S(1)} %broadcast_in_dim.6), channel_id=1, replica_groups=mesh['x'=2,'z'=8,'core'=2,'cols'=8] {'x','z'}, dimensions={0} | all-to-all | bytes 524288 | tf_op jit(solution)/shard_map/all_to_all | solution.py:298
  19.4 2.3 collective-permute-start
  22.3 3.4 %prepare.1.packed = bf16[16,256,256]{2,1,0:T(8,128)(2,1)S(1)} custom-call(f32[16,2,128,128]{3,2,1,0:T(8,128)} %source.3, s32[1,16]{1,0:T(1,128)S(1)} %bitcast.36), custom_call_target="tpu_custom_call" | custom-call | tf_op jit(solution)/shard_map/prepare/pallas_call | solution.py:28
  26.9 14.0 %all_to_all.86.arrived.parts = f32[8,64,128]{2,1,0:T(8,128)S(1)} all-to-all(f32[8,64,128]{2,1,0:T(8,128)S(1)} %product.8), channel_id=1, replica_groups=mesh['x'=2,'z'=8,'core'=2,'cols'=8] {'cols'}, dimensions={0} | all-to-all | bytes 524288 | tf_op jit(solution)/shard_map/all_to_all | solution.py:301
  40.9 5.2 %transposed.1 = (f32[16,32,128]{2,1,0:T(8,128)S(1)}, f32[16,32,128]{2,1,0:T(8,128)S(1)}) custom-call(f32[16,2,128,128]{3,2,1,0:T(8,128)} %source.3, f32[8,64,128]{2,1,0:T(8,128)S(1)} %all_to_all.86.arrived.parts, s32[2,16]{1,0:T(2,128)S(1)} %bitcast.19, s32[1,16]{1,0:T(1,128)S(1)} %bitcast.37, s32[1]{0:T(128)} %bitcast.3.core), custom_call_target="tpu_custom_call" | custom-call | tf_op jit(solution)/shard_map/transposed/pallas_call | solution.py:28
  49.3 21.2 %all_to_all.87.own.arrived = f32[16,72,128]{2,1,0:T(8,128)S(1)} all-to-all(f32[16,72,128]{2,1,0:T(8,128)S(1)} %get-tuple-element.44), channel_id=1, replica_groups=mesh['x'=2,'z'=8,'core'=2,'cols'=8] {'x','z'}, dimensions={0} | all-to-all | bytes 1179648 | tf_op jit(solution)/shard_map/all_to_all | solution.py:298
  70.5 2.7 collective-permute-start.2
  75.9 9.8 %all_to_all.88.parts = f32[8,40,128]{2,1,0:T(8,128)S(1)} all-to-all(f32[8,40,128]{2,1,0:T(8,128)S(1)} %product.9), channel_id=1, replica_groups=mesh['x'=2,'z'=8,'core'=2,'cols'=8] {'cols'}, dimensions={0} | all-to-all | bytes 327680 | tf_op jit(solution)/shard_map/all_to_all | solution.py:301
  87.5 11.4 %all_to_all.89.own = f32[16,40,128]{2,1,0:T(8,128)S(1)} all-to-all(f32[16,40,128]{2,1,0:T(8,128)S(1)} %get-tuple-element.46), channel_id=1, replica_groups=mesh['x'=2,'z'=8,'core'=2,'cols'=8] {'x','z'}, dimensions={0} | all-to-all | bytes 655360 | tf_op jit(solution)/shard_map/all_to_all | solution.py:298
  99.0 3.3 %collective-permute-start.3 = (f32[16,40,128]{2,1,0:T(8,128)S(1)}, f32[16,40,128]{2,1,0:T(8,128)S(1)}, u32[]{:S(2)}, u32[]{:S(2)}) collective-permute-start(f32[16,40,128]{2,1,0:T(8,128)S(1)} %all_to_all.89.own), channel_id=1, source_target_pairs={{0,8},{8,0},{1,9},{9,1},{2,10},{10,2},{3,11},{11,3},{4,12},{12,4},... | collective-permute-start | bytes 983048 | tf_op jit(solution)/shard_map/ppermute | solution.py:304
  104.6 10.1 %all_to_all.90.parts = f32[8,40,128]{2,1,0:T(8,128)S(1)} all-to-all(f32[8,40,128]{2,1,0:T(8,128)S(1)} %product.10), channel_id=1, replica_groups=mesh['x'=2,'z'=8,'core'=2,'cols'=8] {'cols'}, dimensions={0} | all-to-all | bytes 327680 | tf_op jit(solution)/shard_map/all_to_all | solution.py:301
  114.8 3.5 %second.1 = (f32[16,256]{1,0:T(8,128)S(1)}, f32[16,256]{1,0:T(8,128)S(1)}, f32[16,256]{1,0:T(8,128)S(1)}, f32[16,256]{1,0:T(8,128)S(1)}, f32[16,16]{1,0:T(8,128)S(1)}, /*index=5*/f32[16,40,128]{2,1,0:T(8,128)S(1)}) custom-call(f32[8,40,128]{2,1,0:T(8,128)S(1)} %all_to_all.90.parts, f32[16,256]{1,0:T(8,128)S(1)} %bitcast.12, f32[1,256]{1,0:T(1,128)S(1)} %bitcast.29, ...), custom_call_target="tpu_custom_call" | custom-call | tf_op jit(solution)/shard_map/second/pallas_call | solution.py:28
  118.3 12.0 %all_to_all.91.own = f32[16,40,128]{2,1,0:T(8,128)S(1)} all-to-all(f32[16,40,128]{2,1,0:T(8,128)S(1)} %get-tuple-element.54), channel_id=1, replica_groups=mesh['x'=2,'z'=8,'core'=2,'cols'=8] {'x','z'}, dimensions={0} | all-to-all | bytes 655360 | tf_op jit(solution)/shard_map/all_to_all | solution.py:298
  130.3 4.2 %collective-permute-start.4 = (f32[16,40,128]{2,1,0:T(8,128)S(1)}, f32[16,40,128]{2,1,0:T(8,128)S(1)}, u32[]{:S(2)}, u32[]{:S(2)}) collective-permute-start(f32[16,40,128]{2,1,0:T(8,128)S(1)} %all_to_all.91.own), channel_id=1, source_target_pairs={{0,8},{8,0},{1,9},{9,1},{2,10},{10,2},{3,11},{11,3},{4,12},{12,4},... | collective-permute-start | bytes 983048 | tf_op jit(solution)/shard_map/ppermute | solution.py:304
  136.8 10.0 %all_to_all.92.parts = f32[8,40,128]{2,1,0:T(8,128)S(1)} all-to-all(f32[8,40,128]{2,1,0:T(8,128)S(1)} %product.11), channel_id=1, replica_groups=mesh['x'=2,'z'=8,'core'=2,'cols'=8] {'cols'}, dimensions={0} | all-to-all | bytes 327680 | tf_op jit(solution)/shard_map/all_to_all | solution.py:301
  146.8 1.9 odd.2
  148.7 12.2 %all_to_all.93.own = f32[16,40,128]{2,1,0:T(8,128)S(1)} all-to-all(f32[16,40,128]{2,1,0:T(8,128)S(1)} %get-tuple-element.59), channel_id=1, replica_groups=mesh['x'=2,'z'=8,'core'=2,'cols'=8] {'x','z'}, dimensions={0} | all-to-all | bytes 655360 | tf_op jit(solution)/shard_map/all_to_all | solution.py:298
  160.8 4.2 %collective-permute-start.5 = (f32[16,40,128]{2,1,0:T(8,128)S(1)}, f32[16,40,128]{2,1,0:T(8,128)S(1)}, u32[]{:S(2)}, u32[]{:S(2)}) collective-permute-start(f32[16,40,128]{2,1,0:T(8,128)S(1)} %all_to_all.93.own), channel_id=1, source_target_pairs={{0,8},{8,0},{1,9},{9,1},{2,10},{10,2},{3,11},{11,3},{4,12},{12,4},... | collective-permute-start | bytes 983048 | tf_op jit(solution)/shard_map/ppermute | solution.py:304
  167.3 9.8 %all_to_all.94.parts = f32[8,40,128]{2,1,0:T(8,128)S(1)} all-to-all(f32[8,40,128]{2,1,0:T(8,128)S(1)} %product.12), channel_id=1, replica_groups=mesh['x'=2,'z'=8,'core'=2,'cols'=8] {'cols'}, dimensions={0} | all-to-all | bytes 327680 | tf_op jit(solution)/shard_map/all_to_all | solution.py:301
  177.2 2.1 even.2
  179.2 12.2 %all_to_all.95.own = f32[16,40,128]{2,1,0:T(8,128)S(1)} all-to-all(f32[16,40,128]{2,1,0:T(8,128)S(1)} %get-tuple-element.65), channel_id=1, replica_groups=mesh['x'=2,'z'=8,'core'=2,'cols'=8] {'x','z'}, dimensions={0} | all-to-all | bytes 655360 | tf_op jit(solution)/shard_map/all_to_all | solution.py:298
  191.4 4.2 %collective-permute-start.6 = (f32[16,40,128]{2,1,0:T(8,128)S(1)}, f32[16,40,128]{2,1,0:T(8,128)S(1)}, u32[]{:S(2)}, u32[]{:S(2)}) collective-permute-start(f32[16,40,128]{2,1,0:T(8,128)S(1)} %all_to_all.95.own), channel_id=1, source_target_pairs={{0,8},{8,0},{1,9},{9,1},{2,10},{10,2},{3,11},{11,3},{4,12},{12,4},... | collective-permute-start | bytes 983048 | tf_op jit(solution)/shard_map/ppermute | solution.py:304
  197.9 10.0 %all_to_all.96.parts = f32[8,40,128]{2,1,0:T(8,128)S(1)} all-to-all(f32[8,40,128]{2,1,0:T(8,128)S(1)} %product.13), channel_id=1, replica_groups=mesh['x'=2,'z'=8,'core'=2,'cols'=8] {'cols'}, dimensions={0} | all-to-all | bytes 327680 | tf_op jit(solution)/shard_map/all_to_all | solution.py:301
  207.9 1.9 odd.3
  209.8 12.2 %all_to_all.97.own = f32[16,40,128]{2,1,0:T(8,128)S(1)} all-to-all(f32[16,40,128]{2,1,0:T(8,128)S(1)} %get-tuple-element.70), channel_id=1, replica_groups=mesh['x'=2,'z'=8,'core'=2,'cols'=8] {'x','z'}, dimensions={0} | all-to-all | bytes 655360 | tf_op jit(solution)/shard_map/all_to_all | solution.py:298
  222.0 4.2 %collective-permute-start.7 = (f32[16,40,128]{2,1,0:T(8,128)S(1)}, f32[16,40,128]{2,1,0:T(8,128)S(1)}, u32[]{:S(2)}, u32[]{:S(2)}) collective-permute-start(f32[16,40,128]{2,1,0:T(8,128)S(1)} %all_to_all.97.own), channel_id=1, source_target_pairs={{0,8},{8,0},{1,9},{9,1},{2,10},{10,2},{3,11},{11,3},{4,12},{12,4},... | collective-permute-start | bytes 983048 | tf_op jit(solution)/shard_map/ppermute | solution.py:304
  228.5 9.8 %all_to_all.98.parts = f32[8,40,128]{2,1,0:T(8,128)S(1)} all-to-all(f32[8,40,128]{2,1,0:T(8,128)S(1)} %product.14), channel_id=1, replica_groups=mesh['x'=2,'z'=8,'core'=2,'cols'=8] {'cols'}, dimensions={0} | all-to-all | bytes 327680 | tf_op jit(solution)/shard_map/all_to_all | solution.py:301
  238.3 2.6 even.3
  240.9 12.2 %all_to_all.99.own = f32[16,40,128]{2,1,0:T(8,128)S(1)} all-to-all(f32[16,40,128]{2,1,0:T(8,128)S(1)} %get-tuple-element.76), channel_id=1, replica_groups=mesh['x'=2,'z'=8,'core'=2,'cols'=8] {'x','z'}, dimensions={0} | all-to-all | bytes 655360 | tf_op jit(solution)/shard_map/all_to_all | solution.py:298
  253.1 4.2 %collective-permute-start.8 = (f32[16,40,128]{2,1,0:T(8,128)S(1)}, f32[16,40,128]{2,1,0:T(8,128)S(1)}, u32[]{:S(2)}, u32[]{:S(2)}) collective-permute-start(f32[16,40,128]{2,1,0:T(8,128)S(1)} %all_to_all.99.own), channel_id=1, source_target_pairs={{0,8},{8,0},{1,9},{9,1},{2,10},{10,2},{3,11},{11,3},{4,12},{12,4},... | collective-permute-start | bytes 983048 | tf_op jit(solution)/shard_map/ppermute | solution.py:304
  259.6 10.0 %all_to_all.100.parts = f32[8,40,128]{2,1,0:T(8,128)S(1)} all-to-all(f32[8,40,128]{2,1,0:T(8,128)S(1)} %product.15), channel_id=1, replica_groups=mesh['x'=2,'z'=8,'core'=2,'cols'=8] {'cols'}, dimensions={0} | all-to-all | bytes 327680 | tf_op jit(solution)/shard_map/all_to_all | solution.py:301
  269.8 20.3 %all_to_all.101 = f32[256,1,128]{2,1,0:T(1,128)S(1)} all-to-all(f32[256,1,128]{2,1,0:T(1,128)S(1)} %broadcast_in_dim.16), channel_id=1, replica_groups=mesh['x'=2,'z'=8,'core'=2,'cols'=8] {'x','z','core','cols'}, dimensions={0} | all-to-all | bytes 262144 | tf_op jit(solution)/shard_map/all_to_all | solution.py:356
  (37 shorter events, 25.2 us)
Async XLA Ops:
  19.4 6.4 %collective-permute-start = (f32[16,32,128]{2,1,0:T(8,128)S(1)}, f32[16,32,128]{2,1,0:T(8,128)S(1)}, u32[]{:S(2)}, u32[]{:S(2)}) collective-permute-start(f32[16,32,128]{2,1,0:T(8,128)S(1)} %all_to_all.85.own), channel_id=1, source_target_pairs={{0,8},{8,0},{1,9},{9,1},{2,10},{10,2},{3,11},{11,3},{4,12},{12,4},... | collective-permute-start | bytes 786440 | tf_op jit(solution)/shard_map/ppermute | solution.py:304
  21.7 0.7 copy-start.3
  22.3 3.4 %copy-start.1 = (s32[16,2]{0,1:T(2,128)S(1)}, s32[16,2]{0,1:T(2,128)}, u32[]{:S(2)}) copy-start(s32[16,2]{0,1:T(2,128)} %param.8) | copy-start | bytes 388
  25.7 15.1 %copy-start.4 = (s32[16,1]{0,1:T(1,128)S(1)}, s32[16,1]{0,1:T(1,128)}, u32[]{:S(2)}) copy-start(s32[16,1]{0,1:T(1,128)} %param.9) | copy-start | bytes 196
  26.9 22.2 %copy-start = (f32[256,16]{0,1:T(8,128)S(1)}, f32[256,16]{0,1:T(8,128)}, u32[]{:S(2)}) copy-start(f32[256,16]{0,1:T(8,128)} %param.5) | copy-start | bytes 49156
  26.9 22.2 %copy-start.2 = (f32[256]{0:T(256)S(1)}, f32[256]{0:T(256)}, u32[]{:S(2)}) copy-start(f32[256]{0:T(256)} %param.6) | copy-start | bytes 3076
  46.1 3.0 %collective-permute-start.1 = (f32[16,32,128]{2,1,0:T(8,128)S(1)}, f32[16,32,128]{2,1,0:T(8,128)S(1)}, u32[]{:S(2)}, u32[]{:S(2)}) collective-permute-start(f32[16,32,128]{2,1,0:T(8,128)S(1)} %get-tuple-element.43), channel_id=1, source_target_pairs={{0,8},{8,0},{1,9},{9,1},{2,10},{10,2},{3,11},{11,3},{4,12},{12,4},... | collective-permute-start | bytes 786440 | tf_op jit(solution)/shard_map/ppermute | solution.py:324
  70.5 4.3 %collective-permute-start.2 = (f32[16,72,128]{2,1,0:T(8,128)S(1)}, f32[16,72,128]{2,1,0:T(8,128)S(1)}, u32[]{:S(2)}, u32[]{:S(2)}) collective-permute-start(f32[16,72,128]{2,1,0:T(8,128)S(1)} %all_to_all.87.own.arrived), channel_id=1, source_target_pairs={{0,8},{8,0},{1,9},{9,1},{2,10},{10,2},{3,11},{11,3},{4,12},{12,4},... | collective-permute-start | bytes 1769480 | tf_op jit(solution)/shard_map/ppermute | solution.py:304
  99.0 4.6 %collective-permute-start.3 = (f32[16,40,128]{2,1,0:T(8,128)S(1)}, f32[16,40,128]{2,1,0:T(8,128)S(1)}, u32[]{:S(2)}, u32[]{:S(2)}) collective-permute-start(f32[16,40,128]{2,1,0:T(8,128)S(1)} %all_to_all.89.own), channel_id=1, source_target_pairs={{0,8},{8,0},{1,9},{9,1},{2,10},{10,2},{3,11},{11,3},{4,12},{12,4},... | collective-permute-start | bytes 983048 | tf_op jit(solution)/shard_map/ppermute | solution.py:304
  130.3 5.4 %collective-permute-start.4 = (f32[16,40,128]{2,1,0:T(8,128)S(1)}, f32[16,40,128]{2,1,0:T(8,128)S(1)}, u32[]{:S(2)}, u32[]{:S(2)}) collective-permute-start(f32[16,40,128]{2,1,0:T(8,128)S(1)} %all_to_all.91.own), channel_id=1, source_target_pairs={{0,8},{8,0},{1,9},{9,1},{2,10},{10,2},{3,11},{11,3},{4,12},{12,4},... | collective-permute-start | bytes 983048 | tf_op jit(solution)/shard_map/ppermute | solution.py:304
  160.8 5.4 %collective-permute-start.5 = (f32[16,40,128]{2,1,0:T(8,128)S(1)}, f32[16,40,128]{2,1,0:T(8,128)S(1)}, u32[]{:S(2)}, u32[]{:S(2)}) collective-permute-start(f32[16,40,128]{2,1,0:T(8,128)S(1)} %all_to_all.93.own), channel_id=1, source_target_pairs={{0,8},{8,0},{1,9},{9,1},{2,10},{10,2},{3,11},{11,3},{4,12},{12,4},... | collective-permute-start | bytes 983048 | tf_op jit(solution)/shard_map/ppermute | solution.py:304
  191.4 5.4 %collective-permute-start.6 = (f32[16,40,128]{2,1,0:T(8,128)S(1)}, f32[16,40,128]{2,1,0:T(8,128)S(1)}, u32[]{:S(2)}, u32[]{:S(2)}) collective-permute-start(f32[16,40,128]{2,1,0:T(8,128)S(1)} %all_to_all.95.own), channel_id=1, source_target_pairs={{0,8},{8,0},{1,9},{9,1},{2,10},{10,2},{3,11},{11,3},{4,12},{12,4},... | collective-permute-start | bytes 983048 | tf_op jit(solution)/shard_map/ppermute | solution.py:304
  222.0 5.4 %collective-permute-start.7 = (f32[16,40,128]{2,1,0:T(8,128)S(1)}, f32[16,40,128]{2,1,0:T(8,128)S(1)}, u32[]{:S(2)}, u32[]{:S(2)}) collective-permute-start(f32[16,40,128]{2,1,0:T(8,128)S(1)} %all_to_all.97.own), channel_id=1, source_target_pairs={{0,8},{8,0},{1,9},{9,1},{2,10},{10,2},{3,11},{11,3},{4,12},{12,4},... | collective-permute-start | bytes 983048 | tf_op jit(solution)/shard_map/ppermute | solution.py:304
  253.1 5.4 %collective-permute-start.8 = (f32[16,40,128]{2,1,0:T(8,128)S(1)}, f32[16,40,128]{2,1,0:T(8,128)S(1)}, u32[]{:S(2)}, u32[]{:S(2)}) collective-permute-start(f32[16,40,128]{2,1,0:T(8,128)S(1)} %all_to_all.99.own), channel_id=1, source_target_pairs={{0,8},{8,0},{1,9},{9,1},{2,10},{10,2},{3,11},{11,3},{4,12},{12,4},... | collective-permute-start | bytes 983048 | tf_op jit(solution)/shard_map/ppermute | solution.py:304

commit v4 on v3

v4 whole, which is shorter than its diff:
```python
import jax
import jax.numpy as jnp
from jax import lax
from jax.experimental import pallas as pl
from jax.experimental.pallas import tpu as pltpu
from jax.sharding import PartitionSpec as P

ITERS = 4
S = 16
BS = 128
F32 = jnp.float32
HI = lax.Precision.HIGHEST
VMEM = pl.BlockSpec(memory_space=pltpu.VMEM)
SMEM = pl.BlockSpec(memory_space=pltpu.SMEM)
HBM = pl.BlockSpec(memory_space=pltpu.HBM)
TILE = 8


def sds(*shape, dtype=F32):
    return pltpu.VMEM(shape, dtype)


def call(body, outs, specs, *args, name, scratch=()):
    args = [
        a if spec is SMEM else pltpu.with_memory_space_constraint(a, spec.memory_space)
        for a, spec in zip(args, specs)
    ]
    return pl.pallas_call(
        body,
        out_shape=outs,
        in_specs=specs,
        out_specs=tuple(VMEM for _ in outs) if isinstance(outs, tuple) else VMEM,
        scratch_shapes=scratch,
        name=name,
        compiler_params=pltpu.CompilerParams(vmem_limit_bytes=8 << 20),
    )(*args)


def dot(a, b, contract=((1,), (0,))):
    return lax.dot_general(a, b, (contract, ((), ())), precision=HI, preferred_element_type=F32)


def bdot(a, b):
    return lax.dot_general(a, b, (((1,), (0,)), ((), ())), preferred_element_type=F32)


def halves(x):
    high = x.astype(jnp.bfloat16)
    return high, (x - high.astype(F32)).astype(jnp.bfloat16)


def wide(ref, at=()):
    return jnp.concatenate([ref[(*at, slice(0, S))], ref[(*at, slice(S, 2 * S))]], axis=1)


def spread(ref, value, tile):
    for k in range(ref.shape[0]):
        ref[k, 0:S] = value[:, :BS]
        ref[k, S : 2 * S] = value[:, BS:]
        ref[k, 2 * S : 2 * S + TILE] = tile


def solve(matrix, right):
    joined = jnp.concatenate([matrix, right], axis=1)
    row = lax.broadcasted_iota(jnp.int32, joined.shape, 0)
    for i in range(S):
        column = jnp.broadcast_to(joined[:, i : i + 1], joined.shape)
        pivot = joined[i : i + 1, :] / column[i : i + 1, :]
        joined = jnp.where(row == i, pivot, joined - column * pivot)
    return joined[:, S:]


def mix(vectors, small):
    return dot(small.T, vectors)


def grams(left, right):
    return dot(left, right, ((1,), (1,)))


def pack(products, sums=()):
    lane = lax.broadcasted_iota(jnp.int32, (TILE, 2 * S), 1)
    row = lax.broadcasted_iota(jnp.int32, (TILE, 2 * S), 0)
    rest = jnp.zeros((TILE, 2 * S), F32)
    for k, value in enumerate(sums):
        rest = jnp.where((row == 0) & (lane == k), value, rest)
    return jnp.concatenate([products[:TILE], products[TILE:], rest, rest], axis=1)


def unpack(tile):
    whole = jnp.concatenate([tile[:, : 2 * S], tile[:, 2 * S : 4 * S]], axis=0)
    return whole[:, :S], whole[:, S:], tile[:, 4 * S :]


def total(ref, first=0, last=None):
    value = ref[0, first:last]
    for k in range(1, ref.shape[0]):
        value = value + ref[k, first:last]
    image = jnp.concatenate([value[0:S], value[S : 2 * S]], axis=1)
    return image, value[2 * S :]


def entire(x):
    return jnp.sum(jnp.sum(x, axis=1, keepdims=True), axis=0, keepdims=True)


def fetch(blocks, held, done):
    copies = [pltpu.make_async_copy(blocks.at[i], held.at[i], done.at[i]) for i in range(16)]
    for copy in copies:
        copy.start()
    return copies


def prepare_body(source, counts, packed, blocks, done):
    copies = fetch(source, blocks, done)
    for i in range(16):
        copies[i].wait()
        for k in range(2):
            keep = (k < counts[0, i]).astype(F32)
            high, low = halves((blocks[i, k] * keep).T)
            packed[i, k * BS : (k + 1) * BS, 0:BS] = high
            packed[i, k * BS : (k + 1) * BS, BS : 2 * BS] = low


def product_body(own, peer, packed, cols, core, out):
    me = core[0]
    for i in range(16):
        picked = []
        for k in range(2):
            col = cols[k, i]
            m = col // 4
            b = pl.multiple_of((col % 2) * S, S)
            here = own[m, pl.ds(b, S), :]
            there = peer[m, pl.ds(b, S), :]
            picked.append(jnp.where((col // 2) % 2 == me, here, there))
        high, low = halves(jnp.concatenate(picked, axis=1))
        result = bdot(jnp.concatenate([high, low], axis=0), packed[i])
        result = (result[:S, :BS] + result[:S, BS:]) + (result[S:, :BS] + result[S:, BS:])
        out[i // 2, (i % 2) * S : (i % 2 + 1) * S] = result
    if own.shape[1] > 2 * S:
        tile, tile2 = own[0, 2 * S :], peer[0, 2 * S :]
        for m in range(1, 16):
            tile = tile + own[m, 2 * S :]
            tile2 = tile2 + peer[m, 2 * S :]
        for c in range(8):
            out[c, 2 * S :] = tile + tile2


def first_body(parts, shadow, diag, image, message):
    value, _ = total(parts)
    s = shadow[...]
    v = value + diag[...] * s
    image[...] = v
    spread(message, v, pack(grams(s, jnp.concatenate([v, s], axis=0))))


def lead_step(parts, diag, image, forward, residual, direction, solution):
    value, tile = total(parts)
    v = image[...]
    z = value + diag[...] * v
    matrix, right, _ = unpack(tile)
    alpha = solve(matrix, right)
    q = residual[...] - mix(v, alpha)
    t = forward[...] - mix(z, alpha)
    x = mix(direction[...], alpha)
    if solution is not None:
        x = x + solution[...]
    return matrix, z, q, t, x


def lead_body(
    parts, shadow, diag, image, forward, residual, direction, *rest
):
    solution, (z_out, q_out, t_out, x_out, matrix_out, message) = rest[:-6], rest[-6:]
    matrix, z, q, t, x = lead_step(
        parts, diag, image, forward, residual, direction, solution[0] if solution else None
    )
    z_out[...] = z
    q_out[...] = q
    t_out[...] = t
    x_out[...] = x
    matrix_out[...] = matrix
    products = grams(shadow[...], jnp.concatenate([t, t], axis=0))
    spread(message, t, pack(products, (entire(t * t), entire(t * q))))


def follow_body(
    parts, shadow, diag, image, direction, z, q, t, x, matrix,
    v_out, f_out, r_out, p_out, x_out, message,
):
    value, tile = total(parts)
    middle = t[...]
    f = value + diag[...] * middle
    cross, _, sums = unpack(tile)
    omega = sums[0:1, 1:2] / sums[0:1, 0:1]
    beta = -solve(matrix[...], cross)
    v = image[...]
    u = middle + mix(v, beta)
    y = f + mix(z[...], beta)
    residual = q[...] - omega * middle
    image_new = u - omega * y
    v_out[...] = image_new
    f_out[...] = middle - omega * f
    r_out[...] = residual
    p_out[...] = residual + mix(direction[...] - omega * v, beta)
    x_out[...] = x[...] + omega * q[...]
    products = grams(shadow[...], jnp.concatenate([image_new, residual], axis=0))
    spread(message, image_new, pack(products))


def last_body(parts, diag, image, forward, residual, direction, solution, q_out, x_out, sums):
    _, _, q, t, x = lead_step(parts, diag, image, forward, residual, direction, solution)
    q_out[...] = q
    x_out[...] = x
    lane = lax.broadcasted_iota(jnp.int32, (1, BS), 1)
    sums[...] = jnp.where(lane == 0, entire(t * t), jnp.where(lane == 1, entire(t * q), 0.0))


def end_body(sums, x, q, out):
    value = jnp.sum(sums[...], axis=0, keepdims=True)
    omega = value[0:1, 1:2] / value[0:1, 0:1]
    out[...] = x[...] + omega * q[...]


def per_device(rhs, diagonal, blocks, block_cols, counts):
    core = lax.axis_index("core").astype(jnp.int32).reshape(1)
    block_cols = block_cols.T
    counts = counts.T
    shadow = rhs.T
    diag = diagonal.reshape(1, 2 * BS)
    vec = sds(S, 2 * BS)
    small = sds(S, S)
    message = sds(16, 2 * S + TILE, BS)

    def among(x):
        return lax.all_to_all(x, ("x", "z"), 0, 0, tiled=True)

    def across(x):
        return lax.all_to_all(x, "cols", 0, 0, tiled=True)

    def product(own):
        peer = lax.ppermute(own, "core", [(0, 1), (1, 0)])
        out = call(
            product_body, sds(8, own.shape[1], BS), [VMEM, VMEM, VMEM, SMEM, SMEM],
            own, peer, packed, block_cols, core, name="product",
        )
        return across(out)

    held = [pltpu.VMEM((16, 2, BS, BS), F32), pltpu.SemaphoreType.DMA((16,))]
    piece = jnp.concatenate([shadow[:, :BS], shadow[:, BS:]], axis=0)
    packed = call(
        prepare_body, sds(16, 2 * BS, 2 * BS, dtype=jnp.bfloat16), [HBM, SMEM],
        blocks, counts, name="prepare", scratch=held,
    )
    parts = product(among(jnp.broadcast_to(piece[None], (16, 2 * S, BS))))
    v, msg = call(first_body, (vec, message), [VMEM] * 3, parts, shadow, diag, name="first")
    f, r, p, x = v, shadow, shadow, ()
    for iteration in range(ITERS):
        parts = product(among(msg))
        if iteration == ITERS - 1:
            break
        z, q, t, x, matrix, msg = call(
            lead_body, (vec, vec, vec, vec, small, message), [VMEM] * (7 + len(x)),
            parts, shadow, diag, v, f, r, p, *x, name="lead",
        )
        parts = product(among(msg))
        v, f, r, p, x, msg = call(
            follow_body, (vec, vec, vec, vec, vec, message), [VMEM] * 10,
            parts, shadow, diag, v, p, z, q, t, x, matrix, name="follow",
        )
        x = (x,)
    q, x, sums = call(
        last_body, (vec, vec, sds(1, BS)), [VMEM] * 7,
        parts, diag, v, f, r, p, *x, name="last",
    )
    everyone = 2 * 16 * 8
    sums = jnp.broadcast_to(sums[None], (everyone, 1, BS))
    sums = lax.all_to_all(sums, ("x", "z", "core", "cols"), 0, 0, tiled=True)
    out = call(end_body, vec, [VMEM] * 3, sums.reshape(everyone, BS), x, q, name="end")
    return out.T


def solution(mesh):
    parts = ("x", "z", "core")
    mesh = jax.sharding.Mesh(mesh.devices.reshape(2, 8, 2, 8), (*parts, "cols"))
    in_specs = (
        P((*parts, "cols"), None),
        P((*parts, "cols")),
        P(parts, "cols", None, None),
        P(parts, "cols"),
        P(parts, "cols"),
    )
    out_specs = P((*parts, "cols"), None)
    return jax.shard_map(
        per_device, mesh=mesh, in_specs=in_specs, out_specs=out_specs, check_vma=False
    )
```

time: 292 us -> 275 us (0.942)
  blocking collectives: 216 us -> 208 us
  Pallas kernels: 31.4 us -> 24.8 us
    all_to_all x8, blocking collectives: 112 us -> 104 us  [among(): return lax.all_to_all(x, ('x', 'z'), 0, 0, tiled=True)]
    pallas_call x19 -> x18, Pallas kernels: 31.4 us -> 24.8 us  [call(): pl.pallas_call(body, out_shape=outs, in_specs=specs, out_specs=tuple((VME...]
  transfers between devices with their start and end apart: 9 -> 8, of which waited for: 8 -> 7; matrix products, arithmetic and copies ran while one was open for 0% -> 0% of each run, Pallas kernels for 1% -> 1%
where the time goes in v4:
time: 275 us
  blocking collectives  208 us (76%)
  starting transfers between devices  30.5 us (11%)
  Pallas kernels  24.8 us (9%)
  waiting for transfers between devices  8.79 us (3%)
    all_to_all x8, blocking collectives, among(): return lax.all_to_all(x, ('x', 'z'), 0, 0, tiled=True)  104 us
    all_to_all x8, blocking collectives, across(): return lax.all_to_all(x, 'cols', 0, 0, tiled=True)  83.4 us
    ppermute x8, starting transfers between devices, product(): peer = lax.ppermute(own, 'core', [(0, 1), (1, 0)])  30.5 us
    pallas_call x18, Pallas kernels, call(): pl.pallas_call(body, out_shape=outs, in_specs=specs, out_specs=tuple((VME...  24.8 us
    all_to_all x1, blocking collectives, per_device(): sums = lax.all_to_all(sums, ('x', 'z', 'core', 'cols'), 0, 0, tiled=True)  20.4 us
    ppermute x8, waiting for transfers between devices, product(): peer = lax.ppermute(own, 'core', [(0, 1), (1, 0)])  8.79 us
  transfers between devices with their start and end apart: 8, of which 7 were waited for; matrix products, arithmetic and copies ran while one was open for 0% of the time, Pallas kernels for 1%

profile of v4, /device:TPU:1, one launch (start us, length us, event | category | flops | bytes accessed | tf_op | source)
XLA Modules:
  0.0 274.6 jit_solution(8369834813730011528)
XLA Ops:
  0.8 18.6 %all_to_all.85.own = f32[16,32,128]{2,1,0:T(8,128)S(1)} all-to-all(f32[16,32,128]{2,1,0:T(8,128)S(1)} %broadcast_in_dim.6), channel_id=1, replica_groups=mesh['x'=2,'z'=8,'core'=2,'cols'=8] {'x','z'}, dimensions={0} | all-to-all | bytes 524288 | tf_op jit(solution)/shard_map/all_to_all | solution.py:236
  19.4 2.3 collective-permute-start
  22.3 3.4 %prepare.1.packed = bf16[16,256,256]{2,1,0:T(8,128)(2,1)S(1)} custom-call(f32[16,2,128,128]{3,2,1,0:T(8,128)} %source.1, s32[1,16]{1,0:T(1,128)S(1)} %bitcast.37), custom_call_target="tpu_custom_call" | custom-call | tf_op jit(solution)/shard_map/prepare/pallas_call | solution.py:28
  26.9 13.1 %all_to_all.86.parts = f32[8,32,128]{2,1,0:T(8,128)S(1)} all-to-all(f32[8,32,128]{2,1,0:T(8,128)S(1)} %product.8), channel_id=1, replica_groups=mesh['x'=2,'z'=8,'core'=2,'cols'=8] {'cols'}, dimensions={0} | all-to-all | bytes 262144 | tf_op jit(solution)/shard_map/all_to_all | solution.py:239
  40.2 12.8 %all_to_all.87.own = f32[16,40,128]{2,1,0:T(8,128)S(1)} all-to-all(f32[16,40,128]{2,1,0:T(8,128)S(1)} %get-tuple-element.46), channel_id=1, replica_groups=mesh['x'=2,'z'=8,'core'=2,'cols'=8] {'x','z'}, dimensions={0} | all-to-all | bytes 655360 | tf_op jit(solution)/shard_map/all_to_all | solution.py:236
  53.0 3.2 %collective-permute-start.1 = (f32[16,40,128]{2,1,0:T(8,128)S(1)}, f32[16,40,128]{2,1,0:T(8,128)S(1)}, u32[]{:S(2)}, u32[]{:S(2)}) collective-permute-start(f32[16,40,128]{2,1,0:T(8,128)S(1)} %all_to_all.87.own), channel_id=1, source_target_pairs={{0,8},{8,0},{1,9},{9,1},{2,10},{10,2},{3,11},{11,3},{4,12},{12,4},... | collective-permute-start | bytes 983048 | tf_op jit(solution)/shard_map/ppermute | solution.py:242
  58.5 10.0 %all_to_all.88.parts = f32[8,40,128]{2,1,0:T(8,128)S(1)} all-to-all(f32[8,40,128]{2,1,0:T(8,128)S(1)} %product.9), channel_id=1, replica_groups=mesh['x'=2,'z'=8,'core'=2,'cols'=8] {'cols'}, dimensions={0} | all-to-all | bytes 327680 | tf_op jit(solution)/shard_map/all_to_all | solution.py:239
  68.5 1.8 lead.3
  70.3 12.1 %all_to_all.89.own = f32[16,40,128]{2,1,0:T(8,128)S(1)} all-to-all(f32[16,40,128]{2,1,0:T(8,128)S(1)} %get-tuple-element.48), channel_id=1, replica_groups=mesh['x'=2,'z'=8,'core'=2,'cols'=8] {'x','z'}, dimensions={0} | all-to-all | bytes 655360 | tf_op jit(solution)/shard_map/all_to_all | solution.py:236
  82.4 4.2 %collective-permute-start.2 = (f32[16,40,128]{2,1,0:T(8,128)S(1)}, f32[16,40,128]{2,1,0:T(8,128)S(1)}, u32[]{:S(2)}, u32[]{:S(2)}) collective-permute-start(f32[16,40,128]{2,1,0:T(8,128)S(1)} %all_to_all.89.own), channel_id=1, source_target_pairs={{0,8},{8,0},{1,9},{9,1},{2,10},{10,2},{3,11},{11,3},{4,12},{12,4},... | collective-permute-start | bytes 983048 | tf_op jit(solution)/shard_map/ppermute | solution.py:242
  88.9 10.7 %all_to_all.90.parts = f32[8,40,128]{2,1,0:T(8,128)S(1)} all-to-all(f32[8,40,128]{2,1,0:T(8,128)S(1)} %product.10), channel_id=1, replica_groups=mesh['x'=2,'z'=8,'core'=2,'cols'=8] {'cols'}, dimensions={0} | all-to-all | bytes 327680 | tf_op jit(solution)/shard_map/all_to_all | solution.py:239
  99.6 1.8 follow.3
  101.4 12.1 %all_to_all.91.own = f32[16,40,128]{2,1,0:T(8,128)S(1)} all-to-all(f32[16,40,128]{2,1,0:T(8,128)S(1)} %get-tuple-element.54), channel_id=1, replica_groups=mesh['x'=2,'z'=8,'core'=2,'cols'=8] {'x','z'}, dimensions={0} | all-to-all | bytes 655360 | tf_op jit(solution)/shard_map/all_to_all | solution.py:236
  113.5 4.2 %collective-permute-start.3 = (f32[16,40,128]{2,1,0:T(8,128)S(1)}, f32[16,40,128]{2,1,0:T(8,128)S(1)}, u32[]{:S(2)}, u32[]{:S(2)}) collective-permute-start(f32[16,40,128]{2,1,0:T(8,128)S(1)} %all_to_all.91.own), channel_id=1, source_target_pairs={{0,8},{8,0},{1,9},{9,1},{2,10},{10,2},{3,11},{11,3},{4,12},{12,4},... | collective-permute-start | bytes 983048 | tf_op jit(solution)/shard_map/ppermute | solution.py:242
  120.0 9.8 %all_to_all.92.parts = f32[8,40,128]{2,1,0:T(8,128)S(1)} all-to-all(f32[8,40,128]{2,1,0:T(8,128)S(1)} %product.11), channel_id=1, replica_groups=mesh['x'=2,'z'=8,'core'=2,'cols'=8] {'cols'}, dimensions={0} | all-to-all | bytes 327680 | tf_op jit(solution)/shard_map/all_to_all | solution.py:239
  129.7 1.8 lead.4
  131.5 12.3 %all_to_all.93.own = f32[16,40,128]{2,1,0:T(8,128)S(1)} all-to-all(f32[16,40,128]{2,1,0:T(8,128)S(1)} %get-tuple-element.60), channel_id=1, replica_groups=mesh['x'=2,'z'=8,'core'=2,'cols'=8] {'x','z'}, dimensions={0} | all-to-all | bytes 655360 | tf_op jit(solution)/shard_map/all_to_all | solution.py:236
  143.8 4.2 %collective-permute-start.4 = (f32[16,40,128]{2,1,0:T(8,128)S(1)}, f32[16,40,128]{2,1,0:T(8,128)S(1)}, u32[]{:S(2)}, u32[]{:S(2)}) collective-permute-start(f32[16,40,128]{2,1,0:T(8,128)S(1)} %all_to_all.93.own), channel_id=1, source_target_pairs={{0,8},{8,0},{1,9},{9,1},{2,10},{10,2},{3,11},{11,3},{4,12},{12,4},... | collective-permute-start | bytes 983048 | tf_op jit(solution)/shard_map/ppermute | solution.py:242
  150.3 10.1 %all_to_all.94.parts = f32[8,40,128]{2,1,0:T(8,128)S(1)} all-to-all(f32[8,40,128]{2,1,0:T(8,128)S(1)} %product.12), channel_id=1, replica_groups=mesh['x'=2,'z'=8,'core'=2,'cols'=8] {'cols'}, dimensions={0} | all-to-all | bytes 327680 | tf_op jit(solution)/shard_map/all_to_all | solution.py:239
  160.4 1.8 follow.4
  162.2 12.2 %all_to_all.95.own = f32[16,40,128]{2,1,0:T(8,128)S(1)} all-to-all(f32[16,40,128]{2,1,0:T(8,128)S(1)} %get-tuple-element.66), channel_id=1, replica_groups=mesh['x'=2,'z'=8,'core'=2,'cols'=8] {'x','z'}, dimensions={0} | all-to-all | bytes 655360 | tf_op jit(solution)/shard_map/all_to_all | solution.py:236
  174.4 4.2 %collective-permute-start.5 = (f32[16,40,128]{2,1,0:T(8,128)S(1)}, f32[16,40,128]{2,1,0:T(8,128)S(1)}, u32[]{:S(2)}, u32[]{:S(2)}) collective-permute-start(f32[16,40,128]{2,1,0:T(8,128)S(1)} %all_to_all.95.own), channel_id=1, source_target_pairs={{0,8},{8,0},{1,9},{9,1},{2,10},{10,2},{3,11},{11,3},{4,12},{12,4},... | collective-permute-start | bytes 983048 | tf_op jit(solution)/shard_map/ppermute | solution.py:242
  180.9 9.8 %all_to_all.96.parts = f32[8,40,128]{2,1,0:T(8,128)S(1)} all-to-all(f32[8,40,128]{2,1,0:T(8,128)S(1)} %product.13), channel_id=1, replica_groups=mesh['x'=2,'z'=8,'core'=2,'cols'=8] {'cols'}, dimensions={0} | all-to-all | bytes 327680 | tf_op jit(solution)/shard_map/all_to_all | solution.py:239
  190.7 1.8 lead.5
  192.4 12.3 %all_to_all.97.own = f32[16,40,128]{2,1,0:T(8,128)S(1)} all-to-all(f32[16,40,128]{2,1,0:T(8,128)S(1)} %get-tuple-element.72), channel_id=1, replica_groups=mesh['x'=2,'z'=8,'core'=2,'cols'=8] {'x','z'}, dimensions={0} | all-to-all | bytes 655360 | tf_op jit(solution)/shard_map/all_to_all | solution.py:236
  204.7 4.2 %collective-permute-start.6 = (f32[16,40,128]{2,1,0:T(8,128)S(1)}, f32[16,40,128]{2,1,0:T(8,128)S(1)}, u32[]{:S(2)}, u32[]{:S(2)}) collective-permute-start(f32[16,40,128]{2,1,0:T(8,128)S(1)} %all_to_all.97.own), channel_id=1, source_target_pairs={{0,8},{8,0},{1,9},{9,1},{2,10},{10,2},{3,11},{11,3},{4,12},{12,4},... | collective-permute-start | bytes 983048 | tf_op jit(solution)/shard_map/ppermute | solution.py:242
  211.2 10.1 %all_to_all.98.parts = f32[8,40,128]{2,1,0:T(8,128)S(1)} all-to-all(f32[8,40,128]{2,1,0:T(8,128)S(1)} %product.14), channel_id=1, replica_groups=mesh['x'=2,'z'=8,'core'=2,'cols'=8] {'cols'}, dimensions={0} | all-to-all | bytes 327680 | tf_op jit(solution)/shard_map/all_to_all | solution.py:239
  221.3 1.8 follow.5
  223.1 12.2 %all_to_all.99.own = f32[16,40,128]{2,1,0:T(8,128)S(1)} all-to-all(f32[16,40,128]{2,1,0:T(8,128)S(1)} %get-tuple-element.78), channel_id=1, replica_groups=mesh['x'=2,'z'=8,'core'=2,'cols'=8] {'x','z'}, dimensions={0} | all-to-all | bytes 655360 | tf_op jit(solution)/shard_map/all_to_all | solution.py:236
  235.3 4.2 %collective-permute-start.7 = (f32[16,40,128]{2,1,0:T(8,128)S(1)}, f32[16,40,128]{2,1,0:T(8,128)S(1)}, u32[]{:S(2)}, u32[]{:S(2)}) collective-permute-start(f32[16,40,128]{2,1,0:T(8,128)S(1)} %all_to_all.99.own), channel_id=1, source_target_pairs={{0,8},{8,0},{1,9},{9,1},{2,10},{10,2},{3,11},{11,3},{4,12},{12,4},... | collective-permute-start | bytes 983048 | tf_op jit(solution)/shard_map/ppermute | solution.py:242
  241.8 9.8 %all_to_all.100.parts = f32[8,40,128]{2,1,0:T(8,128)S(1)} all-to-all(f32[8,40,128]{2,1,0:T(8,128)S(1)} %product.15), channel_id=1, replica_groups=mesh['x'=2,'z'=8,'core'=2,'cols'=8] {'cols'}, dimensions={0} | all-to-all | bytes 327680 | tf_op jit(solution)/shard_map/all_to_all | solution.py:239
  253.4 20.4 %all_to_all.101 = f32[256,1,128]{2,1,0:T(1,128)S(1)} all-to-all(f32[256,1,128]{2,1,0:T(1,128)S(1)} %broadcast_in_dim.16), channel_id=1, replica_groups=mesh['x'=2,'z'=8,'core'=2,'cols'=8] {'x','z','core','cols'}, dimensions={0} | all-to-all | bytes 262144 | tf_op jit(solution)/shard_map/all_to_all | solution.py:278
  (32 shorter events, 21.5 us)
Async XLA Ops:
  19.4 6.4 %collective-permute-start = (f32[16,32,128]{2,1,0:T(8,128)S(1)}, f32[16,32,128]{2,1,0:T(8,128)S(1)}, u32[]{:S(2)}, u32[]{:S(2)}) collective-permute-start(f32[16,32,128]{2,1,0:T(8,128)S(1)} %all_to_all.85.own), channel_id=1, source_target_pairs={{0,8},{8,0},{1,9},{9,1},{2,10},{10,2},{3,11},{11,3},{4,12},{12,4},... | collective-permute-start | bytes 786440 | tf_op jit(solution)/shard_map/ppermute | solution.py:242
  21.7 0.7 copy-start.3
  22.3 3.4 %copy-start.1 = (s32[16,2]{0,1:T(2,128)S(1)}, s32[16,2]{0,1:T(2,128)}, u32[]{:S(2)}) copy-start(s32[16,2]{0,1:T(2,128)} %param.8) | copy-start | bytes 388
  25.7 14.2 %copy-start = (f32[256,16]{0,1:T(8,128)S(1)}, f32[256,16]{0,1:T(8,128)}, u32[]{:S(2)}) copy-start(f32[256,16]{0,1:T(8,128)} %param.5) | copy-start | bytes 49156
  25.8 14.2 %copy-start.2 = (f32[256]{0:T(256)S(1)}, f32[256]{0:T(256)}, u32[]{:S(2)}) copy-start(f32[256]{0:T(256)} %param.6) | copy-start | bytes 3076
  53.0 4.4 %collective-permute-start.1 = (f32[16,40,128]{2,1,0:T(8,128)S(1)}, f32[16,40,128]{2,1,0:T(8,128)S(1)}, u32[]{:S(2)}, u32[]{:S(2)}) collective-permute-start(f32[16,40,128]{2,1,0:T(8,128)S(1)} %all_to_all.87.own), channel_id=1, source_target_pairs={{0,8},{8,0},{1,9},{9,1},{2,10},{10,2},{3,11},{11,3},{4,12},{12,4},... | collective-permute-start | bytes 983048 | tf_op jit(solution)/shard_map/ppermute | solution.py:242
  82.4 5.4 %collective-permute-start.2 = (f32[16,40,128]{2,1,0:T(8,128)S(1)}, f32[16,40,128]{2,1,0:T(8,128)S(1)}, u32[]{:S(2)}, u32[]{:S(2)}) collective-permute-start(f32[16,40,128]{2,1,0:T(8,128)S(1)} %all_to_all.89.own), channel_id=1, source_target_pairs={{0,8},{8,0},{1,9},{9,1},{2,10},{10,2},{3,11},{11,3},{4,12},{12,4},... | collective-permute-start | bytes 983048 | tf_op jit(solution)/shard_map/ppermute | solution.py:242
  113.5 5.4 %collective-permute-start.3 = (f32[16,40,128]{2,1,0:T(8,128)S(1)}, f32[16,40,128]{2,1,0:T(8,128)S(1)}, u32[]{:S(2)}, u32[]{:S(2)}) collective-permute-start(f32[16,40,128]{2,1,0:T(8,128)S(1)} %all_to_all.91.own), channel_id=1, source_target_pairs={{0,8},{8,0},{1,9},{9,1},{2,10},{10,2},{3,11},{11,3},{4,12},{12,4},... | collective-permute-start | bytes 983048 | tf_op jit(solution)/shard_map/ppermute | solution.py:242
  143.8 5.4 %collective-permute-start.4 = (f32[16,40,128]{2,1,0:T(8,128)S(1)}, f32[16,40,128]{2,1,0:T(8,128)S(1)}, u32[]{:S(2)}, u32[]{:S(2)}) collective-permute-start(f32[16,40,128]{2,1,0:T(8,128)S(1)} %all_to_all.93.own), channel_id=1, source_target_pairs={{0,8},{8,0},{1,9},{9,1},{2,10},{10,2},{3,11},{11,3},{4,12},{12,4},... | collective-permute-start | bytes 983048 | tf_op jit(solution)/shard_map/ppermute | solution.py:242
  174.4 5.4 %collective-permute-start.5 = (f32[16,40,128]{2,1,0:T(8,128)S(1)}, f32[16,40,128]{2,1,0:T(8,128)S(1)}, u32[]{:S(2)}, u32[]{:S(2)}) collective-permute-start(f32[16,40,128]{2,1,0:T(8,128)S(1)} %all_to_all.95.own), channel_id=1, source_target_pairs={{0,8},{8,0},{1,9},{9,1},{2,10},{10,2},{3,11},{11,3},{4,12},{12,4},... | collective-permute-start | bytes 983048 | tf_op jit(solution)/shard_map/ppermute | solution.py:242
  204.7 5.4 %collective-permute-start.6 = (f32[16,40,128]{2,1,0:T(8,128)S(1)}, f32[16,40,128]{2,1,0:T(8,128)S(1)}, u32[]{:S(2)}, u32[]{:S(2)}) collective-permute-start(f32[16,40,128]{2,1,0:T(8,128)S(1)} %all_to_all.97.own), channel_id=1, source_target_pairs={{0,8},{8,0},{1,9},{9,1},{2,10},{10,2},{3,11},{11,3},{4,12},{12,4},... | collective-permute-start | bytes 983048 | tf_op jit(solution)/shard_map/ppermute | solution.py:242
  235.3 5.4 %collective-permute-start.7 = (f32[16,40,128]{2,1,0:T(8,128)S(1)}, f32[16,40,128]{2,1,0:T(8,128)S(1)}, u32[]{:S(2)}, u32[]{:S(2)}) collective-permute-start(f32[16,40,128]{2,1,0:T(8,128)S(1)} %all_to_all.99.own), channel_id=1, source_target_pairs={{0,8},{8,0},{1,9},{9,1},{2,10},{10,2},{3,11},{11,3},{4,12},{12,4},... | collective-permute-start | bytes 983048 | tf_op jit(solution)/shard_map/ppermute | solution.py:242

commit v5 on v4

--- a/solution.py
+++ b/solution.py
@@ -4,6 +4,7 @@
 from jax.experimental import pallas as pl
 from jax.experimental.pallas import tpu as pltpu
 from jax.sharding import PartitionSpec as P
+
 
 ITERS = 4
 S = 16
@@ -20,7 +21,7 @@
     return pltpu.VMEM(shape, dtype)
 
 
-def call(body, outs, specs, *args, name, scratch=()):
+def call(body, outs, specs, *args, scratch=()):
     args = [
         a if spec is SMEM else pltpu.with_memory_space_constraint(a, spec.memory_space)
         for a, spec in zip(args, specs)
@@ -31,7 +32,6 @@
         in_specs=specs,
         out_specs=tuple(VMEM for _ in outs) if isinstance(outs, tuple) else VMEM,
         scratch_shapes=scratch,
-        name=name,
         compiler_params=pltpu.CompilerParams(vmem_limit_bytes=8 << 20),
     )(*args)
 
@@ -47,10 +47,6 @@
 def halves(x):
     high = x.astype(jnp.bfloat16)
     return high, (x - high.astype(F32)).astype(jnp.bfloat16)
-
-
-def wide(ref, at=()):
-    return jnp.concatenate([ref[(*at, slice(0, S))], ref[(*at, slice(S, 2 * S))]], axis=1)
 
 
 def spread(ref, value, tile):
@@ -154,7 +150,7 @@
     spread(message, v, pack(grams(s, jnp.concatenate([v, s], axis=0))))
 
 
-def lead_step(parts, diag, image, forward, residual, direction, solution):
+def lead_step(parts, diag, image, forward, residual):
     value, tile = total(parts)
     v = image[...]
     z = value + diag[...] * v
@@ -162,58 +158,73 @@
     alpha = solve(matrix, right)
     q = residual[...] - mix(v, alpha)
     t = forward[...] - mix(z, alpha)
-    x = mix(direction[...], alpha)
-    if solution is not None:
-        x = x + solution[...]
-    return matrix, z, q, t, x
+    return matrix, alpha, z, q, t
 
 
 def lead_body(
-    parts, shadow, diag, image, forward, residual, direction, *rest
+    parts, shadow, diag, image, forward, residual, z_out, q_out, t_out, alpha_out, matrix_out, message
 ):
-    solution, (z_out, q_out, t_out, x_out, matrix_out, message) = rest[:-6], rest[-6:]
-    matrix, z, q, t, x = lead_step(
-        parts, diag, image, forward, residual, direction, solution[0] if solution else None
-    )
+    matrix, alpha, z, q, t = lead_step(parts, diag, image, forward, residual)
     z_out[...] = z
     q_out[...] = q
     t_out[...] = t
-    x_out[...] = x
+    alpha_out[...] = alpha
     matrix_out[...] = matrix
     products = grams(shadow[...], jnp.concatenate([t, t], axis=0))
     spread(message, t, pack(products, (entire(t * t), entire(t * q))))
 
 
+def lead_rest_body(matrix, alpha, direction, *rest):
+    solution, (inverse_out, x_out) = rest[:-2], rest[-2:]
+    row = lax.broadcasted_iota(jnp.int32, (S, S), 0)
+    col = lax.broadcasted_iota(jnp.int32, (S, S), 1)
+    inverse_out[...] = solve(matrix[...], (row == col).astype(F32))
+    x = mix(direction[...], alpha[...])
+    x_out[...] = x + solution[0][...] if solution else x
+
+
 def follow_body(
-    parts, shadow, diag, image, direction, z, q, t, x, matrix,
-    v_out, f_out, r_out, p_out, x_out, message,
+    parts, shadow, diag, image, z, q, t, inverse, v_out, f_out, r_out, beta_out, omega_out, message
 ):
     value, tile = total(parts)
     middle = t[...]
     f = value + diag[...] * middle
     cross, _, sums = unpack(tile)
     omega = sums[0:1, 1:2] / sums[0:1, 0:1]
-    beta = -solve(matrix[...], cross)
-    v = image[...]
-    u = middle + mix(v, beta)
+    beta = -dot(inverse[...], cross)
+    residual = q[...] - omega * middle
     y = f + mix(z[...], beta)
-    residual = q[...] - omega * middle
-    image_new = u - omega * y
+    image_new = (middle + mix(image[...], beta)) - omega * y
     v_out[...] = image_new
-    f_out[...] = middle - omega * f
+    f_out[...] = f
     r_out[...] = residual
-    p_out[...] = residual + mix(direction[...] - omega * v, beta)
-    x_out[...] = x[...] + omega * q[...]
+    beta_out[...] = beta
+    omega_out[...] = jnp.broadcast_to(omega, omega_out.shape)
     products = grams(shadow[...], jnp.concatenate([image_new, residual], axis=0))
     spread(message, image_new, pack(products))
 
 
-def last_body(parts, diag, image, forward, residual, direction, solution, q_out, x_out, sums):
-    _, _, q, t, x = lead_step(parts, diag, image, forward, residual, direction, solution)
+def follow_rest_body(t, f, r, beta, omega, image, direction, q, x, forward_out, p_out, x_out):
+    o = omega[0:1, 0:1]
+    forward_out[...] = t[...] - o * f[...]
+    p_out[...] = r[...] + mix(direction[...] - o * image[...], beta[...])
+    x_out[...] = x[...] + o * q[...]
+
+
+def last_body(parts, diag, image, forward, residual, q_out, alpha_out, sums):
+    _, alpha, _, q, t = lead_step(parts, diag, image, forward, residual)
     q_out[...] = q
-    x_out[...] = x
+    alpha_out[...] = alpha
     lane = lax.broadcasted_iota(jnp.int32, (1, BS), 1)
     sums[...] = jnp.where(lane == 0, entire(t * t), jnp.where(lane == 1, entire(t * q), 0.0))
+
+
+def last_rest_body(alpha, direction, x, x_out):
+    x_out[...] = x[...] + mix(direction[...], alpha[...])
+
+
+def join_body(mine, theirs, out):
+    out[...] = jnp.broadcast_to((mine[...] + theirs[...])[None], out.shape)
 
 
 def end_body(sums, x, q, out):
@@ -232,6 +243,8 @@
     small = sds(S, S)
     message = sds(16, 2 * S + TILE, BS)
 
+    swap = [(0, 1), (1, 0)]
+
     def among(x):
         return lax.all_to_all(x, ("x", "z"), 0, 0, tiled=True)
 
@@ -239,44 +252,50 @@
         return lax.all_to_all(x, "cols", 0, 0, tiled=True)
 
     def product(own):
-        peer = lax.ppermute(own, "core", [(0, 1), (1, 0)])
+        peer = lax.ppermute(own, "core", swap)
         out = call(
             product_body, sds(8, own.shape[1], BS), [VMEM, VMEM, VMEM, SMEM, SMEM],
-            own, peer, packed, block_cols, core, name="product",
+            own, peer, packed, block_cols, core,
         )
         return across(out)
 
     held = [pltpu.VMEM((16, 2, BS, BS), F32), pltpu.SemaphoreType.DMA((16,))]
     piece = jnp.concatenate([shadow[:, :BS], shadow[:, BS:]], axis=0)
+    own = among(jnp.broadcast_to(piece[None], (16, 2 * S, BS)))
     packed = call(
         prepare_body, sds(16, 2 * BS, 2 * BS, dtype=jnp.bfloat16), [HBM, SMEM],
-        blocks, counts, name="prepare", scratch=held,
+        blocks, counts, scratch=held,
     )
-    parts = product(among(jnp.broadcast_to(piece[None], (16, 2 * S, BS))))
-    v, msg = call(first_body, (vec, message), [VMEM] * 3, parts, shadow, diag, name="first")
+    parts = product(own)
+    v, msg = call(first_body, (vec, message), [VMEM] * 3, parts, shadow, diag)
     f, r, p, x = v, shadow, shadow, ()
-    for iteration in range(ITERS):
-        parts = product(among(msg))
-        if iteration == ITERS - 1:
-            break
-        z, q, t, x, matrix, msg = call(
-            lead_body, (vec, vec, vec, vec, small, message), [VMEM] * (7 + len(x)),
-            parts, shadow, diag, v, f, r, p, *x, name="lead",
+    parts = product(among(msg))
+    for _ in range(1, ITERS):
+        z, q, t, alpha, matrix, msg = call(
+            lead_body, (vec, vec, vec, small, small, message), [VMEM] * 6,
+            parts, shadow, diag, v, f, r,
         )
-        parts = product(among(msg))
-        v, f, r, p, x, msg = call(
-            follow_body, (vec, vec, vec, vec, vec, message), [VMEM] * 10,
-            parts, shadow, diag, v, p, z, q, t, x, matrix, name="follow",
+        own = among(msg)
+        inverse, x = call(lead_rest_body, (small, vec), [VMEM] * (3 + len(x)), matrix, alpha, p, *x)
+        parts = product(own)
+        image = v
+        v, half, r, beta, omega, msg = call(
+            follow_body, (vec, vec, vec, small, sds(1, BS), message), [VMEM] * 8,
+            parts, shadow, diag, image, z, q, t, inverse,
         )
+        own = among(msg)
+        f, p, x = call(
+            follow_rest_body, (vec, vec, vec), [VMEM] * 9,
+            t, half, r, beta, omega, image, p, q, x,
+        )
+        parts = product(own)
         x = (x,)
-    q, x, sums = call(
-        last_body, (vec, vec, sds(1, BS)), [VMEM] * 7,
-        parts, diag, v, f, r, p, *x, name="last",
-    )
-    everyone = 2 * 16 * 8
-    sums = jnp.broadcast_to(sums[None], (everyone, 1, BS))
-    sums = lax.all_to_all(sums, ("x", "z", "core", "cols"), 0, 0, tiled=True)
-    out = call(end_body, vec, [VMEM] * 3, sums.reshape(everyone, BS), x, q, name="end")
+    q, alpha, sums = call(last_body, (vec, small, sds(1, BS)), [VMEM] * 5, parts, diag, v, f, r)
+    theirs = lax.ppermute(sums, "core", swap)
+    x = call(last_rest_body, vec, [VMEM] * 3, alpha, p, *x)
+    sums = call(join_body, sds(128, 1, BS), [VMEM] * 2, sums, theirs)
+    sums = lax.all_to_all(sums, ("x", "z", "cols"), 0, 0, tiled=True)
+    out = call(end_body, vec, [VMEM] * 3, sums.reshape(128, BS), x, q)
     return out.T
 
 

time: 275 us -> 280 us (1.018)
  blocking collectives: 208 us -> 129 us
  waiting for transfers between devices: 8.79 us -> 57.5 us
  starting transfers between devices: 30.5 us -> 59.6 us
  Pallas kernels: 24.8 us -> 30.9 us
    all_to_all x8 -> x2, blocking collectives: 83.4 us -> 23.1 us  [across(): return lax.all_to_all(x, 'cols', 0, 0, tiled=True)]
    all_to_all x0 -> x7, waiting for transfers between devices: none -> 47.9 us  [the longest x6 37.7 us: across(): return lax.all_to_all(x, 'cols', 0, 0, tiled=True)]
    all_to_all x0 -> x7, starting transfers between devices: none -> 29.2 us  [the longest x6 21.9 us: across(): return lax.all_to_all(x, 'cols', 0, 0, tiled=True)]
    all_to_all x1 -> x0, blocking collectives: 20.4 us -> none  [per_device(): sums = lax.all_to_all(sums, ('x', 'z', 'core', 'cols'), 0, 0, tiled=True)]
    pallas_call x18 -> x26, Pallas kernels: 24.8 us -> 30.9 us  [call(): pl.pallas_call(body, out_shape=outs, in_specs=specs, out_specs=tuple((VME...]
    ppermute x8 -> x9, waiting for transfers between devices: 8.79 us -> 9.61 us  [the longest x8 8.79 us: product(): peer = lax.ppermute(own, 'core', swap)]
    ppermute x8 -> x9, starting transfers between devices: 30.5 us -> 30.4 us  [the longest x8 28.8 us: product(): peer = lax.ppermute(own, 'core', swap)]
  transfers between devices with their start and end apart: 8 -> 16, of which waited for: 7 -> 15; matrix products, arithmetic and copies ran while one was open for 0% -> 0% of each run, Pallas kernels for 1% -> 3%
where the time goes in v5:
time: 280 us; the launch traced here: 279 us
  blocking collectives  129 us (46%)
  starting transfers between devices  59.6 us (21%)
  waiting for transfers between devices  57.5 us (21%)
  Pallas kernels  30.9 us (11%)
    all_to_all x8, blocking collectives, among(): return lax.all_to_all(x, ('x', 'z'), 0, 0, tiled=True)  106 us
    all_to_all x6, waiting for transfers between devices, across(): return lax.all_to_all(x, 'cols', 0, 0, tiled=True)  37.7 us
    pallas_call x26, Pallas kernels, call(): pl.pallas_call(body, out_shape=outs, in_specs=specs, out_specs=tuple((VME...  30.9 us
    ppermute x8, starting transfers between devices, product(): peer = lax.ppermute(own, 'core', swap)  28.8 us
    all_to_all x2, blocking collectives, across(): return lax.all_to_all(x, 'cols', 0, 0, tiled=True)  23.1 us
    all_to_all x6, starting transfers between devices, across(): return lax.all_to_all(x, 'cols', 0, 0, tiled=True)  21.9 us
    all_to_all x1, waiting for transfers between devices, per_device(): sums = lax.all_to_all(sums, ('x', 'z', 'cols'), 0, 0, tiled=True)  10.2 us
    ppermute x8, waiting for transfers between devices, product(): peer = lax.ppermute(own, 'core', swap)  8.79 us
  transfers between devices with their start and end apart: 16, of which 15 were waited for; matrix products, arithmetic and copies ran while one was open for 0% of the time, Pallas kernels for 3%

profile of v5, /device:TPU:1, one launch (start us, length us, event | category | flops | bytes accessed | tf_op | source)
XLA Modules:
  0.0 279.0 jit_solution(5010162401840931664)
XLA Ops:
  0.8 18.6 %all_to_all.85.own = f32[16,32,128]{2,1,0:T(8,128)S(1)} all-to-all(f32[16,32,128]{2,1,0:T(8,128)S(1)} %broadcast_in_dim.2), channel_id=1, replica_groups=mesh['x'=2,'z'=8,'core'=2,'cols'=8] {'x','z'}, dimensions={0} | all-to-all | bytes 524288 | tf_op jit(solution)/shard_map/all_to_all | solution.py:249
  22.3 3.4 %shard_map.55.packed = bf16[16,256,256]{2,1,0:T(8,128)(2,1)S(1)} custom-call(f32[16,2,128,128]{3,2,1,0:T(8,128)} %source.1, s32[1,16]{1,0:T(1,128)S(1)} %bitcast.36), custom_call_target="tpu_custom_call" | custom-call | tf_op jit(solution)/shard_map/pallas_call | solution.py:29
  26.9 13.1 %all_to_all.86.parts = f32[8,32,128]{2,1,0:T(8,128)S(1)} all-to-all(f32[8,32,128]{2,1,0:T(8,128)S(1)} %shard_map.56), channel_id=1, replica_groups=mesh['x'=2,'z'=8,'core'=2,'cols'=8] {'cols'}, dimensions={0} | all-to-all | bytes 262144 | tf_op jit(solution)/shard_map/all_to_all | solution.py:252
  40.2 12.8 %all_to_all.87.own = f32[16,40,128]{2,1,0:T(8,128)S(1)} all-to-all(f32[16,40,128]{2,1,0:T(8,128)S(1)} %get-tuple-element.61), channel_id=1, replica_groups=mesh['x'=2,'z'=8,'core'=2,'cols'=8] {'x','z'}, dimensions={0} | all-to-all | bytes 655360 | tf_op jit(solution)/shard_map/all_to_all | solution.py:249
  53.0 3.2 %collective-permute-start.1 = (f32[16,40,128]{2,1,0:T(8,128)S(1)}, f32[16,40,128]{2,1,0:T(8,128)S(1)}, u32[]{:S(2)}, u32[]{:S(2)}) collective-permute-start(f32[16,40,128]{2,1,0:T(8,128)S(1)} %all_to_all.87.own), channel_id=1, source_target_pairs={{0,8},{8,0},{1,9},{9,1},{2,10},{10,2},{3,11},{11,3},{4,12},{12,4},... | collective-permute-start | bytes 983048 | tf_op jit(solution)/shard_map/ppermute | solution.py:255
  58.5 10.0 %all_to_all.88.parts = f32[8,40,128]{2,1,0:T(8,128)S(1)} all-to-all(f32[8,40,128]{2,1,0:T(8,128)S(1)} %shard_map.58), channel_id=1, replica_groups=mesh['x'=2,'z'=8,'core'=2,'cols'=8] {'cols'}, dimensions={0} | all-to-all | bytes 327680 | tf_op jit(solution)/shard_map/all_to_all | solution.py:252
  70.3 12.0 %all_to_all.89.own = f32[16,40,128]{2,1,0:T(8,128)S(1)} all-to-all(f32[16,40,128]{2,1,0:T(8,128)S(1)} %get-tuple-element.63), channel_id=1, replica_groups=mesh['x'=2,'z'=8,'core'=2,'cols'=8] {'x','z'}, dimensions={0} | all-to-all | bytes 655360 | tf_op jit(solution)/shard_map/all_to_all | solution.py:249
  82.3 4.2 %collective-permute-start.2 = (f32[16,40,128]{2,1,0:T(8,128)S(1)}, f32[16,40,128]{2,1,0:T(8,128)S(1)}, u32[]{:S(2)}, u32[]{:S(2)}) collective-permute-start(f32[16,40,128]{2,1,0:T(8,128)S(1)} %all_to_all.89.own), channel_id=1, source_target_pairs={{0,8},{8,0},{1,9},{9,1},{2,10},{10,2},{3,11},{11,3},{4,12},{12,4},... | collective-permute-start | bytes 983048 | tf_op jit(solution)/shard_map/ppermute | solution.py:255
  89.5 3.8 %all-to-all-start.5 = ((f32[8,40,128]{2,1,0:T(8,128)}), f32[8,40,128]{2,1,0:T(8,128)S(1)}, u32[]{:S(2)}, u32[]{:S(2)}) async-start(f32[8,40,128]{2,1,0:T(8,128)} %shard_map.60), calls=%async_computation.5 | async-start | bytes 327680 | tf_op jit(solution)/shard_map/all_to_all | solution.py:252
  94.7 5.7 %all-to-all-done.5.parts = f32[8,40,128]{2,1,0:T(8,128)S(1)} async-done(((f32[8,40,128]{2,1,0:T(8,128)}), f32[8,40,128]{2,1,0:T(8,128)S(1)}, u32[]{:S(2)}, u32[]{:S(2)}) %all-to-all-start.5) | async-done | bytes 163872 | tf_op jit(solution)/shard_map/all_to_all | solution.py:252
  101.0 12.0 %all_to_all.90.own = f32[16,40,128]{2,1,0:T(8,128)S(1)} all-to-all(f32[16,40,128]{2,1,0:T(8,128)S(1)} %get-tuple-element.70), channel_id=1, replica_groups=mesh['x'=2,'z'=8,'core'=2,'cols'=8] {'x','z'}, dimensions={0} | all-to-all | bytes 655360 | tf_op jit(solution)/shard_map/all_to_all | solution.py:249
  113.1 4.2 %collective-permute-start.3 = (f32[16,40,128]{2,1,0:T(8,128)S(1)}, f32[16,40,128]{2,1,0:T(8,128)S(1)}, u32[]{:S(2)}, u32[]{:S(2)}) collective-permute-start(f32[16,40,128]{2,1,0:T(8,128)S(1)} %all_to_all.90.own), channel_id=1, source_target_pairs={{0,8},{8,0},{1,9},{9,1},{2,10},{10,2},{3,11},{11,3},{4,12},{12,4},... | collective-permute-start | bytes 983048 | tf_op jit(solution)/shard_map/ppermute | solution.py:255
  120.2 3.4 %all-to-all-start.7 = ((f32[8,40,128]{2,1,0:T(8,128)}), f32[8,40,128]{2,1,0:T(8,128)S(1)}, u32[]{:S(2)}, u32[]{:S(2)}) async-start(f32[8,40,128]{2,1,0:T(8,128)} %shard_map.63), calls=%async_computation.7 | async-start | bytes 327680 | tf_op jit(solution)/shard_map/all_to_all | solution.py:252
  123.8 6.8 %all-to-all-done.7.parts = f32[8,40,128]{2,1,0:T(8,128)S(1)} async-done(((f32[8,40,128]{2,1,0:T(8,128)}), f32[8,40,128]{2,1,0:T(8,128)S(1)}, u32[]{:S(2)}, u32[]{:S(2)}) %all-to-all-start.7) | async-done | bytes 163872 | tf_op jit(solution)/shard_map/all_to_all | solution.py:252
  132.4 13.1 %all_to_all.91.own = f32[16,40,128]{2,1,0:T(8,128)S(1)} all-to-all(f32[16,40,128]{2,1,0:T(8,128)S(1)} %get-tuple-element.78), channel_id=1, replica_groups=mesh['x'=2,'z'=8,'core'=2,'cols'=8] {'x','z'}, dimensions={0} | all-to-all | bytes 655360 | tf_op jit(solution)/shard_map/all_to_all | solution.py:249
  145.5 3.3 %collective-permute-start.4 = (f32[16,40,128]{2,1,0:T(8,128)S(1)}, f32[16,40,128]{2,1,0:T(8,128)S(1)}, u32[]{:S(2)}, u32[]{:S(2)}) collective-permute-start(f32[16,40,128]{2,1,0:T(8,128)S(1)} %all_to_all.91.own), channel_id=1, source_target_pairs={{0,8},{8,0},{1,9},{9,1},{2,10},{10,2},{3,11},{11,3},{4,12},{12,4},... | collective-permute-start | bytes 983048 | tf_op jit(solution)/shard_map/ppermute | solution.py:255
  151.8 4.0 %all-to-all-start.9 = ((f32[8,40,128]{2,1,0:T(8,128)}), f32[8,40,128]{2,1,0:T(8,128)S(1)}, u32[]{:S(2)}, u32[]{:S(2)}) async-start(f32[8,40,128]{2,1,0:T(8,128)} %shard_map.66), calls=%async_computation.9 | async-start | bytes 327680 | tf_op jit(solution)/shard_map/all_to_all | solution.py:252
  157.2 5.7 %all-to-all-done.9.parts = f32[8,40,128]{2,1,0:T(8,128)S(1)} async-done(((f32[8,40,128]{2,1,0:T(8,128)}), f32[8,40,128]{2,1,0:T(8,128)S(1)}, u32[]{:S(2)}, u32[]{:S(2)}) %all-to-all-start.9) | async-done | bytes 163872 | tf_op jit(solution)/shard_map/all_to_all | solution.py:252
  163.6 12.0 %all_to_all.92.own = f32[16,40,128]{2,1,0:T(8,128)S(1)} all-to-all(f32[16,40,128]{2,1,0:T(8,128)S(1)} %get-tuple-element.87), channel_id=1, replica_groups=mesh['x'=2,'z'=8,'core'=2,'cols'=8] {'x','z'}, dimensions={0} | all-to-all | bytes 655360 | tf_op jit(solution)/shard_map/all_to_all | solution.py:249
  175.6 4.2 %collective-permute-start.5 = (f32[16,40,128]{2,1,0:T(8,128)S(1)}, f32[16,40,128]{2,1,0:T(8,128)S(1)}, u32[]{:S(2)}, u32[]{:S(2)}) collective-permute-start(f32[16,40,128]{2,1,0:T(8,128)S(1)} %all_to_all.92.own), channel_id=1, source_target_pairs={{0,8},{8,0},{1,9},{9,1},{2,10},{10,2},{3,11},{11,3},{4,12},{12,4},... | collective-permute-start | bytes 983048 | tf_op jit(solution)/shard_map/ppermute | solution.py:255
  182.8 3.4 %all-to-all-start.11 = ((f32[8,40,128]{2,1,0:T(8,128)}), f32[8,40,128]{2,1,0:T(8,128)S(1)}, u32[]{:S(2)}, u32[]{:S(2)}) async-start(f32[8,40,128]{2,1,0:T(8,128)} %shard_map.69), calls=%async_computation.11 | async-start | bytes 327680 | tf_op jit(solution)/shard_map/all_to_all | solution.py:252
  186.4 6.8 %all-to-all-done.11.parts = f32[8,40,128]{2,1,0:T(8,128)S(1)} async-done(((f32[8,40,128]{2,1,0:T(8,128)}), f32[8,40,128]{2,1,0:T(8,128)S(1)}, u32[]{:S(2)}, u32[]{:S(2)}) %all-to-all-start.11) | async-done | bytes 163872 | tf_op jit(solution)/shard_map/all_to_all | solution.py:252
  195.0 13.1 %all_to_all.93.own = f32[16,40,128]{2,1,0:T(8,128)S(1)} all-to-all(f32[16,40,128]{2,1,0:T(8,128)S(1)} %get-tuple-element.95), channel_id=1, replica_groups=mesh['x'=2,'z'=8,'core'=2,'cols'=8] {'x','z'}, dimensions={0} | all-to-all | bytes 655360 | tf_op jit(solution)/shard_map/all_to_all | solution.py:249
  208.1 3.3 %collective-permute-start.6 = (f32[16,40,128]{2,1,0:T(8,128)S(1)}, f32[16,40,128]{2,1,0:T(8,128)S(1)}, u32[]{:S(2)}, u32[]{:S(2)}) collective-permute-start(f32[16,40,128]{2,1,0:T(8,128)S(1)} %all_to_all.93.own), channel_id=1, source_target_pairs={{0,8},{8,0},{1,9},{9,1},{2,10},{10,2},{3,11},{11,3},{4,12},{12,4},... | collective-permute-start | bytes 983048 | tf_op jit(solution)/shard_map/ppermute | solution.py:255
  214.4 4.0 %all-to-all-start.13 = ((f32[8,40,128]{2,1,0:T(8,128)}), f32[8,40,128]{2,1,0:T(8,128)S(1)}, u32[]{:S(2)}, u32[]{:S(2)}) async-start(f32[8,40,128]{2,1,0:T(8,128)} %shard_map.72), calls=%async_computation.13 | async-start | bytes 327680 | tf_op jit(solution)/shard_map/all_to_all | solution.py:252
  219.8 5.7 %all-to-all-done.13.parts = f32[8,40,128]{2,1,0:T(8,128)S(1)} async-done(((f32[8,40,128]{2,1,0:T(8,128)}), f32[8,40,128]{2,1,0:T(8,128)S(1)}, u32[]{:S(2)}, u32[]{:S(2)}) %all-to-all-start.13) | async-done | bytes 163872 | tf_op jit(solution)/shard_map/all_to_all | solution.py:252
  226.1 12.0 %all_to_all.94.own = f32[16,40,128]{2,1,0:T(8,128)S(1)} all-to-all(f32[16,40,128]{2,1,0:T(8,128)S(1)} %get-tuple-element.104), channel_id=1, replica_groups=mesh['x'=2,'z'=8,'core'=2,'cols'=8] {'x','z'}, dimensions={0} | all-to-all | bytes 655360 | tf_op jit(solution)/shard_map/all_to_all | solution.py:249
  238.1 4.2 %collective-permute-start.7 = (f32[16,40,128]{2,1,0:T(8,128)S(1)}, f32[16,40,128]{2,1,0:T(8,128)S(1)}, u32[]{:S(2)}, u32[]{:S(2)}) collective-permute-start(f32[16,40,128]{2,1,0:T(8,128)S(1)} %all_to_all.94.own), channel_id=1, source_target_pairs={{0,8},{8,0},{1,9},{9,1},{2,10},{10,2},{3,11},{11,3},{4,12},{12,4},... | collective-permute-start | bytes 983048 | tf_op jit(solution)/shard_map/ppermute | solution.py:255
  245.3 3.4 %all-to-all-start.15 = ((f32[8,40,128]{2,1,0:T(8,128)}), f32[8,40,128]{2,1,0:T(8,128)S(1)}, u32[]{:S(2)}, u32[]{:S(2)}) async-start(f32[8,40,128]{2,1,0:T(8,128)} %shard_map.75), calls=%async_computation.15 | async-start | bytes 327680 | tf_op jit(solution)/shard_map/all_to_all | solution.py:252
  248.9 6.8 %all-to-all-done.15.parts = f32[8,40,128]{2,1,0:T(8,128)S(1)} async-done(((f32[8,40,128]{2,1,0:T(8,128)}), f32[8,40,128]{2,1,0:T(8,128)S(1)}, u32[]{:S(2)}, u32[]{:S(2)}) %all-to-all-start.15) | async-done | bytes 163872 | tf_op jit(solution)/shard_map/all_to_all | solution.py:252
  260.5 7.3 %all-to-all-start.16 = ((f32[128,1,128]{2,1,0:T(1,128)}), f32[128,1,128]{2,1,0:T(1,128)S(1)}, u32[]{:S(2)}, u32[]{:S(2)}) async-start(f32[128,1,128]{2,1,0:T(1,128)} %shard_map.78), calls=%async_computation.16 | async-start | bytes 131072 | tf_op jit(solution)/shard_map/all_to_all | solution.py:297
  267.9 10.2 %all-to-all-done.16 = f32[128,1,128]{2,1,0:T(1,128)S(1)} async-done(((f32[128,1,128]{2,1,0:T(1,128)}), f32[128,1,128]{2,1,0:T(1,128)S(1)}, u32[]{:S(2)}, u32[]{:S(2)}) %all-to-all-start.16) | async-done | bytes 65568 | tf_op jit(solution)/shard_map/all_to_all | solution.py:297
  (48 shorter events, 43.0 us)
Async XLA Ops:
  19.4 6.4 %collective-permute-start = (f32[16,32,128]{2,1,0:T(8,128)S(1)}, f32[16,32,128]{2,1,0:T(8,128)S(1)}, u32[]{:S(2)}, u32[]{:S(2)}) collective-permute-start(f32[16,32,128]{2,1,0:T(8,128)S(1)} %all_to_all.85.own), channel_id=1, source_target_pairs={{0,8},{8,0},{1,9},{9,1},{2,10},{10,2},{3,11},{11,3},{4,12},{12,4},... | collective-permute-start | bytes 786440 | tf_op jit(solution)/shard_map/ppermute | solution.py:255
  21.7 0.7 copy-start.3
  22.3 3.4 %copy-start.1 = (s32[16,2]{0,1:T(2,128)S(1)}, s32[16,2]{0,1:T(2,128)}, u32[]{:S(2)}) copy-start(s32[16,2]{0,1:T(2,128)} %param.8) | copy-start | bytes 388
  25.7 14.2 %copy-start = (f32[256,16]{0,1:T(8,128)S(1)}, f32[256,16]{0,1:T(8,128)}, u32[]{:S(2)}) copy-start(f32[256,16]{0,1:T(8,128)} %param.5) | copy-start | bytes 49156
  25.8 14.2 %copy-start.2 = (f32[256]{0:T(256)S(1)}, f32[256]{0:T(256)}, u32[]{:S(2)}) copy-start(f32[256]{0:T(256)} %param.6) | copy-start | bytes 3076
  53.0 4.4 %collective-permute-start.1 = (f32[16,40,128]{2,1,0:T(8,128)S(1)}, f32[16,40,128]{2,1,0:T(8,128)S(1)}, u32[]{:S(2)}, u32[]{:S(2)}) collective-permute-start(f32[16,40,128]{2,1,0:T(8,128)S(1)} %all_to_all.87.own), channel_id=1, source_target_pairs={{0,8},{8,0},{1,9},{9,1},{2,10},{10,2},{3,11},{11,3},{4,12},{12,4},... | collective-permute-start | bytes 983048 | tf_op jit(solution)/shard_map/ppermute | solution.py:255
  82.3 5.4 %collective-permute-start.2 = (f32[16,40,128]{2,1,0:T(8,128)S(1)}, f32[16,40,128]{2,1,0:T(8,128)S(1)}, u32[]{:S(2)}, u32[]{:S(2)}) collective-permute-start(f32[16,40,128]{2,1,0:T(8,128)S(1)} %all_to_all.89.own), channel_id=1, source_target_pairs={{0,8},{8,0},{1,9},{9,1},{2,10},{10,2},{3,11},{11,3},{4,12},{12,4},... | collective-permute-start | bytes 983048 | tf_op jit(solution)/shard_map/ppermute | solution.py:255
  89.5 10.9 %all-to-all-start.5 = ((f32[8,40,128]{2,1,0:T(8,128)}), f32[8,40,128]{2,1,0:T(8,128)S(1)}, u32[]{:S(2)}, u32[]{:S(2)}) async-start(f32[8,40,128]{2,1,0:T(8,128)} %shard_map.60), calls=%async_computation.5 | async-start | bytes 327680 | tf_op jit(solution)/shard_map/all_to_all | solution.py:252
  113.1 5.4 %collective-permute-start.3 = (f32[16,40,128]{2,1,0:T(8,128)S(1)}, f32[16,40,128]{2,1,0:T(8,128)S(1)}, u32[]{:S(2)}, u32[]{:S(2)}) collective-permute-start(f32[16,40,128]{2,1,0:T(8,128)S(1)} %all_to_all.90.own), channel_id=1, source_target_pairs={{0,8},{8,0},{1,9},{9,1},{2,10},{10,2},{3,11},{11,3},{4,12},{12,4},... | collective-permute-start | bytes 983048 | tf_op jit(solution)/shard_map/ppermute | solution.py:255
  120.2 10.4 %all-to-all-start.7 = ((f32[8,40,128]{2,1,0:T(8,128)}), f32[8,40,128]{2,1,0:T(8,128)S(1)}, u32[]{:S(2)}, u32[]{:S(2)}) async-start(f32[8,40,128]{2,1,0:T(8,128)} %shard_map.63), calls=%async_computation.7 | async-start | bytes 327680 | tf_op jit(solution)/shard_map/all_to_all | solution.py:252
  145.5 4.6 %collective-permute-start.4 = (f32[16,40,128]{2,1,0:T(8,128)S(1)}, f32[16,40,128]{2,1,0:T(8,128)S(1)}, u32[]{:S(2)}, u32[]{:S(2)}) collective-permute-start(f32[16,40,128]{2,1,0:T(8,128)S(1)} %all_to_all.91.own), channel_id=1, source_target_pairs={{0,8},{8,0},{1,9},{9,1},{2,10},{10,2},{3,11},{11,3},{4,12},{12,4},... | collective-permute-start | bytes 983048 | tf_op jit(solution)/shard_map/ppermute | solution.py:255
  151.8 11.1 %all-to-all-start.9 = ((f32[8,40,128]{2,1,0:T(8,128)}), f32[8,40,128]{2,1,0:T(8,128)S(1)}, u32[]{:S(2)}, u32[]{:S(2)}) async-start(f32[8,40,128]{2,1,0:T(8,128)} %shard_map.66), calls=%async_computation.9 | async-start | bytes 327680 | tf_op jit(solution)/shard_map/all_to_all | solution.py:252
  175.6 5.4 %collective-permute-start.5 = (f32[16,40,128]{2,1,0:T(8,128)S(1)}, f32[16,40,128]{2,1,0:T(8,128)S(1)}, u32[]{:S(2)}, u32[]{:S(2)}) collective-permute-start(f32[16,40,128]{2,1,0:T(8,128)S(1)} %all_to_all.92.own), channel_id=1, source_target_pairs={{0,8},{8,0},{1,9},{9,1},{2,10},{10,2},{3,11},{11,3},{4,12},{12,4},... | collective-permute-start | bytes 983048 | tf_op jit(solution)/shard_map/ppermute | solution.py:255
  182.8 10.4 %all-to-all-start.11 = ((f32[8,40,128]{2,1,0:T(8,128)}), f32[8,40,128]{2,1,0:T(8,128)S(1)}, u32[]{:S(2)}, u32[]{:S(2)}) async-start(f32[8,40,128]{2,1,0:T(8,128)} %shard_map.69), calls=%async_computation.11 | async-start | bytes 327680 | tf_op jit(solution)/shard_map/all_to_all | solution.py:252
  208.1 4.6 %collective-permute-start.6 = (f32[16,40,128]{2,1,0:T(8,128)S(1)}, f32[16,40,128]{2,1,0:T(8,128)S(1)}, u32[]{:S(2)}, u32[]{:S(2)}) collective-permute-start(f32[16,40,128]{2,1,0:T(8,128)S(1)} %all_to_all.93.own), channel_id=1, source_target_pairs={{0,8},{8,0},{1,9},{9,1},{2,10},{10,2},{3,11},{11,3},{4,12},{12,4},... | collective-permute-start | bytes 983048 | tf_op jit(solution)/shard_map/ppermute | solution.py:255
  214.4 11.1 %all-to-all-start.13 = ((f32[8,40,128]{2,1,0:T(8,128)}), f32[8,40,128]{2,1,0:T(8,128)S(1)}, u32[]{:S(2)}, u32[]{:S(2)}) async-start(f32[8,40,128]{2,1,0:T(8,128)} %shard_map.72), calls=%async_computation.13 | async-start | bytes 327680 | tf_op jit(solution)/shard_map/all_to_all | solution.py:252
  238.1 5.4 %collective-permute-start.7 = (f32[16,40,128]{2,1,0:T(8,128)S(1)}, f32[16,40,128]{2,1,0:T(8,128)S(1)}, u32[]{:S(2)}, u32[]{:S(2)}) collective-permute-start(f32[16,40,128]{2,1,0:T(8,128)S(1)} %all_to_all.94.own), channel_id=1, source_target_pairs={{0,8},{8,0},{1,9},{9,1},{2,10},{10,2},{3,11},{11,3},{4,12},{12,4},... | collective-permute-start | bytes 983048 | tf_op jit(solution)/shard_map/ppermute | solution.py:255
  245.3 10.4 %all-to-all-start.15 = ((f32[8,40,128]{2,1,0:T(8,128)}), f32[8,40,128]{2,1,0:T(8,128)S(1)}, u32[]{:S(2)}, u32[]{:S(2)}) async-start(f32[8,40,128]{2,1,0:T(8,128)} %shard_map.75), calls=%async_computation.15 | async-start | bytes 327680 | tf_op jit(solution)/shard_map/all_to_all | solution.py:252
  257.4 2.4 collective-permute-start.8
  260.5 17.7 %all-to-all-start.16 = ((f32[128,1,128]{2,1,0:T(1,128)}), f32[128,1,128]{2,1,0:T(1,128)S(1)}, u32[]{:S(2)}, u32[]{:S(2)}) async-start(f32[128,1,128]{2,1,0:T(1,128)} %shard_map.78), calls=%async_computation.16 | async-start | bytes 131072 | tf_op jit(solution)/shard_map/all_to_all | solution.py:297

commit v6 on v5

--- a/solution.py
+++ b/solution.py
@@ -14,6 +14,7 @@
 VMEM = pl.BlockSpec(memory_space=pltpu.VMEM)
 SMEM = pl.BlockSpec(memory_space=pltpu.SMEM)
 HBM = pl.BlockSpec(memory_space=pltpu.HBM)
+GROUP = 8
 TILE = 8
 
 
@@ -59,10 +60,20 @@
 def solve(matrix, right):
     joined = jnp.concatenate([matrix, right], axis=1)
     row = lax.broadcasted_iota(jnp.int32, joined.shape, 0)
-    for i in range(S):
-        column = jnp.broadcast_to(joined[:, i : i + 1], joined.shape)
-        pivot = joined[i : i + 1, :] / column[i : i + 1, :]
-        joined = jnp.where(row == i, pivot, joined - column * pivot)
+
+    def step(i, x, column):
+        pivot = x[i : i + 1, :] / column[i : i + 1, :]
+        return jnp.where(row == i, pivot, x - column * pivot)
+
+    for first in range(0, S, GROUP):
+        last = first + GROUP
+        columns = {
+            j: jnp.broadcast_to(joined[:, j : j + 1], joined.shape) for j in range(first, last)
+        }
+        for i in range(first, last):
+            joined = step(i, joined, columns[i])
+            for j in range(i + 1, last):
+                columns[j] = step(i, columns[j], columns[i])
     return joined[:, S:]
 
 
@@ -219,18 +230,10 @@
     sums[...] = jnp.where(lane == 0, entire(t * t), jnp.where(lane == 1, entire(t * q), 0.0))
 
 
-def last_rest_body(alpha, direction, x, x_out):
-    x_out[...] = x[...] + mix(direction[...], alpha[...])
-
-
-def join_body(mine, theirs, out):
-    out[...] = jnp.broadcast_to((mine[...] + theirs[...])[None], out.shape)
-
-
-def end_body(sums, x, q, out):
+def end_body(sums, alpha, direction, x, q, out):
     value = jnp.sum(sums[...], axis=0, keepdims=True)
     omega = value[0:1, 1:2] / value[0:1, 0:1]
-    out[...] = x[...] + omega * q[...]
+    out[...] = x[...] + mix(direction[...], alpha[...]) + omega * q[...]
 
 
 def per_device(rhs, diagonal, blocks, block_cols, counts):
@@ -243,16 +246,16 @@
     small = sds(S, S)
     message = sds(16, 2 * S + TILE, BS)
 
-    swap = [(0, 1), (1, 0)]
-
     def among(x):
         return lax.all_to_all(x, ("x", "z"), 0, 0, tiled=True)
 
     def across(x):
         return lax.all_to_all(x, "cols", 0, 0, tiled=True)
 
-    def product(own):
-        peer = lax.ppermute(own, "core", swap)
+    def exchange(own):
+        return lax.ppermute(own, "core", [(0, 1), (1, 0)])
+
+    def product(own, peer):
         out = call(
             product_body, sds(8, own.shape[1], BS), [VMEM, VMEM, VMEM, SMEM, SMEM],
             own, peer, packed, block_cols, core,
@@ -266,36 +269,38 @@
         prepare_body, sds(16, 2 * BS, 2 * BS, dtype=jnp.bfloat16), [HBM, SMEM],
         blocks, counts, scratch=held,
     )
-    parts = product(own)
+    parts = product(own, exchange(own))
     v, msg = call(first_body, (vec, message), [VMEM] * 3, parts, shadow, diag)
     f, r, p, x = v, shadow, shadow, ()
-    parts = product(among(msg))
+    own = among(msg)
+    parts = product(own, exchange(own))
     for _ in range(1, ITERS):
         z, q, t, alpha, matrix, msg = call(
             lead_body, (vec, vec, vec, small, small, message), [VMEM] * 6,
             parts, shadow, diag, v, f, r,
         )
         own = among(msg)
+        peer = exchange(own)
         inverse, x = call(lead_rest_body, (small, vec), [VMEM] * (3 + len(x)), matrix, alpha, p, *x)
-        parts = product(own)
+        parts = product(own, peer)
         image = v
         v, half, r, beta, omega, msg = call(
             follow_body, (vec, vec, vec, small, sds(1, BS), message), [VMEM] * 8,
             parts, shadow, diag, image, z, q, t, inverse,
         )
         own = among(msg)
+        peer = exchange(own)
         f, p, x = call(
             follow_rest_body, (vec, vec, vec), [VMEM] * 9,
             t, half, r, beta, omega, image, p, q, x,
         )
-        parts = product(own)
+        parts = product(own, peer)
         x = (x,)
     q, alpha, sums = call(last_body, (vec, small, sds(1, BS)), [VMEM] * 5, parts, diag, v, f, r)
-    theirs = lax.ppermute(sums, "core", swap)
-    x = call(last_rest_body, vec, [VMEM] * 3, alpha, p, *x)
-    sums = call(join_body, sds(128, 1, BS), [VMEM] * 2, sums, theirs)
-    sums = lax.all_to_all(sums, ("x", "z", "cols"), 0, 0, tiled=True)
-    out = call(end_body, vec, [VMEM] * 3, sums.reshape(128, BS), x, q)
+    everyone = 2 * 16 * 8
+    sums = jnp.broadcast_to(sums[None], (everyone, 1, BS))
+    sums = lax.all_to_all(sums, ("x", "z", "core", "cols"), 0, 0, tiled=True)
+    out = call(end_body, vec, [VMEM] * 5, sums.reshape(everyone, BS), alpha, p, x[0], q)
     return out.T
 
 

time: 280 us -> 276 us (0.986)
  blocking collectives: 129 us -> 149 us
  starting transfers between devices: 59.6 us -> 50.7 us
  waiting for transfers between devices: 57.5 us -> 49.3 us
  Pallas kernels: 30.9 us -> 23.5 us
    all_to_all x0 -> x1, blocking collectives: none -> 20.1 us  [per_device(): sums = lax.all_to_all(sums, ('x', 'z', 'core', 'cols'), 0, 0, tiled=True)]
    all_to_all x1 -> x0, waiting for transfers between devices: 10.2 us -> none  [per_device(): sums = lax.all_to_all(sums, ('x', 'z', 'cols'), 0, 0, tiled=True)]
    pallas_call x26 -> x24, Pallas kernels: 30.9 us -> 23.5 us  [call(): pl.pallas_call(body, out_shape=outs, in_specs=specs, out_specs=tuple((VME...]
    all_to_all x1 -> x0, starting transfers between devices: 7.28 us -> none  [per_device(): sums = lax.all_to_all(sums, ('x', 'z', 'cols'), 0, 0, tiled=True)]
    all_to_all x6, waiting for transfers between devices: 37.7 us -> 40.5 us  [across(): return lax.all_to_all(x, 'cols', 0, 0, tiled=True)]
    ppermute x9 -> x8, starting transfers between devices: 30.4 us -> 28.8 us  [exchange(): return lax.ppermute(own, 'core', [(0, 1), (1, 0)])]
    ppermute x9 -> x8, waiting for transfers between devices: 9.61 us -> 8.79 us  [exchange(): return lax.ppermute(own, 'core', [(0, 1), (1, 0)])]
  transfers between devices with their start and end apart: 16 -> 14, of which waited for: 15 -> 13; matrix products, arithmetic and copies ran while one was open for 0% -> 0% of each run, Pallas kernels for 3% -> 2%
where the time goes in v6:
time: 276 us; the launch traced here: 275 us
  blocking collectives  149 us (54%)
  starting transfers between devices  50.7 us (18%)
  waiting for transfers between devices  49.3 us (18%)
  Pallas kernels  23.5 us (9%)
    all_to_all x8, blocking collectives, among(): return lax.all_to_all(x, ('x', 'z'), 0, 0, tiled=True)  106 us
    all_to_all x6, waiting for transfers between devices, across(): return lax.all_to_all(x, 'cols', 0, 0, tiled=True)  40.5 us
    ppermute x8, starting transfers between devices, exchange(): return lax.ppermute(own, 'core', [(0, 1), (1, 0)])  28.8 us
    pallas_call x24, Pallas kernels, call(): pl.pallas_call(body, out_shape=outs, in_specs=specs, out_specs=tuple((VME...  23.5 us
    all_to_all x2, blocking collectives, across(): return lax.all_to_all(x, 'cols', 0, 0, tiled=True)  23.1 us
    all_to_all x6, starting transfers between devices, across(): return lax.all_to_all(x, 'cols', 0, 0, tiled=True)  21.9 us
    all_to_all x1, blocking collectives, per_device(): sums = lax.all_to_all(sums, ('x', 'z', 'core', 'cols'), 0, 0, tiled=True)  20.1 us
    ppermute x8, waiting for transfers between devices, exchange(): return lax.ppermute(own, 'core', [(0, 1), (1, 0)])  8.79 us
  transfers between devices with their start and end apart: 14, of which 13 were waited for; matrix products, arithmetic and copies ran while one was open for 0% of the time, Pallas kernels for 2%

profile of v6, /device:TPU:1, one launch (start us, length us, event | category | flops | bytes accessed | tf_op | source)
XLA Modules:
  0.0 274.6 jit_solution(4191641122537319900)
XLA Ops:
  0.8 18.6 %all_to_all.85.own = f32[16,32,128]{2,1,0:T(8,128)S(1)} all-to-all(f32[16,32,128]{2,1,0:T(8,128)S(1)} %broadcast_in_dim.6), channel_id=1, replica_groups=mesh['x'=2,'z'=8,'core'=2,'cols'=8] {'x','z'}, dimensions={0} | all-to-all | bytes 524288 | tf_op jit(solution)/shard_map/all_to_all | solution.py:250
  19.4 2.3 collective-permute-start
  22.3 3.4 %shard_map.55.packed = bf16[16,256,256]{2,1,0:T(8,128)(2,1)S(1)} custom-call(f32[16,2,128,128]{3,2,1,0:T(8,128)} %source.1, s32[1,16]{1,0:T(1,128)S(1)} %bitcast.37), custom_call_target="tpu_custom_call" | custom-call | tf_op jit(solution)/shard_map/pallas_call | solution.py:30
  26.9 13.1 %all_to_all.86.parts = f32[8,32,128]{2,1,0:T(8,128)S(1)} all-to-all(f32[8,32,128]{2,1,0:T(8,128)S(1)} %shard_map.56), channel_id=1, replica_groups=mesh['x'=2,'z'=8,'core'=2,'cols'=8] {'cols'}, dimensions={0} | all-to-all | bytes 262144 | tf_op jit(solution)/shard_map/all_to_all | solution.py:253
  40.2 12.8 %all_to_all.87.own = f32[16,40,128]{2,1,0:T(8,128)S(1)} all-to-all(f32[16,40,128]{2,1,0:T(8,128)S(1)} %get-tuple-element.61), channel_id=1, replica_groups=mesh['x'=2,'z'=8,'core'=2,'cols'=8] {'x','z'}, dimensions={0} | all-to-all | bytes 655360 | tf_op jit(solution)/shard_map/all_to_all | solution.py:250
  53.0 3.2 %collective-permute-start.1 = (f32[16,40,128]{2,1,0:T(8,128)S(1)}, f32[16,40,128]{2,1,0:T(8,128)S(1)}, u32[]{:S(2)}, u32[]{:S(2)}) collective-permute-start(f32[16,40,128]{2,1,0:T(8,128)S(1)} %all_to_all.87.own), channel_id=1, source_target_pairs={{0,8},{8,0},{1,9},{9,1},{2,10},{10,2},{3,11},{11,3},{4,12},{12,4},... | collective-permute-start | bytes 983048 | tf_op jit(solution)/shard_map/ppermute | solution.py:256
  58.5 10.0 %all_to_all.88.parts = f32[8,40,128]{2,1,0:T(8,128)S(1)} all-to-all(f32[8,40,128]{2,1,0:T(8,128)S(1)} %shard_map.58), channel_id=1, replica_groups=mesh['x'=2,'z'=8,'core'=2,'cols'=8] {'cols'}, dimensions={0} | all-to-all | bytes 327680 | tf_op jit(solution)/shard_map/all_to_all | solution.py:253
  69.3 12.0 %all_to_all.89.own = f32[16,40,128]{2,1,0:T(8,128)S(1)} all-to-all(f32[16,40,128]{2,1,0:T(8,128)S(1)} %get-tuple-element.63), channel_id=1, replica_groups=mesh['x'=2,'z'=8,'core'=2,'cols'=8] {'x','z'}, dimensions={0} | all-to-all | bytes 655360 | tf_op jit(solution)/shard_map/all_to_all | solution.py:250
  81.4 4.2 %collective-permute-start.2 = (f32[16,40,128]{2,1,0:T(8,128)S(1)}, f32[16,40,128]{2,1,0:T(8,128)S(1)}, u32[]{:S(2)}, u32[]{:S(2)}) collective-permute-start(f32[16,40,128]{2,1,0:T(8,128)S(1)} %all_to_all.89.own), channel_id=1, source_target_pairs={{0,8},{8,0},{1,9},{9,1},{2,10},{10,2},{3,11},{11,3},{4,12},{12,4},... | collective-permute-start | bytes 983048 | tf_op jit(solution)/shard_map/ppermute | solution.py:256
  88.6 3.8 %all-to-all-start.5 = ((f32[8,40,128]{2,1,0:T(8,128)}), f32[8,40,128]{2,1,0:T(8,128)S(1)}, u32[]{:S(2)}, u32[]{:S(2)}) async-start(f32[8,40,128]{2,1,0:T(8,128)} %shard_map.60), calls=%async_computation.5 | async-start | bytes 327680 | tf_op jit(solution)/shard_map/all_to_all | solution.py:253
  92.8 6.7 %all-to-all-done.5.parts = f32[8,40,128]{2,1,0:T(8,128)S(1)} async-done(((f32[8,40,128]{2,1,0:T(8,128)}), f32[8,40,128]{2,1,0:T(8,128)S(1)}, u32[]{:S(2)}, u32[]{:S(2)}) %all-to-all-start.5) | async-done | bytes 163872 | tf_op jit(solution)/shard_map/all_to_all | solution.py:253
  100.1 12.0 %all_to_all.90.own = f32[16,40,128]{2,1,0:T(8,128)S(1)} all-to-all(f32[16,40,128]{2,1,0:T(8,128)S(1)} %get-tuple-element.70), channel_id=1, replica_groups=mesh['x'=2,'z'=8,'core'=2,'cols'=8] {'x','z'}, dimensions={0} | all-to-all | bytes 655360 | tf_op jit(solution)/shard_map/all_to_all | solution.py:250
  112.1 4.2 %collective-permute-start.3 = (f32[16,40,128]{2,1,0:T(8,128)S(1)}, f32[16,40,128]{2,1,0:T(8,128)S(1)}, u32[]{:S(2)}, u32[]{:S(2)}) collective-permute-start(f32[16,40,128]{2,1,0:T(8,128)S(1)} %all_to_all.90.own), channel_id=1, source_target_pairs={{0,8},{8,0},{1,9},{9,1},{2,10},{10,2},{3,11},{11,3},{4,12},{12,4},... | collective-permute-start | bytes 983048 | tf_op jit(solution)/shard_map/ppermute | solution.py:256
  119.3 3.4 %all-to-all-start.7 = ((f32[8,40,128]{2,1,0:T(8,128)}), f32[8,40,128]{2,1,0:T(8,128)S(1)}, u32[]{:S(2)}, u32[]{:S(2)}) async-start(f32[8,40,128]{2,1,0:T(8,128)} %shard_map.63), calls=%async_computation.7 | async-start | bytes 327680 | tf_op jit(solution)/shard_map/all_to_all | solution.py:253
  122.9 6.8 %all-to-all-done.7.parts = f32[8,40,128]{2,1,0:T(8,128)S(1)} async-done(((f32[8,40,128]{2,1,0:T(8,128)}), f32[8,40,128]{2,1,0:T(8,128)S(1)}, u32[]{:S(2)}, u32[]{:S(2)}) %all-to-all-start.7) | async-done | bytes 163872 | tf_op jit(solution)/shard_map/all_to_all | solution.py:253
  130.5 13.1 %all_to_all.91.own = f32[16,40,128]{2,1,0:T(8,128)S(1)} all-to-all(f32[16,40,128]{2,1,0:T(8,128)S(1)} %get-tuple-element.78), channel_id=1, replica_groups=mesh['x'=2,'z'=8,'core'=2,'cols'=8] {'x','z'}, dimensions={0} | all-to-all | bytes 655360 | tf_op jit(solution)/shard_map/all_to_all | solution.py:250
  143.7 3.3 %collective-permute-start.4 = (f32[16,40,128]{2,1,0:T(8,128)S(1)}, f32[16,40,128]{2,1,0:T(8,128)S(1)}, u32[]{:S(2)}, u32[]{:S(2)}) collective-permute-start(f32[16,40,128]{2,1,0:T(8,128)S(1)} %all_to_all.91.own), channel_id=1, source_target_pairs={{0,8},{8,0},{1,9},{9,1},{2,10},{10,2},{3,11},{11,3},{4,12},{12,4},... | collective-permute-start | bytes 983048 | tf_op jit(solution)/shard_map/ppermute | solution.py:256
  150.0 4.0 %all-to-all-start.9 = ((f32[8,40,128]{2,1,0:T(8,128)}), f32[8,40,128]{2,1,0:T(8,128)S(1)}, u32[]{:S(2)}, u32[]{:S(2)}) async-start(f32[8,40,128]{2,1,0:T(8,128)} %shard_map.66), calls=%async_computation.9 | async-start | bytes 327680 | tf_op jit(solution)/shard_map/all_to_all | solution.py:253
  154.4 6.7 %all-to-all-done.9.parts = f32[8,40,128]{2,1,0:T(8,128)S(1)} async-done(((f32[8,40,128]{2,1,0:T(8,128)}), f32[8,40,128]{2,1,0:T(8,128)S(1)}, u32[]{:S(2)}, u32[]{:S(2)}) %all-to-all-start.9) | async-done | bytes 163872 | tf_op jit(solution)/shard_map/all_to_all | solution.py:253
  161.7 12.0 %all_to_all.92.own = f32[16,40,128]{2,1,0:T(8,128)S(1)} all-to-all(f32[16,40,128]{2,1,0:T(8,128)S(1)} %get-tuple-element.87), channel_id=1, replica_groups=mesh['x'=2,'z'=8,'core'=2,'cols'=8] {'x','z'}, dimensions={0} | all-to-all | bytes 655360 | tf_op jit(solution)/shard_map/all_to_all | solution.py:250
  173.7 4.2 %collective-permute-start.5 = (f32[16,40,128]{2,1,0:T(8,128)S(1)}, f32[16,40,128]{2,1,0:T(8,128)S(1)}, u32[]{:S(2)}, u32[]{:S(2)}) collective-permute-start(f32[16,40,128]{2,1,0:T(8,128)S(1)} %all_to_all.92.own), channel_id=1, source_target_pairs={{0,8},{8,0},{1,9},{9,1},{2,10},{10,2},{3,11},{11,3},{4,12},{12,4},... | collective-permute-start | bytes 983048 | tf_op jit(solution)/shard_map/ppermute | solution.py:256
  180.9 3.4 %all-to-all-start.11 = ((f32[8,40,128]{2,1,0:T(8,128)}), f32[8,40,128]{2,1,0:T(8,128)S(1)}, u32[]{:S(2)}, u32[]{:S(2)}) async-start(f32[8,40,128]{2,1,0:T(8,128)} %shard_map.69), calls=%async_computation.11 | async-start | bytes 327680 | tf_op jit(solution)/shard_map/all_to_all | solution.py:253
  184.5 6.8 %all-to-all-done.11.parts = f32[8,40,128]{2,1,0:T(8,128)S(1)} async-done(((f32[8,40,128]{2,1,0:T(8,128)}), f32[8,40,128]{2,1,0:T(8,128)S(1)}, u32[]{:S(2)}, u32[]{:S(2)}) %all-to-all-start.11) | async-done | bytes 163872 | tf_op jit(solution)/shard_map/all_to_all | solution.py:253
  192.2 13.1 %all_to_all.93.own = f32[16,40,128]{2,1,0:T(8,128)S(1)} all-to-all(f32[16,40,128]{2,1,0:T(8,128)S(1)} %get-tuple-element.95), channel_id=1, replica_groups=mesh['x'=2,'z'=8,'core'=2,'cols'=8] {'x','z'}, dimensions={0} | all-to-all | bytes 655360 | tf_op jit(solution)/shard_map/all_to_all | solution.py:250
  205.3 3.3 %collective-permute-start.6 = (f32[16,40,128]{2,1,0:T(8,128)S(1)}, f32[16,40,128]{2,1,0:T(8,128)S(1)}, u32[]{:S(2)}, u32[]{:S(2)}) collective-permute-start(f32[16,40,128]{2,1,0:T(8,128)S(1)} %all_to_all.93.own), channel_id=1, source_target_pairs={{0,8},{8,0},{1,9},{9,1},{2,10},{10,2},{3,11},{11,3},{4,12},{12,4},... | collective-permute-start | bytes 983048 | tf_op jit(solution)/shard_map/ppermute | solution.py:256
  211.6 4.0 %all-to-all-start.13 = ((f32[8,40,128]{2,1,0:T(8,128)}), f32[8,40,128]{2,1,0:T(8,128)S(1)}, u32[]{:S(2)}, u32[]{:S(2)}) async-start(f32[8,40,128]{2,1,0:T(8,128)} %shard_map.72), calls=%async_computation.13 | async-start | bytes 327680 | tf_op jit(solution)/shard_map/all_to_all | solution.py:253
  216.0 6.7 %all-to-all-done.13.parts = f32[8,40,128]{2,1,0:T(8,128)S(1)} async-done(((f32[8,40,128]{2,1,0:T(8,128)}), f32[8,40,128]{2,1,0:T(8,128)S(1)}, u32[]{:S(2)}, u32[]{:S(2)}) %all-to-all-start.13) | async-done | bytes 163872 | tf_op jit(solution)/shard_map/all_to_all | solution.py:253
  223.3 12.0 %all_to_all.94.own = f32[16,40,128]{2,1,0:T(8,128)S(1)} all-to-all(f32[16,40,128]{2,1,0:T(8,128)S(1)} %get-tuple-element.104), channel_id=1, replica_groups=mesh['x'=2,'z'=8,'core'=2,'cols'=8] {'x','z'}, dimensions={0} | all-to-all | bytes 655360 | tf_op jit(solution)/shard_map/all_to_all | solution.py:250
  235.3 4.2 %collective-permute-start.7 = (f32[16,40,128]{2,1,0:T(8,128)S(1)}, f32[16,40,128]{2,1,0:T(8,128)S(1)}, u32[]{:S(2)}, u32[]{:S(2)}) collective-permute-start(f32[16,40,128]{2,1,0:T(8,128)S(1)} %all_to_all.94.own), channel_id=1, source_target_pairs={{0,8},{8,0},{1,9},{9,1},{2,10},{10,2},{3,11},{11,3},{4,12},{12,4},... | collective-permute-start | bytes 983048 | tf_op jit(solution)/shard_map/ppermute | solution.py:256
  242.5 3.4 %all-to-all-start.15 = ((f32[8,40,128]{2,1,0:T(8,128)}), f32[8,40,128]{2,1,0:T(8,128)S(1)}, u32[]{:S(2)}, u32[]{:S(2)}) async-start(f32[8,40,128]{2,1,0:T(8,128)} %shard_map.75), calls=%async_computation.15 | async-start | bytes 327680 | tf_op jit(solution)/shard_map/all_to_all | solution.py:253
  246.1 6.8 %all-to-all-done.15.parts = f32[8,40,128]{2,1,0:T(8,128)S(1)} async-done(((f32[8,40,128]{2,1,0:T(8,128)}), f32[8,40,128]{2,1,0:T(8,128)S(1)}, u32[]{:S(2)}, u32[]{:S(2)}) %all-to-all-start.15) | async-done | bytes 163872 | tf_op jit(solution)/shard_map/all_to_all | solution.py:253
  253.7 20.1 %all_to_all.95 = f32[256,1,128]{2,1,0:T(1,128)S(1)} all-to-all(f32[256,1,128]{2,1,0:T(1,128)S(1)} %broadcast_in_dim.16), channel_id=1, replica_groups=mesh['x'=2,'z'=8,'core'=2,'cols'=8] {'x','z','core','cols'}, dimensions={0} | all-to-all | bytes 262144 | tf_op jit(solution)/shard_map/all_to_all | solution.py:302
  (44 shorter events, 31.0 us)
Async XLA Ops:
  19.4 6.4 %collective-permute-start = (f32[16,32,128]{2,1,0:T(8,128)S(1)}, f32[16,32,128]{2,1,0:T(8,128)S(1)}, u32[]{:S(2)}, u32[]{:S(2)}) collective-permute-start(f32[16,32,128]{2,1,0:T(8,128)S(1)} %all_to_all.85.own), channel_id=1, source_target_pairs={{0,8},{8,0},{1,9},{9,1},{2,10},{10,2},{3,11},{11,3},{4,12},{12,4},... | collective-permute-start | bytes 786440 | tf_op jit(solution)/shard_map/ppermute | solution.py:256
  21.7 0.7 copy-start.3
  22.3 3.4 %copy-start.1 = (s32[16,2]{0,1:T(2,128)S(1)}, s32[16,2]{0,1:T(2,128)}, u32[]{:S(2)}) copy-start(s32[16,2]{0,1:T(2,128)} %param.8) | copy-start | bytes 388
  25.7 14.2 %copy-start = (f32[256,16]{0,1:T(8,128)S(1)}, f32[256,16]{0,1:T(8,128)}, u32[]{:S(2)}) copy-start(f32[256,16]{0,1:T(8,128)} %param.5) | copy-start | bytes 49156
  25.8 14.2 %copy-start.2 = (f32[256]{0:T(256)S(1)}, f32[256]{0:T(256)}, u32[]{:S(2)}) copy-start(f32[256]{0:T(256)} %param.6) | copy-start | bytes 3076
  53.0 4.4 %collective-permute-start.1 = (f32[16,40,128]{2,1,0:T(8,128)S(1)}, f32[16,40,128]{2,1,0:T(8,128)S(1)}, u32[]{:S(2)}, u32[]{:S(2)}) collective-permute-start(f32[16,40,128]{2,1,0:T(8,128)S(1)} %all_to_all.87.own), channel_id=1, source_target_pairs={{0,8},{8,0},{1,9},{9,1},{2,10},{10,2},{3,11},{11,3},{4,12},{12,4},... | collective-permute-start | bytes 983048 | tf_op jit(solution)/shard_map/ppermute | solution.py:256
  81.4 5.4 %collective-permute-start.2 = (f32[16,40,128]{2,1,0:T(8,128)S(1)}, f32[16,40,128]{2,1,0:T(8,128)S(1)}, u32[]{:S(2)}, u32[]{:S(2)}) collective-permute-start(f32[16,40,128]{2,1,0:T(8,128)S(1)} %all_to_all.89.own), channel_id=1, source_target_pairs={{0,8},{8,0},{1,9},{9,1},{2,10},{10,2},{3,11},{11,3},{4,12},{12,4},... | collective-permute-start | bytes 983048 | tf_op jit(solution)/shard_map/ppermute | solution.py:256
  88.6 10.9 %all-to-all-start.5 = ((f32[8,40,128]{2,1,0:T(8,128)}), f32[8,40,128]{2,1,0:T(8,128)S(1)}, u32[]{:S(2)}, u32[]{:S(2)}) async-start(f32[8,40,128]{2,1,0:T(8,128)} %shard_map.60), calls=%async_computation.5 | async-start | bytes 327680 | tf_op jit(solution)/shard_map/all_to_all | solution.py:253
  112.1 5.4 %collective-permute-start.3 = (f32[16,40,128]{2,1,0:T(8,128)S(1)}, f32[16,40,128]{2,1,0:T(8,128)S(1)}, u32[]{:S(2)}, u32[]{:S(2)}) collective-permute-start(f32[16,40,128]{2,1,0:T(8,128)S(1)} %all_to_all.90.own), channel_id=1, source_target_pairs={{0,8},{8,0},{1,9},{9,1},{2,10},{10,2},{3,11},{11,3},{4,12},{12,4},... | collective-permute-start | bytes 983048 | tf_op jit(solution)/shard_map/ppermute | solution.py:256
  119.3 10.4 %all-to-all-start.7 = ((f32[8,40,128]{2,1,0:T(8,128)}), f32[8,40,128]{2,1,0:T(8,128)S(1)}, u32[]{:S(2)}, u32[]{:S(2)}) async-start(f32[8,40,128]{2,1,0:T(8,128)} %shard_map.63), calls=%async_computation.7 | async-start | bytes 327680 | tf_op jit(solution)/shard_map/all_to_all | solution.py:253
  143.7 4.6 %collective-permute-start.4 = (f32[16,40,128]{2,1,0:T(8,128)S(1)}, f32[16,40,128]{2,1,0:T(8,128)S(1)}, u32[]{:S(2)}, u32[]{:S(2)}) collective-permute-start(f32[16,40,128]{2,1,0:T(8,128)S(1)} %all_to_all.91.own), channel_id=1, source_target_pairs={{0,8},{8,0},{1,9},{9,1},{2,10},{10,2},{3,11},{11,3},{4,12},{12,4},... | collective-permute-start | bytes 983048 | tf_op jit(solution)/shard_map/ppermute | solution.py:256
  150.0 11.1 %all-to-all-start.9 = ((f32[8,40,128]{2,1,0:T(8,128)}), f32[8,40,128]{2,1,0:T(8,128)S(1)}, u32[]{:S(2)}, u32[]{:S(2)}) async-start(f32[8,40,128]{2,1,0:T(8,128)} %shard_map.66), calls=%async_computation.9 | async-start | bytes 327680 | tf_op jit(solution)/shard_map/all_to_all | solution.py:253
  173.7 5.4 %collective-permute-start.5 = (f32[16,40,128]{2,1,0:T(8,128)S(1)}, f32[16,40,128]{2,1,0:T(8,128)S(1)}, u32[]{:S(2)}, u32[]{:S(2)}) collective-permute-start(f32[16,40,128]{2,1,0:T(8,128)S(1)} %all_to_all.92.own), channel_id=1, source_target_pairs={{0,8},{8,0},{1,9},{9,1},{2,10},{10,2},{3,11},{11,3},{4,12},{12,4},... | collective-permute-start | bytes 983048 | tf_op jit(solution)/shard_map/ppermute | solution.py:256
  180.9 10.4 %all-to-all-start.11 = ((f32[8,40,128]{2,1,0:T(8,128)}), f32[8,40,128]{2,1,0:T(8,128)S(1)}, u32[]{:S(2)}, u32[]{:S(2)}) async-start(f32[8,40,128]{2,1,0:T(8,128)} %shard_map.69), calls=%async_computation.11 | async-start | bytes 327680 | tf_op jit(solution)/shard_map/all_to_all | solution.py:253
  205.3 4.6 %collective-permute-start.6 = (f32[16,40,128]{2,1,0:T(8,128)S(1)}, f32[16,40,128]{2,1,0:T(8,128)S(1)}, u32[]{:S(2)}, u32[]{:S(2)}) collective-permute-start(f32[16,40,128]{2,1,0:T(8,128)S(1)} %all_to_all.93.own), channel_id=1, source_target_pairs={{0,8},{8,0},{1,9},{9,1},{2,10},{10,2},{3,11},{11,3},{4,12},{12,4},... | collective-permute-start | bytes 983048 | tf_op jit(solution)/shard_map/ppermute | solution.py:256
  211.6 11.1 %all-to-all-start.13 = ((f32[8,40,128]{2,1,0:T(8,128)}), f32[8,40,128]{2,1,0:T(8,128)S(1)}, u32[]{:S(2)}, u32[]{:S(2)}) async-start(f32[8,40,128]{2,1,0:T(8,128)} %shard_map.72), calls=%async_computation.13 | async-start | bytes 327680 | tf_op jit(solution)/shard_map/all_to_all | solution.py:253
  235.3 5.4 %collective-permute-start.7 = (f32[16,40,128]{2,1,0:T(8,128)S(1)}, f32[16,40,128]{2,1,0:T(8,128)S(1)}, u32[]{:S(2)}, u32[]{:S(2)}) collective-permute-start(f32[16,40,128]{2,1,0:T(8,128)S(1)} %all_to_all.94.own), channel_id=1, source_target_pairs={{0,8},{8,0},{1,9},{9,1},{2,10},{10,2},{3,11},{11,3},{4,12},{12,4},... | collective-permute-start | bytes 983048 | tf_op jit(solution)/shard_map/ppermute | solution.py:256
  242.5 10.4 %all-to-all-start.15 = ((f32[8,40,128]{2,1,0:T(8,128)}), f32[8,40,128]{2,1,0:T(8,128)S(1)}, u32[]{:S(2)}, u32[]{:S(2)}) async-start(f32[8,40,128]{2,1,0:T(8,128)} %shard_map.75), calls=%async_computation.15 | async-start | bytes 327680 | tf_op jit(solution)/shard_map/all_to_all | solution.py:253

commit v7 on v6

--- a/solution.py
+++ b/solution.py
@@ -135,11 +135,11 @@
         picked = []
         for k in range(2):
             col = cols[k, i]
-            m = col // 4
-            b = pl.multiple_of((col % 2) * S, S)
+            m = col >> 2
+            b = pl.multiple_of((col & 1) * S, S)
             here = own[m, pl.ds(b, S), :]
             there = peer[m, pl.ds(b, S), :]
-            picked.append(jnp.where((col // 2) % 2 == me, here, there))
+            picked.append(jnp.where((col >> 1) & 1 == me, here, there))
         high, low = halves(jnp.concatenate(picked, axis=1))
         result = bdot(jnp.concatenate([high, low], axis=0), packed[i])
         result = (result[:S, :BS] + result[:S, BS:]) + (result[S:, :BS] + result[S:, BS:])
@@ -151,6 +151,13 @@
             tile2 = tile2 + peer[m, 2 * S :]
         for c in range(8):
             out[c, 2 * S :] = tile + tile2
+
+
+def start_body(shadow, message):
+    value = shadow[...]
+    for k in range(message.shape[0]):
+        message[k, 0:S] = value[:, :BS]
+        message[k, S:] = value[:, BS:]
 
 
 def first_body(parts, shadow, diag, image, message):
@@ -263,8 +270,8 @@
         return across(out)
 
     held = [pltpu.VMEM((16, 2, BS, BS), F32), pltpu.SemaphoreType.DMA((16,))]
-    piece = jnp.concatenate([shadow[:, :BS], shadow[:, BS:]], axis=0)
-    own = among(jnp.broadcast_to(piece[None], (16, 2 * S, BS)))
+    msg = call(start_body, jax.ShapeDtypeStruct((16, 2 * S, BS), F32), [VMEM], shadow)
+    own = among(msg)
     packed = call(
         prepare_body, sds(16, 2 * BS, 2 * BS, dtype=jnp.bfloat16), [HBM, SMEM],
         blocks, counts, scratch=held,
@@ -300,7 +307,9 @@
     everyone = 2 * 16 * 8
     sums = jnp.broadcast_to(sums[None], (everyone, 1, BS))
     sums = lax.all_to_all(sums, ("x", "z", "core", "cols"), 0, 0, tiled=True)
-    out = call(end_body, vec, [VMEM] * 5, sums.reshape(everyone, BS), alpha, p, x[0], q)
+    out = call(
+        end_body, jax.ShapeDtypeStruct((S, 2 * BS), F32), [VMEM] * 5, sums.reshape(everyone, BS), alpha, p, x[0], q
+    )
     return out.T
 
 

time: 276 us -> 275 us (level)
    pallas_call x24 -> x25, Pallas kernels: 23.5 us -> 23.7 us  [call(): pl.pallas_call(body, out_shape=outs, in_specs=specs, out_specs=tuple((VME...]
where the time goes in v7:
time: 275 us; the launch traced here: 274 us
  blocking collectives  149 us (54%)
  starting transfers between devices  50.7 us (18%)
  waiting for transfers between devices  49.3 us (18%)
  Pallas kernels  23.7 us (9%)
    all_to_all x8, blocking collectives, among(): return lax.all_to_all(x, ('x', 'z'), 0, 0, tiled=True)  106 us
    all_to_all x6, waiting for transfers between devices, across(): return lax.all_to_all(x, 'cols', 0, 0, tiled=True)  40.5 us
    ppermute x8, starting transfers between devices, exchange(): return lax.ppermute(own, 'core', [(0, 1), (1, 0)])  28.8 us
    pallas_call x25, Pallas kernels, call(): pl.pallas_call(body, out_shape=outs, in_specs=specs, out_specs=tuple((VME...  23.7 us
    all_to_all x2, blocking collectives, across(): return lax.all_to_all(x, 'cols', 0, 0, tiled=True)  23.1 us
    all_to_all x6, starting transfers between devices, across(): return lax.all_to_all(x, 'cols', 0, 0, tiled=True)  21.9 us
    all_to_all x1, blocking collectives, per_device(): sums = lax.all_to_all(sums, ('x', 'z', 'core', 'cols'), 0, 0, tiled=True)  20.1 us
    ppermute x8, waiting for transfers between devices, exchange(): return lax.ppermute(own, 'core', [(0, 1), (1, 0)])  8.79 us
  transfers between devices with their start and end apart: 14, of which 13 were waited for; matrix products, arithmetic and copies ran while one was open for 0% of the time, Pallas kernels for 2%

profile of v7, /device:TPU:1, one launch (start us, length us, event | category | flops | bytes accessed | tf_op | source)
XLA Modules:
  0.0 274.2 jit_solution(7751483774424834263)
XLA Ops:
  0.7 18.6 %all_to_all.85.own = f32[16,32,128]{2,1,0:T(8,128)S(1)} all-to-all(f32[16,32,128]{2,1,0:T(8,128)S(1)} %shard_map.55), channel_id=1, replica_groups=mesh['x'=2,'z'=8,'core'=2,'cols'=8] {'x','z'}, dimensions={0} | all-to-all | bytes 524288 | tf_op jit(solution)/shard_map/all_to_all | solution.py:257
  19.4 2.3 collective-permute-start
  22.3 3.4 %shard_map.56.packed = bf16[16,256,256]{2,1,0:T(8,128)(2,1)S(1)} custom-call(f32[16,2,128,128]{3,2,1,0:T(8,128)} %source.1, s32[1,16]{1,0:T(1,128)S(1)} %bitcast.36), custom_call_target="tpu_custom_call" | custom-call | tf_op jit(solution)/shard_map/pallas_call | solution.py:30
  26.8 13.1 %all_to_all.86.parts = f32[8,32,128]{2,1,0:T(8,128)S(1)} all-to-all(f32[8,32,128]{2,1,0:T(8,128)S(1)} %shard_map.57), channel_id=1, replica_groups=mesh['x'=2,'z'=8,'core'=2,'cols'=8] {'cols'}, dimensions={0} | all-to-all | bytes 262144 | tf_op jit(solution)/shard_map/all_to_all | solution.py:260
  40.1 12.8 %all_to_all.87.own = f32[16,40,128]{2,1,0:T(8,128)S(1)} all-to-all(f32[16,40,128]{2,1,0:T(8,128)S(1)} %get-tuple-element.61), channel_id=1, replica_groups=mesh['x'=2,'z'=8,'core'=2,'cols'=8] {'x','z'}, dimensions={0} | all-to-all | bytes 655360 | tf_op jit(solution)/shard_map/all_to_all | solution.py:257
  52.9 3.2 %collective-permute-start.1 = (f32[16,40,128]{2,1,0:T(8,128)S(1)}, f32[16,40,128]{2,1,0:T(8,128)S(1)}, u32[]{:S(2)}, u32[]{:S(2)}) collective-permute-start(f32[16,40,128]{2,1,0:T(8,128)S(1)} %all_to_all.87.own), channel_id=1, source_target_pairs={{0,8},{8,0},{1,9},{9,1},{2,10},{10,2},{3,11},{11,3},{4,12},{12,4},... | collective-permute-start | bytes 983048 | tf_op jit(solution)/shard_map/ppermute | solution.py:263
  58.4 10.0 %all_to_all.88.parts = f32[8,40,128]{2,1,0:T(8,128)S(1)} all-to-all(f32[8,40,128]{2,1,0:T(8,128)S(1)} %shard_map.59), channel_id=1, replica_groups=mesh['x'=2,'z'=8,'core'=2,'cols'=8] {'cols'}, dimensions={0} | all-to-all | bytes 327680 | tf_op jit(solution)/shard_map/all_to_all | solution.py:260
  69.2 12.0 %all_to_all.89.own = f32[16,40,128]{2,1,0:T(8,128)S(1)} all-to-all(f32[16,40,128]{2,1,0:T(8,128)S(1)} %get-tuple-element.63), channel_id=1, replica_groups=mesh['x'=2,'z'=8,'core'=2,'cols'=8] {'x','z'}, dimensions={0} | all-to-all | bytes 655360 | tf_op jit(solution)/shard_map/all_to_all | solution.py:257
  81.2 4.2 %collective-permute-start.2 = (f32[16,40,128]{2,1,0:T(8,128)S(1)}, f32[16,40,128]{2,1,0:T(8,128)S(1)}, u32[]{:S(2)}, u32[]{:S(2)}) collective-permute-start(f32[16,40,128]{2,1,0:T(8,128)S(1)} %all_to_all.89.own), channel_id=1, source_target_pairs={{0,8},{8,0},{1,9},{9,1},{2,10},{10,2},{3,11},{11,3},{4,12},{12,4},... | collective-permute-start | bytes 983048 | tf_op jit(solution)/shard_map/ppermute | solution.py:263
  88.4 3.8 %all-to-all-start.5 = ((f32[8,40,128]{2,1,0:T(8,128)}), f32[8,40,128]{2,1,0:T(8,128)S(1)}, u32[]{:S(2)}, u32[]{:S(2)}) async-start(f32[8,40,128]{2,1,0:T(8,128)} %shard_map.61), calls=%async_computation.5 | async-start | bytes 327680 | tf_op jit(solution)/shard_map/all_to_all | solution.py:260
  92.6 6.7 %all-to-all-done.5.parts = f32[8,40,128]{2,1,0:T(8,128)S(1)} async-done(((f32[8,40,128]{2,1,0:T(8,128)}), f32[8,40,128]{2,1,0:T(8,128)S(1)}, u32[]{:S(2)}, u32[]{:S(2)}) %all-to-all-start.5) | async-done | bytes 163872 | tf_op jit(solution)/shard_map/all_to_all | solution.py:260
  99.9 12.0 %all_to_all.90.own = f32[16,40,128]{2,1,0:T(8,128)S(1)} all-to-all(f32[16,40,128]{2,1,0:T(8,128)S(1)} %get-tuple-element.70), channel_id=1, replica_groups=mesh['x'=2,'z'=8,'core'=2,'cols'=8] {'x','z'}, dimensions={0} | all-to-all | bytes 655360 | tf_op jit(solution)/shard_map/all_to_all | solution.py:257
  111.9 4.2 %collective-permute-start.3 = (f32[16,40,128]{2,1,0:T(8,128)S(1)}, f32[16,40,128]{2,1,0:T(8,128)S(1)}, u32[]{:S(2)}, u32[]{:S(2)}) collective-permute-start(f32[16,40,128]{2,1,0:T(8,128)S(1)} %all_to_all.90.own), channel_id=1, source_target_pairs={{0,8},{8,0},{1,9},{9,1},{2,10},{10,2},{3,11},{11,3},{4,12},{12,4},... | collective-permute-start | bytes 983048 | tf_op jit(solution)/shard_map/ppermute | solution.py:263
  119.1 3.4 %all-to-all-start.7 = ((f32[8,40,128]{2,1,0:T(8,128)}), f32[8,40,128]{2,1,0:T(8,128)S(1)}, u32[]{:S(2)}, u32[]{:S(2)}) async-start(f32[8,40,128]{2,1,0:T(8,128)} %shard_map.64), calls=%async_computation.7 | async-start | bytes 327680 | tf_op jit(solution)/shard_map/all_to_all | solution.py:260
  122.7 6.8 %all-to-all-done.7.parts = f32[8,40,128]{2,1,0:T(8,128)S(1)} async-done(((f32[8,40,128]{2,1,0:T(8,128)}), f32[8,40,128]{2,1,0:T(8,128)S(1)}, u32[]{:S(2)}, u32[]{:S(2)}) %all-to-all-start.7) | async-done | bytes 163872 | tf_op jit(solution)/shard_map/all_to_all | solution.py:260
  130.3 13.1 %all_to_all.91.own = f32[16,40,128]{2,1,0:T(8,128)S(1)} all-to-all(f32[16,40,128]{2,1,0:T(8,128)S(1)} %get-tuple-element.78), channel_id=1, replica_groups=mesh['x'=2,'z'=8,'core'=2,'cols'=8] {'x','z'}, dimensions={0} | all-to-all | bytes 655360 | tf_op jit(solution)/shard_map/all_to_all | solution.py:257
  143.4 3.3 %collective-permute-start.4 = (f32[16,40,128]{2,1,0:T(8,128)S(1)}, f32[16,40,128]{2,1,0:T(8,128)S(1)}, u32[]{:S(2)}, u32[]{:S(2)}) collective-permute-start(f32[16,40,128]{2,1,0:T(8,128)S(1)} %all_to_all.91.own), channel_id=1, source_target_pairs={{0,8},{8,0},{1,9},{9,1},{2,10},{10,2},{3,11},{11,3},{4,12},{12,4},... | collective-permute-start | bytes 983048 | tf_op jit(solution)/shard_map/ppermute | solution.py:263
  149.7 4.0 %all-to-all-start.9 = ((f32[8,40,128]{2,1,0:T(8,128)}), f32[8,40,128]{2,1,0:T(8,128)S(1)}, u32[]{:S(2)}, u32[]{:S(2)}) async-start(f32[8,40,128]{2,1,0:T(8,128)} %shard_map.67), calls=%async_computation.9 | async-start | bytes 327680 | tf_op jit(solution)/shard_map/all_to_all | solution.py:260
  154.1 6.7 %all-to-all-done.9.parts = f32[8,40,128]{2,1,0:T(8,128)S(1)} async-done(((f32[8,40,128]{2,1,0:T(8,128)}), f32[8,40,128]{2,1,0:T(8,128)S(1)}, u32[]{:S(2)}, u32[]{:S(2)}) %all-to-all-start.9) | async-done | bytes 163872 | tf_op jit(solution)/shard_map/all_to_all | solution.py:260
  161.4 12.0 %all_to_all.92.own = f32[16,40,128]{2,1,0:T(8,128)S(1)} all-to-all(f32[16,40,128]{2,1,0:T(8,128)S(1)} %get-tuple-element.87), channel_id=1, replica_groups=mesh['x'=2,'z'=8,'core'=2,'cols'=8] {'x','z'}, dimensions={0} | all-to-all | bytes 655360 | tf_op jit(solution)/shard_map/all_to_all | solution.py:257
  173.4 4.2 %collective-permute-start.5 = (f32[16,40,128]{2,1,0:T(8,128)S(1)}, f32[16,40,128]{2,1,0:T(8,128)S(1)}, u32[]{:S(2)}, u32[]{:S(2)}) collective-permute-start(f32[16,40,128]{2,1,0:T(8,128)S(1)} %all_to_all.92.own), channel_id=1, source_target_pairs={{0,8},{8,0},{1,9},{9,1},{2,10},{10,2},{3,11},{11,3},{4,12},{12,4},... | collective-permute-start | bytes 983048 | tf_op jit(solution)/shard_map/ppermute | solution.py:263
  180.6 3.4 %all-to-all-start.11 = ((f32[8,40,128]{2,1,0:T(8,128)}), f32[8,40,128]{2,1,0:T(8,128)S(1)}, u32[]{:S(2)}, u32[]{:S(2)}) async-start(f32[8,40,128]{2,1,0:T(8,128)} %shard_map.70), calls=%async_computation.11 | async-start | bytes 327680 | tf_op jit(solution)/shard_map/all_to_all | solution.py:260
  184.2 6.8 %all-to-all-done.11.parts = f32[8,40,128]{2,1,0:T(8,128)S(1)} async-done(((f32[8,40,128]{2,1,0:T(8,128)}), f32[8,40,128]{2,1,0:T(8,128)S(1)}, u32[]{:S(2)}, u32[]{:S(2)}) %all-to-all-start.11) | async-done | bytes 163872 | tf_op jit(solution)/shard_map/all_to_all | solution.py:260
  191.8 13.1 %all_to_all.93.own = f32[16,40,128]{2,1,0:T(8,128)S(1)} all-to-all(f32[16,40,128]{2,1,0:T(8,128)S(1)} %get-tuple-element.95), channel_id=1, replica_groups=mesh['x'=2,'z'=8,'core'=2,'cols'=8] {'x','z'}, dimensions={0} | all-to-all | bytes 655360 | tf_op jit(solution)/shard_map/all_to_all | solution.py:257
  204.9 3.3 %collective-permute-start.6 = (f32[16,40,128]{2,1,0:T(8,128)S(1)}, f32[16,40,128]{2,1,0:T(8,128)S(1)}, u32[]{:S(2)}, u32[]{:S(2)}) collective-permute-start(f32[16,40,128]{2,1,0:T(8,128)S(1)} %all_to_all.93.own), channel_id=1, source_target_pairs={{0,8},{8,0},{1,9},{9,1},{2,10},{10,2},{3,11},{11,3},{4,12},{12,4},... | collective-permute-start | bytes 983048 | tf_op jit(solution)/shard_map/ppermute | solution.py:263
  211.2 4.0 %all-to-all-start.13 = ((f32[8,40,128]{2,1,0:T(8,128)}), f32[8,40,128]{2,1,0:T(8,128)S(1)}, u32[]{:S(2)}, u32[]{:S(2)}) async-start(f32[8,40,128]{2,1,0:T(8,128)} %shard_map.73), calls=%async_computation.13 | async-start | bytes 327680 | tf_op jit(solution)/shard_map/all_to_all | solution.py:260
  215.6 6.7 %all-to-all-done.13.parts = f32[8,40,128]{2,1,0:T(8,128)S(1)} async-done(((f32[8,40,128]{2,1,0:T(8,128)}), f32[8,40,128]{2,1,0:T(8,128)S(1)}, u32[]{:S(2)}, u32[]{:S(2)}) %all-to-all-start.13) | async-done | bytes 163872 | tf_op jit(solution)/shard_map/all_to_all | solution.py:260
  222.9 12.0 %all_to_all.94.own = f32[16,40,128]{2,1,0:T(8,128)S(1)} all-to-all(f32[16,40,128]{2,1,0:T(8,128)S(1)} %get-tuple-element.104), channel_id=1, replica_groups=mesh['x'=2,'z'=8,'core'=2,'cols'=8] {'x','z'}, dimensions={0} | all-to-all | bytes 655360 | tf_op jit(solution)/shard_map/all_to_all | solution.py:257
  234.9 4.2 %collective-permute-start.7 = (f32[16,40,128]{2,1,0:T(8,128)S(1)}, f32[16,40,128]{2,1,0:T(8,128)S(1)}, u32[]{:S(2)}, u32[]{:S(2)}) collective-permute-start(f32[16,40,128]{2,1,0:T(8,128)S(1)} %all_to_all.94.own), channel_id=1, source_target_pairs={{0,8},{8,0},{1,9},{9,1},{2,10},{10,2},{3,11},{11,3},{4,12},{12,4},... | collective-permute-start | bytes 983048 | tf_op jit(solution)/shard_map/ppermute | solution.py:263
  242.1 3.4 %all-to-all-start.15 = ((f32[8,40,128]{2,1,0:T(8,128)}), f32[8,40,128]{2,1,0:T(8,128)S(1)}, u32[]{:S(2)}, u32[]{:S(2)}) async-start(f32[8,40,128]{2,1,0:T(8,128)} %shard_map.76), calls=%async_computation.15 | async-start | bytes 327680 | tf_op jit(solution)/shard_map/all_to_all | solution.py:260
  245.7 6.8 %all-to-all-done.15.parts = f32[8,40,128]{2,1,0:T(8,128)S(1)} async-done(((f32[8,40,128]{2,1,0:T(8,128)}), f32[8,40,128]{2,1,0:T(8,128)S(1)}, u32[]{:S(2)}, u32[]{:S(2)}) %all-to-all-start.15) | async-done | bytes 163872 | tf_op jit(solution)/shard_map/all_to_all | solution.py:260
  253.3 20.1 %all_to_all.95 = f32[256,1,128]{2,1,0:T(1,128)S(1)} all-to-all(f32[256,1,128]{2,1,0:T(1,128)S(1)} %broadcast_in_dim.9), channel_id=1, replica_groups=mesh['x'=2,'z'=8,'core'=2,'cols'=8] {'x','z','core','cols'}, dimensions={0} | all-to-all | bytes 262144 | tf_op jit(solution)/shard_map/all_to_all | solution.py:309
  (43 shorter events, 30.6 us)
Async XLA Ops:
  0.0 0.7 copy-start
  19.4 6.4 %collective-permute-start = (f32[16,32,128]{2,1,0:T(8,128)S(1)}, f32[16,32,128]{2,1,0:T(8,128)S(1)}, u32[]{:S(2)}, u32[]{:S(2)}) collective-permute-start(f32[16,32,128]{2,1,0:T(8,128)S(1)} %all_to_all.85.own), channel_id=1, source_target_pairs={{0,8},{8,0},{1,9},{9,1},{2,10},{10,2},{3,11},{11,3},{4,12},{12,4},... | collective-permute-start | bytes 786440 | tf_op jit(solution)/shard_map/ppermute | solution.py:263
  21.7 0.7 copy-start.4
  22.3 3.4 %copy-start.2 = (s32[16,2]{0,1:T(2,128)S(1)}, s32[16,2]{0,1:T(2,128)}, u32[]{:S(2)}) copy-start(s32[16,2]{0,1:T(2,128)} %param.8) | copy-start | bytes 388
  25.7 14.2 %copy-start.1 = (f32[256,16]{0,1:T(8,128)S(1)}, f32[256,16]{0,1:T(8,128)}, u32[]{:S(2)}) copy-start(f32[256,16]{0,1:T(8,128)} %param.5) | copy-start | bytes 49156
  25.7 14.1 %copy-start.3 = (f32[256]{0:T(256)S(1)}, f32[256]{0:T(256)}, u32[]{:S(2)}) copy-start(f32[256]{0:T(256)} %param.6) | copy-start | bytes 3076
  52.9 4.4 %collective-permute-start.1 = (f32[16,40,128]{2,1,0:T(8,128)S(1)}, f32[16,40,128]{2,1,0:T(8,128)S(1)}, u32[]{:S(2)}, u32[]{:S(2)}) collective-permute-start(f32[16,40,128]{2,1,0:T(8,128)S(1)} %all_to_all.87.own), channel_id=1, source_target_pairs={{0,8},{8,0},{1,9},{9,1},{2,10},{10,2},{3,11},{11,3},{4,12},{12,4},... | collective-permute-start | bytes 983048 | tf_op jit(solution)/shard_map/ppermute | solution.py:263
  81.2 5.4 %collective-permute-start.2 = (f32[16,40,128]{2,1,0:T(8,128)S(1)}, f32[16,40,128]{2,1,0:T(8,128)S(1)}, u32[]{:S(2)}, u32[]{:S(2)}) collective-permute-start(f32[16,40,128]{2,1,0:T(8,128)S(1)} %all_to_all.89.own), channel_id=1, source_target_pairs={{0,8},{8,0},{1,9},{9,1},{2,10},{10,2},{3,11},{11,3},{4,12},{12,4},... | collective-permute-start | bytes 983048 | tf_op jit(solution)/shard_map/ppermute | solution.py:263
  88.4 10.9 %all-to-all-start.5 = ((f32[8,40,128]{2,1,0:T(8,128)}), f32[8,40,128]{2,1,0:T(8,128)S(1)}, u32[]{:S(2)}, u32[]{:S(2)}) async-start(f32[8,40,128]{2,1,0:T(8,128)} %shard_map.61), calls=%async_computation.5 | async-start | bytes 327680 | tf_op jit(solution)/shard_map/all_to_all | solution.py:260
  111.9 5.4 %collective-permute-start.3 = (f32[16,40,128]{2,1,0:T(8,128)S(1)}, f32[16,40,128]{2,1,0:T(8,128)S(1)}, u32[]{:S(2)}, u32[]{:S(2)}) collective-permute-start(f32[16,40,128]{2,1,0:T(8,128)S(1)} %all_to_all.90.own), channel_id=1, source_target_pairs={{0,8},{8,0},{1,9},{9,1},{2,10},{10,2},{3,11},{11,3},{4,12},{12,4},... | collective-permute-start | bytes 983048 | tf_op jit(solution)/shard_map/ppermute | solution.py:263
  119.1 10.4 %all-to-all-start.7 = ((f32[8,40,128]{2,1,0:T(8,128)}), f32[8,40,128]{2,1,0:T(8,128)S(1)}, u32[]{:S(2)}, u32[]{:S(2)}) async-start(f32[8,40,128]{2,1,0:T(8,128)} %shard_map.64), calls=%async_computation.7 | async-start | bytes 327680 | tf_op jit(solution)/shard_map/all_to_all | solution.py:260
  143.4 4.6 %collective-permute-start.4 = (f32[16,40,128]{2,1,0:T(8,128)S(1)}, f32[16,40,128]{2,1,0:T(8,128)S(1)}, u32[]{:S(2)}, u32[]{:S(2)}) collective-permute-start(f32[16,40,128]{2,1,0:T(8,128)S(1)} %all_to_all.91.own), channel_id=1, source_target_pairs={{0,8},{8,0},{1,9},{9,1},{2,10},{10,2},{3,11},{11,3},{4,12},{12,4},... | collective-permute-start | bytes 983048 | tf_op jit(solution)/shard_map/ppermute | solution.py:263
  149.7 11.1 %all-to-all-start.9 = ((f32[8,40,128]{2,1,0:T(8,128)}), f32[8,40,128]{2,1,0:T(8,128)S(1)}, u32[]{:S(2)}, u32[]{:S(2)}) async-start(f32[8,40,128]{2,1,0:T(8,128)} %shard_map.67), calls=%async_computation.9 | async-start | bytes 327680 | tf_op jit(solution)/shard_map/all_to_all | solution.py:260
  173.4 5.4 %collective-permute-start.5 = (f32[16,40,128]{2,1,0:T(8,128)S(1)}, f32[16,40,128]{2,1,0:T(8,128)S(1)}, u32[]{:S(2)}, u32[]{:S(2)}) collective-permute-start(f32[16,40,128]{2,1,0:T(8,128)S(1)} %all_to_all.92.own), channel_id=1, source_target_pairs={{0,8},{8,0},{1,9},{9,1},{2,10},{10,2},{3,11},{11,3},{4,12},{12,4},... | collective-permute-start | bytes 983048 | tf_op jit(solution)/shard_map/ppermute | solution.py:263
  180.6 10.4 %all-to-all-start.11 = ((f32[8,40,128]{2,1,0:T(8,128)}), f32[8,40,128]{2,1,0:T(8,128)S(1)}, u32[]{:S(2)}, u32[]{:S(2)}) async-start(f32[8,40,128]{2,1,0:T(8,128)} %shard_map.70), calls=%async_computation.11 | async-start | bytes 327680 | tf_op jit(solution)/shard_map/all_to_all | solution.py:260
  204.9 4.6 %collective-permute-start.6 = (f32[16,40,128]{2,1,0:T(8,128)S(1)}, f32[16,40,128]{2,1,0:T(8,128)S(1)}, u32[]{:S(2)}, u32[]{:S(2)}) collective-permute-start(f32[16,40,128]{2,1,0:T(8,128)S(1)} %all_to_all.93.own), channel_id=1, source_target_pairs={{0,8},{8,0},{1,9},{9,1},{2,10},{10,2},{3,11},{11,3},{4,12},{12,4},... | collective-permute-start | bytes 983048 | tf_op jit(solution)/shard_map/ppermute | solution.py:263
  211.2 11.1 %all-to-all-start.13 = ((f32[8,40,128]{2,1,0:T(8,128)}), f32[8,40,128]{2,1,0:T(8,128)S(1)}, u32[]{:S(2)}, u32[]{:S(2)}) async-start(f32[8,40,128]{2,1,0:T(8,128)} %shard_map.73), calls=%async_computation.13 | async-start | bytes 327680 | tf_op jit(solution)/shard_map/all_to_all | solution.py:260
  234.9 5.4 %collective-permute-start.7 = (f32[16,40,128]{2,1,0:T(8,128)S(1)}, f32[16,40,128]{2,1,0:T(8,128)S(1)}, u32[]{:S(2)}, u32[]{:S(2)}) collective-permute-start(f32[16,40,128]{2,1,0:T(8,128)S(1)} %all_to_all.94.own), channel_id=1, source_target_pairs={{0,8},{8,0},{1,9},{9,1},{2,10},{10,2},{3,11},{11,3},{4,12},{12,4},... | collective-permute-start | bytes 983048 | tf_op jit(solution)/shard_map/ppermute | solution.py:263
  242.1 10.4 %all-to-all-start.15 = ((f32[8,40,128]{2,1,0:T(8,128)}), f32[8,40,128]{2,1,0:T(8,128)S(1)}, u32[]{:S(2)}, u32[]{:S(2)}) async-start(f32[8,40,128]{2,1,0:T(8,128)} %shard_map.76), calls=%async_computation.15 | async-start | bytes 327680 | tf_op jit(solution)/shard_map/all_to_all | solution.py:260

commit v8 on v7

--- a/solution.py
+++ b/solution.py
@@ -135,7 +135,7 @@
         picked = []
         for k in range(2):
             col = cols[k, i]
-            m = col >> 2
+            m = (col >> 5) * 8 + ((col >> 2) * 3 & 7)
             b = pl.multiple_of((col & 1) * S, S)
             here = own[m, pl.ds(b, S), :]
             there = peer[m, pl.ds(b, S), :]
@@ -244,7 +244,9 @@
 
 
 def per_device(rhs, diagonal, blocks, block_cols, counts):
-    core = lax.axis_index("core").astype(jnp.int32).reshape(1)
+    core = (lax.axis_index("rows") % 2).astype(jnp.int32).reshape(1)
+    groups = [[16 * (m // 8) + 2 * (3 * m % 8) + c for m in range(16)] for c in range(2)]
+    partner = [(r, r ^ 1) for r in range(32)]
     block_cols = block_cols.T
     counts = counts.T
     shadow = rhs.T
@@ -254,13 +256,13 @@
     message = sds(16, 2 * S + TILE, BS)
 
     def among(x):
-        return lax.all_to_all(x, ("x", "z"), 0, 0, tiled=True)
+        return lax.all_to_all(x, "rows", 0, 0, tiled=True, axis_index_groups=groups)
 
     def across(x):
         return lax.all_to_all(x, "cols", 0, 0, tiled=True)
 
     def exchange(own):
-        return lax.ppermute(own, "core", [(0, 1), (1, 0)])
+        return lax.ppermute(own, "rows", partner)
 
     def product(own, peer):
         out = call(
@@ -306,7 +308,7 @@
     q, alpha, sums = call(last_body, (vec, small, sds(1, BS)), [VMEM] * 5, parts, diag, v, f, r)
     everyone = 2 * 16 * 8
     sums = jnp.broadcast_to(sums[None], (everyone, 1, BS))
-    sums = lax.all_to_all(sums, ("x", "z", "core", "cols"), 0, 0, tiled=True)
+    sums = lax.all_to_all(sums, ("rows", "cols"), 0, 0, tiled=True)
     out = call(
         end_body, jax.ShapeDtypeStruct((S, 2 * BS), F32), [VMEM] * 5, sums.reshape(everyone, BS), alpha, p, x[0], q
     )
@@ -314,16 +316,14 @@
 
 
 def solution(mesh):
-    parts = ("x", "z", "core")
-    mesh = jax.sharding.Mesh(mesh.devices.reshape(2, 8, 2, 8), (*parts, "cols"))
     in_specs = (
-        P((*parts, "cols"), None),
-        P((*parts, "cols")),
-        P(parts, "cols", None, None),
-        P(parts, "cols"),
-        P(parts, "cols"),
+        P(("rows", "cols"), None),
+        P(("rows", "cols")),
+        P("rows", "cols", None, None),
+        P("rows", "cols"),
+        P("rows", "cols"),
     )
-    out_specs = P((*parts, "cols"), None)
+    out_specs = P(("rows", "cols"), None)
     return jax.shard_map(
         per_device, mesh=mesh, in_specs=in_specs, out_specs=out_specs, check_vma=False
     )

time: 275 us -> 277 us (level)
  starting transfers between devices: 50.7 us -> 54.9 us
  blocking collectives: 149 us -> 146 us
    ppermute x8, starting transfers between devices: 28.8 us -> 31.9 us  [exchange(): return lax.ppermute(own, 'rows', partner)]
where the time goes in v8:
time: 277 us; the launch traced here: 276 us
  blocking collectives  146 us (53%)
  starting transfers between devices  54.9 us (20%)
  waiting for transfers between devices  49.5 us (18%)
  Pallas kernels  23.7 us (9%)
    all_to_all x8, blocking collectives, among(): return lax.all_to_all(x, 'rows', 0, 0, tiled=True, axis_index_groups=groups)  103 us
    all_to_all x6, waiting for transfers between devices, across(): return lax.all_to_all(x, 'cols', 0, 0, tiled=True)  40.7 us
    ppermute x8, starting transfers between devices, exchange(): return lax.ppermute(own, 'rows', partner)  31.9 us
    pallas_call x25, Pallas kernels, call(): pl.pallas_call(body, out_shape=outs, in_specs=specs, out_specs=tuple((VME...  23.7 us
    all_to_all x6, starting transfers between devices, across(): return lax.all_to_all(x, 'cols', 0, 0, tiled=True)  23 us
    all_to_all x2, blocking collectives, across(): return lax.all_to_all(x, 'cols', 0, 0, tiled=True)  22.9 us
    all_to_all x1, blocking collectives, per_device(): sums = lax.all_to_all(sums, ('rows', 'cols'), 0, 0, tiled=True)  20.3 us
    ppermute x8, waiting for transfers between devices, exchange(): return lax.ppermute(own, 'rows', partner)  8.79 us
  transfers between devices with their start and end apart: 14, of which 13 were waited for; matrix products, arithmetic and copies ran while one was open for 0% of the time, Pallas kernels for 2%

profile of v8, /device:TPU:1, one launch (start us, length us, event | category | flops | bytes accessed | tf_op | source)
XLA Modules:
  0.0 275.6 jit_solution(1294566836716444596)
XLA Ops:
  0.7 17.5 %all_to_all.85.own = f32[16,32,128]{2,1,0:T(8,128)S(1)} all-to-all(f32[16,32,128]{2,1,0:T(8,128)S(1)} %shard_map.55), channel_id=1, replica_groups={{0,48,96,16,64,112,32,80,128,176,224,144,192,240,160,208},{8,56,104,24,..., dimensions={0} | all-to-all | bytes 524288 | tf_op jit(solution)/shard_map/all_to_all | solution.py:259
  18.2 3.2 %collective-permute-start = (f32[16,32,128]{2,1,0:T(8,128)S(1)}, f32[16,32,128]{2,1,0:T(8,128)S(1)}, u32[]{:S(2)}, u32[]{:S(2)}) collective-permute-start(f32[16,32,128]{2,1,0:T(8,128)S(1)} %all_to_all.85.own), channel_id=1, source_target_pairs={{0,8},{8,0},{16,24},{24,16},{32,40},{40,32},{48,56},{56,48},{64,72... | collective-permute-start | bytes 786440 | tf_op jit(solution)/shard_map/ppermute | solution.py:265
  22.1 3.4 %shard_map.56.packed = bf16[16,256,256]{2,1,0:T(8,128)(2,1)S(1)} custom-call(f32[16,2,128,128]{3,2,1,0:T(8,128)} %source.1, s32[1,16]{1,0:T(1,128)S(1)} %bitcast.36), custom_call_target="tpu_custom_call" | custom-call | tf_op jit(solution)/shard_map/pallas_call | solution.py:30
  26.6 13.1 %all_to_all.86.parts = f32[8,32,128]{2,1,0:T(8,128)S(1)} all-to-all(f32[8,32,128]{2,1,0:T(8,128)S(1)} %shard_map.57), channel_id=1, replica_groups=mesh['rows'=32,'cols'=8] {'cols'}, dimensions={0} | all-to-all | bytes 262144 | tf_op jit(solution)/shard_map/all_to_all | solution.py:262
  39.9 12.3 %all_to_all.87.own = f32[16,40,128]{2,1,0:T(8,128)S(1)} all-to-all(f32[16,40,128]{2,1,0:T(8,128)S(1)} %get-tuple-element.61), channel_id=1, replica_groups={{0,48,96,16,64,112,32,80,128,176,224,144,192,240,160,208},{8,56,104,24,..., dimensions={0} | all-to-all | bytes 655360 | tf_op jit(solution)/shard_map/all_to_all | solution.py:259
  52.2 4.1 %collective-permute-start.1 = (f32[16,40,128]{2,1,0:T(8,128)S(1)}, f32[16,40,128]{2,1,0:T(8,128)S(1)}, u32[]{:S(2)}, u32[]{:S(2)}) collective-permute-start(f32[16,40,128]{2,1,0:T(8,128)S(1)} %all_to_all.87.own), channel_id=1, source_target_pairs={{0,8},{8,0},{16,24},{24,16},{32,40},{40,32},{48,56},{56,48},{64,72... | collective-permute-start | bytes 983048 | tf_op jit(solution)/shard_map/ppermute | solution.py:265
  58.6 9.8 %all_to_all.88.parts = f32[8,40,128]{2,1,0:T(8,128)S(1)} all-to-all(f32[8,40,128]{2,1,0:T(8,128)S(1)} %shard_map.59), channel_id=1, replica_groups=mesh['rows'=32,'cols'=8] {'cols'}, dimensions={0} | all-to-all | bytes 327680 | tf_op jit(solution)/shard_map/all_to_all | solution.py:262
  69.2 12.3 %all_to_all.89.own = f32[16,40,128]{2,1,0:T(8,128)S(1)} all-to-all(f32[16,40,128]{2,1,0:T(8,128)S(1)} %get-tuple-element.63), channel_id=1, replica_groups={{0,48,96,16,64,112,32,80,128,176,224,144,192,240,160,208},{8,56,104,24,..., dimensions={0} | all-to-all | bytes 655360 | tf_op jit(solution)/shard_map/all_to_all | solution.py:259
  81.5 4.1 %collective-permute-start.2 = (f32[16,40,128]{2,1,0:T(8,128)S(1)}, f32[16,40,128]{2,1,0:T(8,128)S(1)}, u32[]{:S(2)}, u32[]{:S(2)}) collective-permute-start(f32[16,40,128]{2,1,0:T(8,128)S(1)} %all_to_all.89.own), channel_id=1, source_target_pairs={{0,8},{8,0},{16,24},{24,16},{32,40},{40,32},{48,56},{56,48},{64,72... | collective-permute-start | bytes 983048 | tf_op jit(solution)/shard_map/ppermute | solution.py:265
  88.5 3.9 %all-to-all-start.5 = ((f32[8,40,128]{2,1,0:T(8,128)}), f32[8,40,128]{2,1,0:T(8,128)S(1)}, u32[]{:S(2)}, u32[]{:S(2)}) async-start(f32[8,40,128]{2,1,0:T(8,128)} %shard_map.61), calls=%async_computation.5 | async-start | bytes 327680 | tf_op jit(solution)/shard_map/all_to_all | solution.py:262
  92.9 6.7 %all-to-all-done.5.parts = f32[8,40,128]{2,1,0:T(8,128)S(1)} async-done(((f32[8,40,128]{2,1,0:T(8,128)}), f32[8,40,128]{2,1,0:T(8,128)S(1)}, u32[]{:S(2)}, u32[]{:S(2)}) %all-to-all-start.5) | async-done | bytes 163872 | tf_op jit(solution)/shard_map/all_to_all | solution.py:262
  100.2 12.1 %all_to_all.90.own = f32[16,40,128]{2,1,0:T(8,128)S(1)} all-to-all(f32[16,40,128]{2,1,0:T(8,128)S(1)} %get-tuple-element.70), channel_id=1, replica_groups={{0,48,96,16,64,112,32,80,128,176,224,144,192,240,160,208},{8,56,104,24,..., dimensions={0} | all-to-all | bytes 655360 | tf_op jit(solution)/shard_map/all_to_all | solution.py:259
  112.3 4.1 %collective-permute-start.3 = (f32[16,40,128]{2,1,0:T(8,128)S(1)}, f32[16,40,128]{2,1,0:T(8,128)S(1)}, u32[]{:S(2)}, u32[]{:S(2)}) collective-permute-start(f32[16,40,128]{2,1,0:T(8,128)S(1)} %all_to_all.90.own), channel_id=1, source_target_pairs={{0,8},{8,0},{16,24},{24,16},{32,40},{40,32},{48,56},{56,48},{64,72... | collective-permute-start | bytes 983048 | tf_op jit(solution)/shard_map/ppermute | solution.py:265
  119.4 3.7 %all-to-all-start.7 = ((f32[8,40,128]{2,1,0:T(8,128)}), f32[8,40,128]{2,1,0:T(8,128)S(1)}, u32[]{:S(2)}, u32[]{:S(2)}) async-start(f32[8,40,128]{2,1,0:T(8,128)} %shard_map.64), calls=%async_computation.7 | async-start | bytes 327680 | tf_op jit(solution)/shard_map/all_to_all | solution.py:262
  123.3 6.9 %all-to-all-done.7.parts = f32[8,40,128]{2,1,0:T(8,128)S(1)} async-done(((f32[8,40,128]{2,1,0:T(8,128)}), f32[8,40,128]{2,1,0:T(8,128)S(1)}, u32[]{:S(2)}, u32[]{:S(2)}) %all-to-all-start.7) | async-done | bytes 163872 | tf_op jit(solution)/shard_map/all_to_all | solution.py:262
  131.1 12.1 %all_to_all.91.own = f32[16,40,128]{2,1,0:T(8,128)S(1)} all-to-all(f32[16,40,128]{2,1,0:T(8,128)S(1)} %get-tuple-element.78), channel_id=1, replica_groups={{0,48,96,16,64,112,32,80,128,176,224,144,192,240,160,208},{8,56,104,24,..., dimensions={0} | all-to-all | bytes 655360 | tf_op jit(solution)/shard_map/all_to_all | solution.py:259
  143.2 4.1 %collective-permute-start.4 = (f32[16,40,128]{2,1,0:T(8,128)S(1)}, f32[16,40,128]{2,1,0:T(8,128)S(1)}, u32[]{:S(2)}, u32[]{:S(2)}) collective-permute-start(f32[16,40,128]{2,1,0:T(8,128)S(1)} %all_to_all.91.own), channel_id=1, source_target_pairs={{0,8},{8,0},{16,24},{24,16},{32,40},{40,32},{48,56},{56,48},{64,72... | collective-permute-start | bytes 983048 | tf_op jit(solution)/shard_map/ppermute | solution.py:265
  150.2 3.9 %all-to-all-start.9 = ((f32[8,40,128]{2,1,0:T(8,128)}), f32[8,40,128]{2,1,0:T(8,128)S(1)}, u32[]{:S(2)}, u32[]{:S(2)}) async-start(f32[8,40,128]{2,1,0:T(8,128)} %shard_map.67), calls=%async_computation.9 | async-start | bytes 327680 | tf_op jit(solution)/shard_map/all_to_all | solution.py:262
  154.6 6.7 %all-to-all-done.9.parts = f32[8,40,128]{2,1,0:T(8,128)S(1)} async-done(((f32[8,40,128]{2,1,0:T(8,128)}), f32[8,40,128]{2,1,0:T(8,128)S(1)}, u32[]{:S(2)}, u32[]{:S(2)}) %all-to-all-start.9) | async-done | bytes 163872 | tf_op jit(solution)/shard_map/all_to_all | solution.py:262
  161.9 12.1 %all_to_all.92.own = f32[16,40,128]{2,1,0:T(8,128)S(1)} all-to-all(f32[16,40,128]{2,1,0:T(8,128)S(1)} %get-tuple-element.87), channel_id=1, replica_groups={{0,48,96,16,64,112,32,80,128,176,224,144,192,240,160,208},{8,56,104,24,..., dimensions={0} | all-to-all | bytes 655360 | tf_op jit(solution)/shard_map/all_to_all | solution.py:259
  174.0 4.1 %collective-permute-start.5 = (f32[16,40,128]{2,1,0:T(8,128)S(1)}, f32[16,40,128]{2,1,0:T(8,128)S(1)}, u32[]{:S(2)}, u32[]{:S(2)}) collective-permute-start(f32[16,40,128]{2,1,0:T(8,128)S(1)} %all_to_all.92.own), channel_id=1, source_target_pairs={{0,8},{8,0},{16,24},{24,16},{32,40},{40,32},{48,56},{56,48},{64,72... | collective-permute-start | bytes 983048 | tf_op jit(solution)/shard_map/ppermute | solution.py:265
  181.1 3.7 %all-to-all-start.11 = ((f32[8,40,128]{2,1,0:T(8,128)}), f32[8,40,128]{2,1,0:T(8,128)S(1)}, u32[]{:S(2)}, u32[]{:S(2)}) async-start(f32[8,40,128]{2,1,0:T(8,128)} %shard_map.70), calls=%async_computation.11 | async-start | bytes 327680 | tf_op jit(solution)/shard_map/all_to_all | solution.py:262
  185.0 6.9 %all-to-all-done.11.parts = f32[8,40,128]{2,1,0:T(8,128)S(1)} async-done(((f32[8,40,128]{2,1,0:T(8,128)}), f32[8,40,128]{2,1,0:T(8,128)S(1)}, u32[]{:S(2)}, u32[]{:S(2)}) %all-to-all-start.11) | async-done | bytes 163872 | tf_op jit(solution)/shard_map/all_to_all | solution.py:262
  192.8 12.1 %all_to_all.93.own = f32[16,40,128]{2,1,0:T(8,128)S(1)} all-to-all(f32[16,40,128]{2,1,0:T(8,128)S(1)} %get-tuple-element.95), channel_id=1, replica_groups={{0,48,96,16,64,112,32,80,128,176,224,144,192,240,160,208},{8,56,104,24,..., dimensions={0} | all-to-all | bytes 655360 | tf_op jit(solution)/shard_map/all_to_all | solution.py:259
  204.9 4.1 %collective-permute-start.6 = (f32[16,40,128]{2,1,0:T(8,128)S(1)}, f32[16,40,128]{2,1,0:T(8,128)S(1)}, u32[]{:S(2)}, u32[]{:S(2)}) collective-permute-start(f32[16,40,128]{2,1,0:T(8,128)S(1)} %all_to_all.93.own), channel_id=1, source_target_pairs={{0,8},{8,0},{16,24},{24,16},{32,40},{40,32},{48,56},{56,48},{64,72... | collective-permute-start | bytes 983048 | tf_op jit(solution)/shard_map/ppermute | solution.py:265
  212.0 3.9 %all-to-all-start.13 = ((f32[8,40,128]{2,1,0:T(8,128)}), f32[8,40,128]{2,1,0:T(8,128)S(1)}, u32[]{:S(2)}, u32[]{:S(2)}) async-start(f32[8,40,128]{2,1,0:T(8,128)} %shard_map.73), calls=%async_computation.13 | async-start | bytes 327680 | tf_op jit(solution)/shard_map/all_to_all | solution.py:262
  216.3 6.7 %all-to-all-done.13.parts = f32[8,40,128]{2,1,0:T(8,128)S(1)} async-done(((f32[8,40,128]{2,1,0:T(8,128)}), f32[8,40,128]{2,1,0:T(8,128)S(1)}, u32[]{:S(2)}, u32[]{:S(2)}) %all-to-all-start.13) | async-done | bytes 163872 | tf_op jit(solution)/shard_map/all_to_all | solution.py:262
  223.6 12.1 %all_to_all.94.own = f32[16,40,128]{2,1,0:T(8,128)S(1)} all-to-all(f32[16,40,128]{2,1,0:T(8,128)S(1)} %get-tuple-element.104), channel_id=1, replica_groups={{0,48,96,16,64,112,32,80,128,176,224,144,192,240,160,208},{8,56,104,24,..., dimensions={0} | all-to-all | bytes 655360 | tf_op jit(solution)/shard_map/all_to_all | solution.py:259
  235.8 4.1 %collective-permute-start.7 = (f32[16,40,128]{2,1,0:T(8,128)S(1)}, f32[16,40,128]{2,1,0:T(8,128)S(1)}, u32[]{:S(2)}, u32[]{:S(2)}) collective-permute-start(f32[16,40,128]{2,1,0:T(8,128)S(1)} %all_to_all.94.own), channel_id=1, source_target_pairs={{0,8},{8,0},{16,24},{24,16},{32,40},{40,32},{48,56},{56,48},{64,72... | collective-permute-start | bytes 983048 | tf_op jit(solution)/shard_map/ppermute | solution.py:265
  242.8 3.7 %all-to-all-start.15 = ((f32[8,40,128]{2,1,0:T(8,128)}), f32[8,40,128]{2,1,0:T(8,128)S(1)}, u32[]{:S(2)}, u32[]{:S(2)}) async-start(f32[8,40,128]{2,1,0:T(8,128)} %shard_map.76), calls=%async_computation.15 | async-start | bytes 327680 | tf_op jit(solution)/shard_map/all_to_all | solution.py:262
  246.8 6.9 %all-to-all-done.15.parts = f32[8,40,128]{2,1,0:T(8,128)S(1)} async-done(((f32[8,40,128]{2,1,0:T(8,128)}), f32[8,40,128]{2,1,0:T(8,128)S(1)}, u32[]{:S(2)}, u32[]{:S(2)}) %all-to-all-start.15) | async-done | bytes 163872 | tf_op jit(solution)/shard_map/all_to_all | solution.py:262
  254.5 20.3 %all_to_all.95 = f32[256,1,128]{2,1,0:T(1,128)S(1)} all-to-all(f32[256,1,128]{2,1,0:T(1,128)S(1)} %broadcast_in_dim.9), channel_id=1, replica_groups=mesh['rows'=32,'cols'=8] {'rows','cols'}, dimensions={0} | all-to-all | bytes 262144 | tf_op jit(solution)/shard_map/all_to_all | solution.py:311
  (43 shorter events, 30.6 us)
Async XLA Ops:
  0.0 0.7 copy-start
  18.2 7.3 %collective-permute-start = (f32[16,32,128]{2,1,0:T(8,128)S(1)}, f32[16,32,128]{2,1,0:T(8,128)S(1)}, u32[]{:S(2)}, u32[]{:S(2)}) collective-permute-start(f32[16,32,128]{2,1,0:T(8,128)S(1)} %all_to_all.85.own), channel_id=1, source_target_pairs={{0,8},{8,0},{16,24},{24,16},{32,40},{40,32},{48,56},{56,48},{64,72... | collective-permute-start | bytes 786440 | tf_op jit(solution)/shard_map/ppermute | solution.py:265
  21.4 0.7 copy-start.4
  22.1 3.4 %copy-start.2 = (s32[16,2]{0,1:T(2,128)S(1)}, s32[16,2]{0,1:T(2,128)}, u32[]{:S(2)}) copy-start(s32[16,2]{0,1:T(2,128)} %param.8) | copy-start | bytes 388
  25.5 14.2 %copy-start.1 = (f32[256,16]{0,1:T(8,128)S(1)}, f32[256,16]{0,1:T(8,128)}, u32[]{:S(2)}) copy-start(f32[256,16]{0,1:T(8,128)} %param.5) | copy-start | bytes 49156
  25.5 14.1 %copy-start.3 = (f32[256]{0:T(256)S(1)}, f32[256]{0:T(256)}, u32[]{:S(2)}) copy-start(f32[256]{0:T(256)} %param.6) | copy-start | bytes 3076
  52.2 5.4 %collective-permute-start.1 = (f32[16,40,128]{2,1,0:T(8,128)S(1)}, f32[16,40,128]{2,1,0:T(8,128)S(1)}, u32[]{:S(2)}, u32[]{:S(2)}) collective-permute-start(f32[16,40,128]{2,1,0:T(8,128)S(1)} %all_to_all.87.own), channel_id=1, source_target_pairs={{0,8},{8,0},{16,24},{24,16},{32,40},{40,32},{48,56},{56,48},{64,72... | collective-permute-start | bytes 983048 | tf_op jit(solution)/shard_map/ppermute | solution.py:265
  81.5 5.4 %collective-permute-start.2 = (f32[16,40,128]{2,1,0:T(8,128)S(1)}, f32[16,40,128]{2,1,0:T(8,128)S(1)}, u32[]{:S(2)}, u32[]{:S(2)}) collective-permute-start(f32[16,40,128]{2,1,0:T(8,128)S(1)} %all_to_all.89.own), channel_id=1, source_target_pairs={{0,8},{8,0},{16,24},{24,16},{32,40},{40,32},{48,56},{56,48},{64,72... | collective-permute-start | bytes 983048 | tf_op jit(solution)/shard_map/ppermute | solution.py:265
  88.5 11.0 %all-to-all-start.5 = ((f32[8,40,128]{2,1,0:T(8,128)}), f32[8,40,128]{2,1,0:T(8,128)S(1)}, u32[]{:S(2)}, u32[]{:S(2)}) async-start(f32[8,40,128]{2,1,0:T(8,128)} %shard_map.61), calls=%async_computation.5 | async-start | bytes 327680 | tf_op jit(solution)/shard_map/all_to_all | solution.py:262
  112.3 5.4 %collective-permute-start.3 = (f32[16,40,128]{2,1,0:T(8,128)S(1)}, f32[16,40,128]{2,1,0:T(8,128)S(1)}, u32[]{:S(2)}, u32[]{:S(2)}) collective-permute-start(f32[16,40,128]{2,1,0:T(8,128)S(1)} %all_to_all.90.own), channel_id=1, source_target_pairs={{0,8},{8,0},{16,24},{24,16},{32,40},{40,32},{48,56},{56,48},{64,72... | collective-permute-start | bytes 983048 | tf_op jit(solution)/shard_map/ppermute | solution.py:265
  119.4 10.9 %all-to-all-start.7 = ((f32[8,40,128]{2,1,0:T(8,128)}), f32[8,40,128]{2,1,0:T(8,128)S(1)}, u32[]{:S(2)}, u32[]{:S(2)}) async-start(f32[8,40,128]{2,1,0:T(8,128)} %shard_map.64), calls=%async_computation.7 | async-start | bytes 327680 | tf_op jit(solution)/shard_map/all_to_all | solution.py:262
  143.2 5.4 %collective-permute-start.4 = (f32[16,40,128]{2,1,0:T(8,128)S(1)}, f32[16,40,128]{2,1,0:T(8,128)S(1)}, u32[]{:S(2)}, u32[]{:S(2)}) collective-permute-start(f32[16,40,128]{2,1,0:T(8,128)S(1)} %all_to_all.91.own), channel_id=1, source_target_pairs={{0,8},{8,0},{16,24},{24,16},{32,40},{40,32},{48,56},{56,48},{64,72... | collective-permute-start | bytes 983048 | tf_op jit(solution)/shard_map/ppermute | solution.py:265
  150.2 11.0 %all-to-all-start.9 = ((f32[8,40,128]{2,1,0:T(8,128)}), f32[8,40,128]{2,1,0:T(8,128)S(1)}, u32[]{:S(2)}, u32[]{:S(2)}) async-start(f32[8,40,128]{2,1,0:T(8,128)} %shard_map.67), calls=%async_computation.9 | async-start | bytes 327680 | tf_op jit(solution)/shard_map/all_to_all | solution.py:262
  174.0 5.4 %collective-permute-start.5 = (f32[16,40,128]{2,1,0:T(8,128)S(1)}, f32[16,40,128]{2,1,0:T(8,128)S(1)}, u32[]{:S(2)}, u32[]{:S(2)}) collective-permute-start(f32[16,40,128]{2,1,0:T(8,128)S(1)} %all_to_all.92.own), channel_id=1, source_target_pairs={{0,8},{8,0},{16,24},{24,16},{32,40},{40,32},{48,56},{56,48},{64,72... | collective-permute-start | bytes 983048 | tf_op jit(solution)/shard_map/ppermute | solution.py:265
  181.1 10.9 %all-to-all-start.11 = ((f32[8,40,128]{2,1,0:T(8,128)}), f32[8,40,128]{2,1,0:T(8,128)S(1)}, u32[]{:S(2)}, u32[]{:S(2)}) async-start(f32[8,40,128]{2,1,0:T(8,128)} %shard_map.70), calls=%async_computation.11 | async-start | bytes 327680 | tf_op jit(solution)/shard_map/all_to_all | solution.py:262
  204.9 5.4 %collective-permute-start.6 = (f32[16,40,128]{2,1,0:T(8,128)S(1)}, f32[16,40,128]{2,1,0:T(8,128)S(1)}, u32[]{:S(2)}, u32[]{:S(2)}) collective-permute-start(f32[16,40,128]{2,1,0:T(8,128)S(1)} %all_to_all.93.own), channel_id=1, source_target_pairs={{0,8},{8,0},{16,24},{24,16},{32,40},{40,32},{48,56},{56,48},{64,72... | collective-permute-start | bytes 983048 | tf_op jit(solution)/shard_map/ppermute | solution.py:265
  212.0 11.0 %all-to-all-start.13 = ((f32[8,40,128]{2,1,0:T(8,128)}), f32[8,40,128]{2,1,0:T(8,128)S(1)}, u32[]{:S(2)}, u32[]{:S(2)}) async-start(f32[8,40,128]{2,1,0:T(8,128)} %shard_map.73), calls=%async_computation.13 | async-start | bytes 327680 | tf_op jit(solution)/shard_map/all_to_all | solution.py:262
  235.8 5.4 %collective-permute-start.7 = (f32[16,40,128]{2,1,0:T(8,128)S(1)}, f32[16,40,128]{2,1,0:T(8,128)S(1)}, u32[]{:S(2)}, u32[]{:S(2)}) collective-permute-start(f32[16,40,128]{2,1,0:T(8,128)S(1)} %all_to_all.94.own), channel_id=1, source_target_pairs={{0,8},{8,0},{16,24},{24,16},{32,40},{40,32},{48,56},{56,48},{64,72... | collective-permute-start | bytes 983048 | tf_op jit(solution)/shard_map/ppermute | solution.py:265
  242.8 10.9 %all-to-all-start.15 = ((f32[8,40,128]{2,1,0:T(8,128)}), f32[8,40,128]{2,1,0:T(8,128)S(1)}, u32[]{:S(2)}, u32[]{:S(2)}) async-start(f32[8,40,128]{2,1,0:T(8,128)} %shard_map.76), calls=%async_computation.15 | async-start | bytes 327680 | tf_op jit(solution)/shard_map/all_to_all | solution.py:262

commit v9 on v7

--- a/solution.py
+++ b/solution.py
@@ -14,7 +14,7 @@
 VMEM = pl.BlockSpec(memory_space=pltpu.VMEM)
 SMEM = pl.BlockSpec(memory_space=pltpu.SMEM)
 HBM = pl.BlockSpec(memory_space=pltpu.HBM)
-GROUP = 8
+GROUP = 16
 TILE = 8
 
 
@@ -153,7 +153,10 @@
             out[c, 2 * S :] = tile + tile2
 
 
-def start_body(shadow, message):
+def start_body(source, message, shadow, done):
+    copy = pltpu.make_async_copy(source, shadow, done)
+    copy.start()
+    copy.wait()
     value = shadow[...]
     for k in range(message.shape[0]):
         message[k, 0:S] = value[:, :BS]
@@ -270,7 +273,10 @@
         return across(out)
 
     held = [pltpu.VMEM((16, 2, BS, BS), F32), pltpu.SemaphoreType.DMA((16,))]
-    msg = call(start_body, jax.ShapeDtypeStruct((16, 2 * S, BS), F32), [VMEM], shadow)
+    msg = call(
+        start_body, jax.ShapeDtypeStruct((16, 2 * S, BS), F32), [HBM], shadow,
+        scratch=[pltpu.VMEM((S, 2 * BS), F32), pltpu.SemaphoreType.DMA],
+    )
     own = among(msg)
     packed = call(
         prepare_body, sds(16, 2 * BS, 2 * BS, dtype=jnp.bfloat16), [HBM, SMEM],

time: 275 us -> 275 us (level)
  no operation moved by 1% of the time
where the time goes in v9:
time: 275 us; the launch traced here: 274 us
  blocking collectives  149 us (54%)
  starting transfers between devices  50.7 us (18%)
  waiting for transfers between devices  49.5 us (18%)
  Pallas kernels  23.9 us (9%)
    all_to_all x8, blocking collectives, among(): return lax.all_to_all(x, ('x', 'z'), 0, 0, tiled=True)  106 us
    all_to_all x6, waiting for transfers between devices, across(): return lax.all_to_all(x, 'cols', 0, 0, tiled=True)  40.7 us
    ppermute x8, starting transfers between devices, exchange(): return lax.ppermute(own, 'core', [(0, 1), (1, 0)])  28.8 us
    pallas_call x25, Pallas kernels, call(): pl.pallas_call(body, out_shape=outs, in_specs=specs, out_specs=tuple((VME...  23.9 us
    all_to_all x2, blocking collectives, across(): return lax.all_to_all(x, 'cols', 0, 0, tiled=True)  23.1 us
    all_to_all x6, starting transfers between devices, across(): return lax.all_to_all(x, 'cols', 0, 0, tiled=True)  21.9 us
    all_to_all x1, blocking collectives, per_device(): sums = lax.all_to_all(sums, ('x', 'z', 'core', 'cols'), 0, 0, tiled=True)  20.1 us
    ppermute x8, waiting for transfers between devices, exchange(): return lax.ppermute(own, 'core', [(0, 1), (1, 0)])  8.79 us
  transfers between devices with their start and end apart: 14, of which 13 were waited for; matrix products, arithmetic and copies ran while one was open for 0% of the time, Pallas kernels for 2%

profile of v9, /device:TPU:1, one launch (start us, length us, event | category | flops | bytes accessed | tf_op | source)
XLA Modules:
  0.0 273.9 jit_solution(3155729851603221683)
XLA Ops:
  0.8 18.6 %all_to_all.85.own = f32[16,32,128]{2,1,0:T(8,128)S(1)} all-to-all(f32[16,32,128]{2,1,0:T(8,128)S(1)} %shard_map.55), channel_id=1, replica_groups=mesh['x'=2,'z'=8,'core'=2,'cols'=8] {'x','z'}, dimensions={0} | all-to-all | bytes 524288 | tf_op jit(solution)/shard_map/all_to_all | solution.py:260
  19.4 2.3 collective-permute-start
  22.3 3.4 %shard_map.56.packed = bf16[16,256,256]{2,1,0:T(8,128)(2,1)S(1)} custom-call(f32[16,2,128,128]{3,2,1,0:T(8,128)} %source.1, s32[1,16]{1,0:T(1,128)S(1)} %bitcast.36), custom_call_target="tpu_custom_call" | custom-call | tf_op jit(solution)/shard_map/pallas_call | solution.py:30
  26.8 13.1 %all_to_all.86.parts = f32[8,32,128]{2,1,0:T(8,128)S(1)} all-to-all(f32[8,32,128]{2,1,0:T(8,128)S(1)} %shard_map.57), channel_id=1, replica_groups=mesh['x'=2,'z'=8,'core'=2,'cols'=8] {'cols'}, dimensions={0} | all-to-all | bytes 262144 | tf_op jit(solution)/shard_map/all_to_all | solution.py:263
  40.1 12.8 %all_to_all.87.own = f32[16,40,128]{2,1,0:T(8,128)S(1)} all-to-all(f32[16,40,128]{2,1,0:T(8,128)S(1)} %get-tuple-element.61), channel_id=1, replica_groups=mesh['x'=2,'z'=8,'core'=2,'cols'=8] {'x','z'}, dimensions={0} | all-to-all | bytes 655360 | tf_op jit(solution)/shard_map/all_to_all | solution.py:260
  52.9 3.2 %collective-permute-start.1 = (f32[16,40,128]{2,1,0:T(8,128)S(1)}, f32[16,40,128]{2,1,0:T(8,128)S(1)}, u32[]{:S(2)}, u32[]{:S(2)}) collective-permute-start(f32[16,40,128]{2,1,0:T(8,128)S(1)} %all_to_all.87.own), channel_id=1, source_target_pairs={{0,8},{8,0},{1,9},{9,1},{2,10},{10,2},{3,11},{11,3},{4,12},{12,4},... | collective-permute-start | bytes 983048 | tf_op jit(solution)/shard_map/ppermute | solution.py:266
  58.4 10.0 %all_to_all.88.parts = f32[8,40,128]{2,1,0:T(8,128)S(1)} all-to-all(f32[8,40,128]{2,1,0:T(8,128)S(1)} %shard_map.59), channel_id=1, replica_groups=mesh['x'=2,'z'=8,'core'=2,'cols'=8] {'cols'}, dimensions={0} | all-to-all | bytes 327680 | tf_op jit(solution)/shard_map/all_to_all | solution.py:263
  69.2 12.0 %all_to_all.89.own = f32[16,40,128]{2,1,0:T(8,128)S(1)} all-to-all(f32[16,40,128]{2,1,0:T(8,128)S(1)} %get-tuple-element.63), channel_id=1, replica_groups=mesh['x'=2,'z'=8,'core'=2,'cols'=8] {'x','z'}, dimensions={0} | all-to-all | bytes 655360 | tf_op jit(solution)/shard_map/all_to_all | solution.py:260
  81.2 4.2 %collective-permute-start.2 = (f32[16,40,128]{2,1,0:T(8,128)S(1)}, f32[16,40,128]{2,1,0:T(8,128)S(1)}, u32[]{:S(2)}, u32[]{:S(2)}) collective-permute-start(f32[16,40,128]{2,1,0:T(8,128)S(1)} %all_to_all.89.own), channel_id=1, source_target_pairs={{0,8},{8,0},{1,9},{9,1},{2,10},{10,2},{3,11},{11,3},{4,12},{12,4},... | collective-permute-start | bytes 983048 | tf_op jit(solution)/shard_map/ppermute | solution.py:266
  88.3 3.8 %all-to-all-start.5 = ((f32[8,40,128]{2,1,0:T(8,128)}), f32[8,40,128]{2,1,0:T(8,128)S(1)}, u32[]{:S(2)}, u32[]{:S(2)}) async-start(f32[8,40,128]{2,1,0:T(8,128)} %shard_map.61), calls=%async_computation.5 | async-start | bytes 327680 | tf_op jit(solution)/shard_map/all_to_all | solution.py:263
  92.5 6.7 %all-to-all-done.5.parts = f32[8,40,128]{2,1,0:T(8,128)S(1)} async-done(((f32[8,40,128]{2,1,0:T(8,128)}), f32[8,40,128]{2,1,0:T(8,128)S(1)}, u32[]{:S(2)}, u32[]{:S(2)}) %all-to-all-start.5) | async-done | bytes 163872 | tf_op jit(solution)/shard_map/all_to_all | solution.py:263
  99.9 12.0 %all_to_all.90.own = f32[16,40,128]{2,1,0:T(8,128)S(1)} all-to-all(f32[16,40,128]{2,1,0:T(8,128)S(1)} %get-tuple-element.70), channel_id=1, replica_groups=mesh['x'=2,'z'=8,'core'=2,'cols'=8] {'x','z'}, dimensions={0} | all-to-all | bytes 655360 | tf_op jit(solution)/shard_map/all_to_all | solution.py:260
  111.9 4.2 %collective-permute-start.3 = (f32[16,40,128]{2,1,0:T(8,128)S(1)}, f32[16,40,128]{2,1,0:T(8,128)S(1)}, u32[]{:S(2)}, u32[]{:S(2)}) collective-permute-start(f32[16,40,128]{2,1,0:T(8,128)S(1)} %all_to_all.90.own), channel_id=1, source_target_pairs={{0,8},{8,0},{1,9},{9,1},{2,10},{10,2},{3,11},{11,3},{4,12},{12,4},... | collective-permute-start | bytes 983048 | tf_op jit(solution)/shard_map/ppermute | solution.py:266
  119.0 3.4 %all-to-all-start.7 = ((f32[8,40,128]{2,1,0:T(8,128)}), f32[8,40,128]{2,1,0:T(8,128)S(1)}, u32[]{:S(2)}, u32[]{:S(2)}) async-start(f32[8,40,128]{2,1,0:T(8,128)} %shard_map.64), calls=%async_computation.7 | async-start | bytes 327680 | tf_op jit(solution)/shard_map/all_to_all | solution.py:263
  122.6 6.8 %all-to-all-done.7.parts = f32[8,40,128]{2,1,0:T(8,128)S(1)} async-done(((f32[8,40,128]{2,1,0:T(8,128)}), f32[8,40,128]{2,1,0:T(8,128)S(1)}, u32[]{:S(2)}, u32[]{:S(2)}) %all-to-all-start.7) | async-done | bytes 163872 | tf_op jit(solution)/shard_map/all_to_all | solution.py:263
  130.2 13.1 %all_to_all.91.own = f32[16,40,128]{2,1,0:T(8,128)S(1)} all-to-all(f32[16,40,128]{2,1,0:T(8,128)S(1)} %get-tuple-element.78), channel_id=1, replica_groups=mesh['x'=2,'z'=8,'core'=2,'cols'=8] {'x','z'}, dimensions={0} | all-to-all | bytes 655360 | tf_op jit(solution)/shard_map/all_to_all | solution.py:260
  143.3 3.3 %collective-permute-start.4 = (f32[16,40,128]{2,1,0:T(8,128)S(1)}, f32[16,40,128]{2,1,0:T(8,128)S(1)}, u32[]{:S(2)}, u32[]{:S(2)}) collective-permute-start(f32[16,40,128]{2,1,0:T(8,128)S(1)} %all_to_all.91.own), channel_id=1, source_target_pairs={{0,8},{8,0},{1,9},{9,1},{2,10},{10,2},{3,11},{11,3},{4,12},{12,4},... | collective-permute-start | bytes 983048 | tf_op jit(solution)/shard_map/ppermute | solution.py:266
  149.5 4.0 %all-to-all-start.9 = ((f32[8,40,128]{2,1,0:T(8,128)}), f32[8,40,128]{2,1,0:T(8,128)S(1)}, u32[]{:S(2)}, u32[]{:S(2)}) async-start(f32[8,40,128]{2,1,0:T(8,128)} %shard_map.67), calls=%async_computation.9 | async-start | bytes 327680 | tf_op jit(solution)/shard_map/all_to_all | solution.py:263
  153.9 6.7 %all-to-all-done.9.parts = f32[8,40,128]{2,1,0:T(8,128)S(1)} async-done(((f32[8,40,128]{2,1,0:T(8,128)}), f32[8,40,128]{2,1,0:T(8,128)S(1)}, u32[]{:S(2)}, u32[]{:S(2)}) %all-to-all-start.9) | async-done | bytes 163872 | tf_op jit(solution)/shard_map/all_to_all | solution.py:263
  161.3 12.0 %all_to_all.92.own = f32[16,40,128]{2,1,0:T(8,128)S(1)} all-to-all(f32[16,40,128]{2,1,0:T(8,128)S(1)} %get-tuple-element.87), channel_id=1, replica_groups=mesh['x'=2,'z'=8,'core'=2,'cols'=8] {'x','z'}, dimensions={0} | all-to-all | bytes 655360 | tf_op jit(solution)/shard_map/all_to_all | solution.py:260
  173.3 4.2 %collective-permute-start.5 = (f32[16,40,128]{2,1,0:T(8,128)S(1)}, f32[16,40,128]{2,1,0:T(8,128)S(1)}, u32[]{:S(2)}, u32[]{:S(2)}) collective-permute-start(f32[16,40,128]{2,1,0:T(8,128)S(1)} %all_to_all.92.own), channel_id=1, source_target_pairs={{0,8},{8,0},{1,9},{9,1},{2,10},{10,2},{3,11},{11,3},{4,12},{12,4},... | collective-permute-start | bytes 983048 | tf_op jit(solution)/shard_map/ppermute | solution.py:266
  180.4 3.4 %all-to-all-start.11 = ((f32[8,40,128]{2,1,0:T(8,128)}), f32[8,40,128]{2,1,0:T(8,128)S(1)}, u32[]{:S(2)}, u32[]{:S(2)}) async-start(f32[8,40,128]{2,1,0:T(8,128)} %shard_map.70), calls=%async_computation.11 | async-start | bytes 327680 | tf_op jit(solution)/shard_map/all_to_all | solution.py:263
  184.0 6.8 %all-to-all-done.11.parts = f32[8,40,128]{2,1,0:T(8,128)S(1)} async-done(((f32[8,40,128]{2,1,0:T(8,128)}), f32[8,40,128]{2,1,0:T(8,128)S(1)}, u32[]{:S(2)}, u32[]{:S(2)}) %all-to-all-start.11) | async-done | bytes 163872 | tf_op jit(solution)/shard_map/all_to_all | solution.py:263
  191.6 13.1 %all_to_all.93.own = f32[16,40,128]{2,1,0:T(8,128)S(1)} all-to-all(f32[16,40,128]{2,1,0:T(8,128)S(1)} %get-tuple-element.95), channel_id=1, replica_groups=mesh['x'=2,'z'=8,'core'=2,'cols'=8] {'x','z'}, dimensions={0} | all-to-all | bytes 655360 | tf_op jit(solution)/shard_map/all_to_all | solution.py:260
  204.7 3.3 %collective-permute-start.6 = (f32[16,40,128]{2,1,0:T(8,128)S(1)}, f32[16,40,128]{2,1,0:T(8,128)S(1)}, u32[]{:S(2)}, u32[]{:S(2)}) collective-permute-start(f32[16,40,128]{2,1,0:T(8,128)S(1)} %all_to_all.93.own), channel_id=1, source_target_pairs={{0,8},{8,0},{1,9},{9,1},{2,10},{10,2},{3,11},{11,3},{4,12},{12,4},... | collective-permute-start | bytes 983048 | tf_op jit(solution)/shard_map/ppermute | solution.py:266
  211.0 4.0 %all-to-all-start.13 = ((f32[8,40,128]{2,1,0:T(8,128)}), f32[8,40,128]{2,1,0:T(8,128)S(1)}, u32[]{:S(2)}, u32[]{:S(2)}) async-start(f32[8,40,128]{2,1,0:T(8,128)} %shard_map.73), calls=%async_computation.13 | async-start | bytes 327680 | tf_op jit(solution)/shard_map/all_to_all | solution.py:263
  215.3 6.7 %all-to-all-done.13.parts = f32[8,40,128]{2,1,0:T(8,128)S(1)} async-done(((f32[8,40,128]{2,1,0:T(8,128)}), f32[8,40,128]{2,1,0:T(8,128)S(1)}, u32[]{:S(2)}, u32[]{:S(2)}) %all-to-all-start.13) | async-done | bytes 163872 | tf_op jit(solution)/shard_map/all_to_all | solution.py:263
  222.7 12.0 %all_to_all.94.own = f32[16,40,128]{2,1,0:T(8,128)S(1)} all-to-all(f32[16,40,128]{2,1,0:T(8,128)S(1)} %get-tuple-element.104), channel_id=1, replica_groups=mesh['x'=2,'z'=8,'core'=2,'cols'=8] {'x','z'}, dimensions={0} | all-to-all | bytes 655360 | tf_op jit(solution)/shard_map/all_to_all | solution.py:260
  234.7 4.2 %collective-permute-start.7 = (f32[16,40,128]{2,1,0:T(8,128)S(1)}, f32[16,40,128]{2,1,0:T(8,128)S(1)}, u32[]{:S(2)}, u32[]{:S(2)}) collective-permute-start(f32[16,40,128]{2,1,0:T(8,128)S(1)} %all_to_all.94.own), channel_id=1, source_target_pairs={{0,8},{8,0},{1,9},{9,1},{2,10},{10,2},{3,11},{11,3},{4,12},{12,4},... | collective-permute-start | bytes 983048 | tf_op jit(solution)/shard_map/ppermute | solution.py:266
  241.8 3.4 %all-to-all-start.15 = ((f32[8,40,128]{2,1,0:T(8,128)}), f32[8,40,128]{2,1,0:T(8,128)S(1)}, u32[]{:S(2)}, u32[]{:S(2)}) async-start(f32[8,40,128]{2,1,0:T(8,128)} %shard_map.76), calls=%async_computation.15 | async-start | bytes 327680 | tf_op jit(solution)/shard_map/all_to_all | solution.py:263
  245.4 6.8 %all-to-all-done.15.parts = f32[8,40,128]{2,1,0:T(8,128)S(1)} async-done(((f32[8,40,128]{2,1,0:T(8,128)}), f32[8,40,128]{2,1,0:T(8,128)S(1)}, u32[]{:S(2)}, u32[]{:S(2)}) %all-to-all-start.15) | async-done | bytes 163872 | tf_op jit(solution)/shard_map/all_to_all | solution.py:263
  253.0 20.1 %all_to_all.95 = f32[256,1,128]{2,1,0:T(1,128)S(1)} all-to-all(f32[256,1,128]{2,1,0:T(1,128)S(1)} %broadcast_in_dim.9), channel_id=1, replica_groups=mesh['x'=2,'z'=8,'core'=2,'cols'=8] {'x','z','core','cols'}, dimensions={0} | all-to-all | bytes 262144 | tf_op jit(solution)/shard_map/all_to_all | solution.py:315
  (41 shorter events, 30.1 us)
Async XLA Ops:
  19.4 6.4 %collective-permute-start = (f32[16,32,128]{2,1,0:T(8,128)S(1)}, f32[16,32,128]{2,1,0:T(8,128)S(1)}, u32[]{:S(2)}, u32[]{:S(2)}) collective-permute-start(f32[16,32,128]{2,1,0:T(8,128)S(1)} %all_to_all.85.own), channel_id=1, source_target_pairs={{0,8},{8,0},{1,9},{9,1},{2,10},{10,2},{3,11},{11,3},{4,12},{12,4},... | collective-permute-start | bytes 786440 | tf_op jit(solution)/shard_map/ppermute | solution.py:266
  21.7 0.7 copy-start.3
  22.3 3.4 %copy-start.1 = (s32[16,2]{0,1:T(2,128)S(1)}, s32[16,2]{0,1:T(2,128)}, u32[]{:S(2)}) copy-start(s32[16,2]{0,1:T(2,128)} %param.8) | copy-start | bytes 388
  25.8 14.2 %copy-start = (f32[256,16]{0,1:T(8,128)S(1)}, f32[256,16]{0,1:T(8,128)}, u32[]{:S(2)}) copy-start(f32[256,16]{0,1:T(8,128)} %param.5) | copy-start | bytes 49156
  25.8 14.1 %copy-start.2 = (f32[256]{0:T(256)S(1)}, f32[256]{0:T(256)}, u32[]{:S(2)}) copy-start(f32[256]{0:T(256)} %param.6) | copy-start | bytes 3076
  52.9 4.4 %collective-permute-start.1 = (f32[16,40,128]{2,1,0:T(8,128)S(1)}, f32[16,40,128]{2,1,0:T(8,128)S(1)}, u32[]{:S(2)}, u32[]{:S(2)}) collective-permute-start(f32[16,40,128]{2,1,0:T(8,128)S(1)} %all_to_all.87.own), channel_id=1, source_target_pairs={{0,8},{8,0},{1,9},{9,1},{2,10},{10,2},{3,11},{11,3},{4,12},{12,4},... | collective-permute-start | bytes 983048 | tf_op jit(solution)/shard_map/ppermute | solution.py:266
  81.2 5.4 %collective-permute-start.2 = (f32[16,40,128]{2,1,0:T(8,128)S(1)}, f32[16,40,128]{2,1,0:T(8,128)S(1)}, u32[]{:S(2)}, u32[]{:S(2)}) collective-permute-start(f32[16,40,128]{2,1,0:T(8,128)S(1)} %all_to_all.89.own), channel_id=1, source_target_pairs={{0,8},{8,0},{1,9},{9,1},{2,10},{10,2},{3,11},{11,3},{4,12},{12,4},... | collective-permute-start | bytes 983048 | tf_op jit(solution)/shard_map/ppermute | solution.py:266
  88.3 10.9 %all-to-all-start.5 = ((f32[8,40,128]{2,1,0:T(8,128)}), f32[8,40,128]{2,1,0:T(8,128)S(1)}, u32[]{:S(2)}, u32[]{:S(2)}) async-start(f32[8,40,128]{2,1,0:T(8,128)} %shard_map.61), calls=%async_computation.5 | async-start | bytes 327680 | tf_op jit(solution)/shard_map/all_to_all | solution.py:263
  111.9 5.4 %collective-permute-start.3 = (f32[16,40,128]{2,1,0:T(8,128)S(1)}, f32[16,40,128]{2,1,0:T(8,128)S(1)}, u32[]{:S(2)}, u32[]{:S(2)}) collective-permute-start(f32[16,40,128]{2,1,0:T(8,128)S(1)} %all_to_all.90.own), channel_id=1, source_target_pairs={{0,8},{8,0},{1,9},{9,1},{2,10},{10,2},{3,11},{11,3},{4,12},{12,4},... | collective-permute-start | bytes 983048 | tf_op jit(solution)/shard_map/ppermute | solution.py:266
  119.0 10.4 %all-to-all-start.7 = ((f32[8,40,128]{2,1,0:T(8,128)}), f32[8,40,128]{2,1,0:T(8,128)S(1)}, u32[]{:S(2)}, u32[]{:S(2)}) async-start(f32[8,40,128]{2,1,0:T(8,128)} %shard_map.64), calls=%async_computation.7 | async-start | bytes 327680 | tf_op jit(solution)/shard_map/all_to_all | solution.py:263
  143.3 4.6 %collective-permute-start.4 = (f32[16,40,128]{2,1,0:T(8,128)S(1)}, f32[16,40,128]{2,1,0:T(8,128)S(1)}, u32[]{:S(2)}, u32[]{:S(2)}) collective-permute-start(f32[16,40,128]{2,1,0:T(8,128)S(1)} %all_to_all.91.own), channel_id=1, source_target_pairs={{0,8},{8,0},{1,9},{9,1},{2,10},{10,2},{3,11},{11,3},{4,12},{12,4},... | collective-permute-start | bytes 983048 | tf_op jit(solution)/shard_map/ppermute | solution.py:266
  149.5 11.1 %all-to-all-start.9 = ((f32[8,40,128]{2,1,0:T(8,128)}), f32[8,40,128]{2,1,0:T(8,128)S(1)}, u32[]{:S(2)}, u32[]{:S(2)}) async-start(f32[8,40,128]{2,1,0:T(8,128)} %shard_map.67), calls=%async_computation.9 | async-start | bytes 327680 | tf_op jit(solution)/shard_map/all_to_all | solution.py:263
  173.3 5.4 %collective-permute-start.5 = (f32[16,40,128]{2,1,0:T(8,128)S(1)}, f32[16,40,128]{2,1,0:T(8,128)S(1)}, u32[]{:S(2)}, u32[]{:S(2)}) collective-permute-start(f32[16,40,128]{2,1,0:T(8,128)S(1)} %all_to_all.92.own), channel_id=1, source_target_pairs={{0,8},{8,0},{1,9},{9,1},{2,10},{10,2},{3,11},{11,3},{4,12},{12,4},... | collective-permute-start | bytes 983048 | tf_op jit(solution)/shard_map/ppermute | solution.py:266
  180.4 10.4 %all-to-all-start.11 = ((f32[8,40,128]{2,1,0:T(8,128)}), f32[8,40,128]{2,1,0:T(8,128)S(1)}, u32[]{:S(2)}, u32[]{:S(2)}) async-start(f32[8,40,128]{2,1,0:T(8,128)} %shard_map.70), calls=%async_computation.11 | async-start | bytes 327680 | tf_op jit(solution)/shard_map/all_to_all | solution.py:263
  204.7 4.6 %collective-permute-start.6 = (f32[16,40,128]{2,1,0:T(8,128)S(1)}, f32[16,40,128]{2,1,0:T(8,128)S(1)}, u32[]{:S(2)}, u32[]{:S(2)}) collective-permute-start(f32[16,40,128]{2,1,0:T(8,128)S(1)} %all_to_all.93.own), channel_id=1, source_target_pairs={{0,8},{8,0},{1,9},{9,1},{2,10},{10,2},{3,11},{11,3},{4,12},{12,4},... | collective-permute-start | bytes 983048 | tf_op jit(solution)/shard_map/ppermute | solution.py:266
  211.0 11.1 %all-to-all-start.13 = ((f32[8,40,128]{2,1,0:T(8,128)}), f32[8,40,128]{2,1,0:T(8,128)S(1)}, u32[]{:S(2)}, u32[]{:S(2)}) async-start(f32[8,40,128]{2,1,0:T(8,128)} %shard_map.73), calls=%async_computation.13 | async-start | bytes 327680 | tf_op jit(solution)/shard_map/all_to_all | solution.py:263
  234.7 5.4 %collective-permute-start.7 = (f32[16,40,128]{2,1,0:T(8,128)S(1)}, f32[16,40,128]{2,1,0:T(8,128)S(1)}, u32[]{:S(2)}, u32[]{:S(2)}) collective-permute-start(f32[16,40,128]{2,1,0:T(8,128)S(1)} %all_to_all.94.own), channel_id=1, source_target_pairs={{0,8},{8,0},{1,9},{9,1},{2,10},{10,2},{3,11},{11,3},{4,12},{12,4},... | collective-permute-start | bytes 983048 | tf_op jit(solution)/shard_map/ppermute | solution.py:266
  241.8 10.4 %all-to-all-start.15 = ((f32[8,40,128]{2,1,0:T(8,128)}), f32[8,40,128]{2,1,0:T(8,128)S(1)}, u32[]{:S(2)}, u32[]{:S(2)}) async-start(f32[8,40,128]{2,1,0:T(8,128)} %shard_map.76), calls=%async_computation.15 | async-start | bytes 327680 | tf_op jit(solution)/shard_map/all_to_all | solution.py:263
